TPU v7x, 16 devices: a whole 2x2x2 slice. The times are simulated.
16 devices in a mesh: fsdp: 2 (over z), ep: 8 (over y, x, core).
Axes of the slice: x: 2, y: 2, z: 2, core: 2. Of those that a mesh axis runs over, the one named last changes fastest.
Arguments:
- grad_out: bfloat16 [32768, 768], P(('fsdp', 'ep'))
- expert_idx: int32 [32768, 1], P(('fsdp', 'ep'))
- slot_pos: int32 [32768, 1], P(('fsdp', 'ep'))
- gates: float32 [32768, 1], P(('fsdp', 'ep'))
- x_disp: bfloat16 [8, 5120, 768], P('ep', 'fsdp')
- h_gate: bfloat16 [8, 5120, 3072], P('ep', 'fsdp')
- h_up: bfloat16 [8, 5120, 3072], P('ep', 'fsdp')
- y_disp: bfloat16 [8, 5120, 768], P('ep', 'fsdp')
- w_gate: bfloat16 [8, 768, 3072], P('ep', 'fsdp')
- w_down: bfloat16 [8, 3072, 768], P('ep', 'fsdp')
- w_up: bfloat16 [8, 768, 3072], P('ep', 'fsdp')
Outputs:
- output 1: bfloat16 [32768, 768], P(('fsdp', 'ep'))
- output 2: float32 [32768, 1], P(('fsdp', 'ep'))
- output 3: float32 [8, 768, 3072], P('ep', 'fsdp')
- output 4: float32 [8, 3072, 768], P('ep', 'fsdp')
- output 5: float32 [8, 768, 3072], P('ep', 'fsdp')
All inputs are finite; a program needn't handle non-finite values.
Results may differ from a plain program's by a relative error of at most 0.001.
Values are sent between devices in bfloat16 or wider.
A program may use at most 1 GiB of HBM per device.

v0:
```python
import jax
import jax.numpy as jnp
from jax import lax
from jax.sharding import PartitionSpec as P


def expert_grads(dy_rows, gate_rows, x_rows, h_gate, h_up, y_rows, w_gate, w_down, w_up):
    g_rows = (dy_rows.astype(jnp.float32) * gate_rows[..., None]).astype(jnp.bfloat16)
    gate_pre = h_gate.astype(jnp.float32)
    up_pre = h_up.astype(jnp.float32)
    sigmoid_gate = jax.nn.sigmoid(gate_pre)
    silu_gate = gate_pre * sigmoid_gate
    act_rows = (silu_gate * up_pre).astype(jnp.bfloat16)
    d_act = jnp.einsum('erd,efd->erf', g_rows, w_down, preferred_element_type=jnp.float32)
    dh_gate = (d_act * up_pre * sigmoid_gate * (1.0 + gate_pre * (1.0 - sigmoid_gate))).astype(jnp.bfloat16)
    dh_up = (d_act * silu_gate).astype(jnp.bfloat16)
    dx_rows = (jnp.einsum('erf,edf->erd', dh_gate, w_gate, preferred_element_type=jnp.float32) + jnp.einsum('erf,edf->erd', dh_up, w_up, preferred_element_type=jnp.float32)).astype(jnp.bfloat16)
    dgate_rows = jnp.einsum('erd,erd->er', dy_rows, y_rows, preferred_element_type=jnp.float32)
    dw_gate = jnp.einsum('erd,erf->edf', x_rows, dh_gate, preferred_element_type=jnp.float32)
    dw_down = jnp.einsum('erf,erd->efd', act_rows, g_rows, preferred_element_type=jnp.float32)
    dw_up = jnp.einsum('erd,erf->edf', x_rows, dh_up, preferred_element_type=jnp.float32)
    return dx_rows, dgate_rows, dw_gate, dw_down, dw_up


def solution(mesh):
    ep_n = mesh.shape['ep']
    tok_spec = P(('fsdp', 'ep'), None)
    row_spec = P('ep', 'fsdp', None)

    def local_backward(grad_out, expert_idx, slot_pos, gates, x_disp, h_gate, h_up, y_disp, w_gate, w_down, w_up):
        tok_n, top_n = expert_idx.shape
        e_loc, rows_loc, width = x_disp.shape
        slot_cap = rows_loc // ep_n
        slots_n = e_loc * ep_n * slot_cap
        choices = tok_n * top_n
        send_row = jnp.where(slot_pos >= 0, ((expert_idx % e_loc) * ep_n + expert_idx // e_loc) * slot_cap + slot_pos, slots_n).reshape(-1)
        src_choice = jnp.full((slots_n,), choices, jnp.int32).at[send_row].set(jnp.arange(choices, dtype=jnp.int32), mode='drop')
        send_dy = jnp.take(grad_out, src_choice // top_n, axis=0, mode='fill', fill_value=0).reshape(e_loc, ep_n, slot_cap, width)
        send_gate = jnp.take(gates.reshape(-1), src_choice, mode='fill', fill_value=0).reshape(e_loc, ep_n, slot_cap)
        recv_dy = lax.all_to_all(send_dy, 'ep', 1, 1, tiled=True).reshape(e_loc, rows_loc, width)
        recv_gate = lax.all_to_all(send_gate, 'ep', 1, 1, tiled=True).reshape(e_loc, rows_loc)
        full_w_gate = lax.all_gather(w_gate, 'fsdp', axis=1, tiled=True)
        full_w_down = lax.all_gather(w_down, 'fsdp', axis=1, tiled=True)
        full_w_up = lax.all_gather(w_up, 'fsdp', axis=1, tiled=True)
        dx_rows, dgate_rows, dw_gate, dw_down, dw_up = expert_grads(recv_dy, recv_gate, x_disp, h_gate, h_up, y_disp, full_w_gate, full_w_down, full_w_up)
        back_dx = lax.all_to_all(dx_rows.reshape(e_loc, ep_n, slot_cap, width), 'ep', 1, 1, tiled=True).reshape(slots_n, width)
        back_gate = lax.all_to_all(dgate_rows.reshape(e_loc, ep_n, slot_cap), 'ep', 1, 1, tiled=True).reshape(slots_n)
        picked = jnp.take(back_dx, send_row, axis=0, mode='fill', fill_value=0).reshape(tok_n, top_n, width)
        grad_x = jnp.sum(picked.astype(jnp.float32), axis=1).astype(jnp.bfloat16)
        grad_gates = jnp.take(back_gate, send_row, mode='fill', fill_value=0).reshape(tok_n, top_n)
        grad_w_gate = lax.psum_scatter(dw_gate, 'fsdp', scatter_dimension=1, tiled=True)
        grad_w_down = lax.psum_scatter(dw_down, 'fsdp', scatter_dimension=1, tiled=True)
        grad_w_up = lax.psum_scatter(dw_up, 'fsdp', scatter_dimension=1, tiled=True)
        return grad_x, grad_gates, grad_w_gate, grad_w_down, grad_w_up

    return jax.shard_map(local_backward, mesh=mesh, in_specs=(tok_spec, tok_spec, tok_spec, tok_spec, row_spec, row_spec, row_spec, row_spec, row_spec, row_spec, row_spec), out_specs=(tok_spec, tok_spec, row_spec, row_spec, row_spec), check_vma=False)
```

profile of v0, /device:TPU:0, one launch (start us, length us, event | category | flops | bytes accessed | tf_op | source)
XLA Modules:
  0.0 539.2 jit_solution(8691923175264931052)
XLA Ops:
  7.2 0.0 copy-start
  7.2 0.0 copy-start.2
  7.2 0.0 all-gather.4.cloned.1.call-start
  7.2 0.7 all-gather.4.cloned.1.call-update
  7.9 0.0 all-gather.8.cloned.1.call-start
  8.0 0.7 all-gather.8.cloned.1.call-update
  8.7 1.3 fusion.40
  10.0 0.0 copy-start.3
  10.0 8.1 %scatter_custom_fusion = s32[2560]{0:T(1024)S(1)} fusion(s32[2048]{0:T(1024)S(1)} %bitcast.76, s32[2048]{0:T(1024)S(1)} %iota.3, s32[]{:T(128)} %constant.92.clone.1), kind=kCustom, calls=%fused_computation.52 | custom fusion | bytes 10244 | tf_op jit(solution)/shard_map/scatter | solution.py:37
  18.1 0.0 copy-done.3
  18.1 0.0 copy-done.2
  18.1 13.6 %gather_fusion.1 = f32[2560]{0:T(1024)S(1)} fusion(f32[2048]{0:T(1024)S(1)} %bitcast.73, s32[3072]{0:T(1024)S(1)} %pad_clamp_fusion), kind=kCustom, calls=%fused_computation.1 | custom fusion | bytes 30720 | tf_op jit(solution)/shard_map/jit(_take)/gather | solution.py:39
  31.8 0.7 select_n.72
  32.5 5.5 %all-to-all-start.1 = ((f32[1,8,320]{2,0,1:T(1,128)}), f32[1,8,320]{2,0,1:T(1,128)S(1)}, u32[]{:S(2)}, u32[]{:S(2)}) async-start(f32[1,8,320]{2,0,1:T(1,128)} %select_n.72), calls=%async_computation.1 | async-start | bytes 24576 | tf_op jit(solution)/shard_map/all_to_all | solution.py:41
  37.9 0.1 broadcast_in_dim.50
  38.0 0.0 copy-done
  38.0 8.5 %gather_fusion = bf16[2560,768]{1,0:T(8,128)(2,1)} fusion(bf16[2048,768]{1,0:T(8,128)(2,1)S(1)} %copy-done, s32[3072]{0:T(1024)S(1)} %pad_clamp_fusion), kind=kCustom, calls=%fused_computation | custom fusion | bytes 7874560 | tf_op jit(solution)/shard_map/jit(_take)/gather | solution.py:38
  46.5 3.7 broadcast_select_fusion
  50.3 0.0 all-to-all-done.1
  50.3 4.5 all-to-all-start
  54.8 0.0 all-gather.6.cloned.1.call-start
  54.9 0.7 all-gather.6.cloned.1.call-update
  55.6 0.2 reduce-scatter.4.cloned.1.call-start
  55.8 0.1 mul.63
  55.9 45.1 %all-to-all-done = bf16[1,8,320,768]{3,2,0,1:T(8,128)(2,1)} async-done(((bf16[1,8,320,768]{3,2,0,1:T(8,128)(2,1)}), bf16[1,8,320,768]{3,2,0,1:T(8,128)(2,1)}, u32[]{:S(2)}, u32[]{:S(2)}) %all-to-all-start) | async-done | bytes 3932192 | tf_op jit(solution)/shard_map/all_to_all | solution.py:40
  101.0 0.0 all-gather.4.cloned.1.call-done
  101.0 32.9 %fusion.2 = (bf16[1,2560,3072]{2,1,0:T(8,128)(2,1)}, bf16[2560,3072]{1,0:T(8,128)(2,1)}) fusion(bf16[1,2560,3072]{2,1,0:T(8,128)(2,1)} %param.17, bf16[1,2560,3072]{2,1,0:T(8,128)(2,1)} %param.16, bf16[1,3072,768]{2,1,0:T(8,128)(2,1)} %all-gather.4.cloned.1.call-done, bf16[1,2560,1,1,1,1,768]{6,1,5,4,3,2,0:T(8,128)(2,1)} %bitcast.26, f32[2560]{0:T(1024)S(1)} %mul.63), kind=kOutput, calls=%fused_computation.12 | convolution fusion | flops 12203458560 | bytes 71575552 | tf_op jit(solution)/shard_map/erd,efd->erf/dot_general | solution.py:14
  133.9 18.6 %fusion.21 = f32[1,768,3072]{1,2,0:T(8,128)} fusion(bf16[1,2560,3072]{2,1,0:T(8,128)(2,1)} %get-tuple-element.24, bf16[1,2560,768]{2,1,0:T(8,128)(2,1)} %param.15), kind=kOutput, calls=%fused_computation.32 | convolution fusion | flops 12079595520 | bytes 29097984 | tf_op jit(solution)/shard_map/erd,erf->edf/dot_general | solution.py:19
  152.5 0.0 reduce-scatter.4.cloned.1.call-update
  152.5 0.3 reduce-scatter.8.cloned.1.call-start
  152.8 18.7 %convolution_bitcast_fusion = f32[1,768,3072]{1,2,0:T(8,128)} fusion(bf16[2560,3072]{1,0:T(8,128)(2,1)} %get-tuple-element.25, bf16[1,2560,768]{2,1,0:T(8,128)(2,1)} %param.15), kind=kOutput, calls=%fused_computation.34 | convolution fusion | flops 12079595520 | bytes 29097984 | tf_op jit(solution)/shard_map/erd,erf->edf/dot_general | solution.py:21
  171.4 0.0 reduce-scatter.8.cloned.1.call-update
  171.4 0.0 reduce-scatter.6.cloned.1.call-start
  171.5 27.3 %fusion.24 = f32[1,3072,768]{2,1,0:T(8,128)} fusion(bf16[1,2560,3072]{2,1,0:T(8,128)(2,1)} %param.17, bf16[1,2560,3072]{2,1,0:T(8,128)(2,1)} %param.16, bf16[1,2560,1,1,1,1,768]{6,1,5,4,3,2,0:T(8,128)(2,1)} %bitcast.26, f32[2560]{0:T(1024)S(1)} %mul.63), kind=kOutput, calls=%fused_computation.33 | convolution fusion | flops 12148408320 | bytes 44836864 | tf_op jit(solution)/shard_map/erf,erd->efd/dot_general | solution.py:20
  198.8 0.0 reduce-scatter.6.cloned.1.call-update
  198.8 4.4 fusion.18
  203.2 0.7 reshape.222
  203.9 3.6 all-to-all-start.3
  207.5 0.0 all-gather.8.cloned.1.call-done
  207.6 18.3 %fusion.27 = f32[2560,768]{1,0:T(8,128)} fusion(bf16[2560,3072]{1,0:T(8,128)(2,1)} %get-tuple-element.25, bf16[1,768,3072]{2,1,0:T(8,128)(2,1)} %all-gather.8.cloned.1.call-done), kind=kOutput, calls=%fused_computation.35 | convolution fusion | flops 12079595520 | bytes 28311552 | tf_op jit(solution)/shard_map/erf,edf->erd/dot_general | solution.py:17
  225.8 0.0 all-gather.6.cloned.1.call-done
  225.8 19.7 %add_convert_fusion = bf16[2560,768]{1,0:T(8,128)(2,1)} fusion(f32[2560,768]{1,0:T(8,128)} %fusion.27, bf16[1,2560,3072]{2,1,0:T(8,128)(2,1)} %get-tuple-element.24, bf16[1,768,3072]{2,1,0:T(8,128)(2,1)} %all-gather.6.cloned.1.call-done), kind=kOutput, calls=%fused_computation.31 | convolution fusion | flops 12083527680 | bytes 32243712 | tf_op jit(solution)/shard_map/erf,edf->erd/dot_general | solution.py:17
  245.5 0.0 copy-start.4
  245.5 0.0 all-to-all-done.3
  245.5 4.6 all-to-all-start.2
  250.1 0.0 copy-done.4
  250.1 0.1 reshape.223
  250.2 11.8 %gather_fusion.3 = f32[2048]{0:T(1024)S(1)} fusion(f32[2560]{0:T(1024)S(1)} %reshape.223, s32[2048]{0:T(1024)S(1)} %broadcast_clamp_fusion), kind=kCustom, calls=%fused_computation.3 | custom fusion | bytes 24576 | tf_op jit(solution)/shard_map/jit(_take)/gather | solution.py:50
  262.0 0.6 broadcast_select_fusion.3
  262.6 33.6 %all-to-all-done.2 = bf16[1,8,320,768]{3,2,0,1:T(8,128)(2,1)} async-done(((bf16[1,8,320,768]{3,2,0,1:T(8,128)(2,1)}), bf16[1,8,320,768]{3,2,0,1:T(8,128)(2,1)}, u32[]{:S(2)}, u32[]{:S(2)}) %all-to-all-start.2) | async-done | bytes 3932192 | tf_op jit(solution)/shard_map/all_to_all | solution.py:46
  296.2 0.0 copy-start.5
  296.3 12.7 %gather_fusion.2 = bf16[2048,768]{1,0:T(8,128)(2,1)} fusion(bf16[2560,768]{1,0:T(8,128)(2,1)} %bitcast.14, s32[2048]{0:T(1024)S(1)} %broadcast_clamp_fusion), kind=kCustom, calls=%fused_computation.2 | custom fusion | bytes 6299648 | tf_op jit(solution)/shard_map/jit(_take)/gather | solution.py:48
  308.9 0.0 copy-done.5
  308.9 0.0 copy-start.1
  308.9 3.4 broadcast_select_fusion.1
  312.4 0.0 reduce-scatter.4.cloned.1.call-done
  312.4 6.0 %copy.22 = f32[1,384,3072]{2,1,0:T(8,128)} copy(f32[1,384,3072]{1,2,0:T(8,128)} %reduce-scatter.4.cloned.1.call-done) | data formatting | bytes 9437184
  318.4 102.0 %reduce-scatter.8.cloned.1.call-done = f32[1,384,3072]{1,2,0:T(8,128)} async-done(((f32[1,768,3072]{1,2,0:T(8,128)}), f32[1,384,3072]{1,2,0:T(8,128)}) %reduce-scatter.8.cloned.1.call-update) | async-done | bytes 4718608 | tf_op jit(solution)/shard_map/reduce_scatter | solution.py:53
  420.5 6.0 %copy.23 = f32[1,384,3072]{2,1,0:T(8,128)} copy(f32[1,384,3072]{1,2,0:T(8,128)} %reduce-scatter.8.cloned.1.call-done) | data formatting | bytes 9437184
  426.5 105.4 %reduce-scatter.6.cloned.1.call-done = f32[1,1536,768]{2,1,0:T(8,128)} async-done(((f32[1,3072,768]{2,1,0:T(8,128)}), f32[1,1536,768]{2,1,0:T(8,128)}) %reduce-scatter.6.cloned.1.call-update) | async-done | bytes 4718608 | tf_op jit(solution)/shard_map/reduce_scatter | solution.py:52
  531.9 0.0 copy-done.1
  (7 shorter events, 0.1 us)
Async XLA Ops:
  7.2 30.8 %copy-start = (bf16[2048,768]{1,0:T(8,128)(2,1)S(1)}, bf16[2048,768]{1,0:T(8,128)(2,1)}, u32[]{:S(2)}) copy-start(bf16[2048,768]{1,0:T(8,128)(2,1)} %param.11) | copy-start | bytes 9437188
  7.2 10.9 %copy-start.2 = (f32[2048,1]{0,1:T(1,128)S(1)}, f32[2048,1]{0,1:T(1,128)}, u32[]{:S(2)}) copy-start(f32[2048,1]{0,1:T(1,128)} %param.14) | copy-start | bytes 24580
  7.2 93.8 %all-gather.4.cloned.1.call-start = ((), (), s32[]{:S(2)}) async-start(), calls=%async_computation.7 | async-start | bytes 7077888 | tf_op jit(solution)/shard_map/all_gather | solution.py:43
  7.9 199.6 %all-gather.8.cloned.1.call-start = ((), (), s32[]{:S(2)}) async-start(), calls=%async_computation.9 | async-start | bytes 7077888 | tf_op jit(solution)/shard_map/all_gather | solution.py:44
  10.0 8.1 %copy-start.3 = (s32[2048,1]{0,1:T(1,128)}, s32[2048,1]{0,1:T(1,128)S(1)}, u32[]{:S(2)}) copy-start(s32[2048,1]{0,1:T(1,128)S(1)} %get-tuple-element.21) | copy-start | bytes 24580
  32.5 17.8 %all-to-all-start.1 = ((f32[1,8,320]{2,0,1:T(1,128)}), f32[1,8,320]{2,0,1:T(1,128)S(1)}, u32[]{:S(2)}, u32[]{:S(2)}) async-start(f32[1,8,320]{2,0,1:T(1,128)} %select_n.72), calls=%async_computation.1 | async-start | bytes 24576 | tf_op jit(solution)/shard_map/all_to_all | solution.py:41
  50.3 50.7 %all-to-all-start = ((bf16[1,8,320,768]{3,2,0,1:T(8,128)(2,1)}), bf16[1,8,320,768]{3,2,0,1:T(8,128)(2,1)}, u32[]{:S(2)}, u32[]{:S(2)}) async-start(bf16[1,8,320,768]{3,2,0,1:T(8,128)(2,1)} %broadcast_select_fusion), calls=%async_computation | async-start | bytes 7864320 | tf_op jit(solution)/shard_map/all_to_all | solution.py:40
  54.8 171.0 %all-gather.6.cloned.1.call-start = ((), (), s32[]{:S(2)}) async-start(), calls=%async_computation.8 | async-start | bytes 7077888 | tf_op jit(solution)/shard_map/all_gather | solution.py:42
  55.6 256.8 %reduce-scatter.4.cloned.1.call-start = ((), (), s32[]{:S(2)}) async-start(), calls=%async_computation.10 | async-start | bytes 14155776 | tf_op jit(solution)/shard_map/reduce_scatter | solution.py:51
  152.5 268.0 %reduce-scatter.8.cloned.1.call-start = ((), (), s32[]{:S(2)}) async-start(), calls=%async_computation.12 | async-start | bytes 14155776 | tf_op jit(solution)/shard_map/reduce_scatter | solution.py:53
  171.4 360.4 %reduce-scatter.6.cloned.1.call-start = ((), (), s32[]{:S(2)}) async-start(), calls=%async_computation.11 | async-start | bytes 14155776 | tf_op jit(solution)/shard_map/reduce_scatter | solution.py:52
  203.9 41.6 %all-to-all-start.3 = ((f32[1,8,320]{2,0,1:T(1,128)}), f32[1,8,320]{2,0,1:T(1,128)S(1)}, u32[]{:S(2)}, u32[]{:S(2)}) async-start(f32[1,8,320]{2,0,1:T(1,128)} %reshape.222), calls=%async_computation.3 | async-start | bytes 24576 | tf_op jit(solution)/shard_map/all_to_all | solution.py:47
  245.5 4.6 copy-start.4
  245.5 50.8 %all-to-all-start.2 = ((bf16[1,8,320,768]{3,2,0,1:T(8,128)(2,1)}), bf16[1,8,320,768]{3,2,0,1:T(8,128)(2,1)}, u32[]{:S(2)}, u32[]{:S(2)}) async-start(bf16[1,8,320,768]{3,2,0,1:T(8,128)(2,1)} %bitcast.75), calls=%async_computation.2 | async-start | bytes 7864320 | tf_op jit(solution)/shard_map/all_to_all | solution.py:46
  296.2 12.7 %copy-start.5 = (pred[2048]{0:T(1024)(128)(4,1)S(1)}, pred[2048]{0:T(1024)(128)(4,1)}, u32[]{:S(2)}) copy-start(pred[2048]{0:T(1024)(128)(4,1)} %get-tuple-element.20) | copy-start | bytes 6148
  308.9 222.9 %copy-start.1 = (bf16[2048,768]{1,0:T(8,128)(2,1)S(1)}, bf16[2048,768]{1,0:T(8,128)(2,1)}, u32[]{:S(2)}) copy-start(bf16[2048,768]{1,0:T(8,128)(2,1)} %param.11) | copy-start | bytes 9437188
Sparse Core Ops, SparseCore 0:
  9.5 63.9 all-gather.3
  75.0 61.0 all-gather.7
  137.7 61.0 all-gather.5
  200.9 108.6 reduce-scatter.3
  311.8 108.6 reduce-scatter.7
  423.2 108.6 reduce-scatter.5
where the time goes:
time: 543 us; the launch traced here: 539 us
  waiting for transfers between devices  288 us (53%)
  matrix products  135 us (25%)
  local copies, waits for them, and re-layouts  68.4 us (13%)
  starting transfers between devices  18.8 us (3%)
  between operations  14.7 us (3%)
  other arithmetic  13.6 us (3%)
    reduce_scatter x1, waiting for transfers between devices, local_backward(): lax.psum_scatter(dw_down, 'fsdp', scatter_dimension=1, tiled=True)  105 us
    reduce_scatter x1, waiting for transfers between devices, local_backward(): grad_w_up = lax.psum_scatter(dw_up, 'fsdp', scatter_dimension=1, tiled=True)  102 us
    all_to_all x1, waiting for transfers between devices, local_backward(): lax.all_to_all(send_dy, 'ep', 1, 1, tiled=True)  45.1 us
    all_to_all x1, waiting for transfers between devices, local_backward(): lax.all_to_all(dx_rows.reshape(e_loc, ep_n, slot_cap, width), 'ep', 1, 1,...  33.6 us
    dot_general x1, matrix products, expert_grads(): jnp.einsum('erd,efd->erf', g_rows, w_down, preferred_element_type=jnp.flo...  32.9 us
    dot_general x1, matrix products, expert_grads(): jnp.einsum('erf,erd->efd', act_rows, g_rows, preferred_element_type=jnp.f...  27.3 us
    dot_general x1, matrix products, expert_grads(): jnp.einsum('erf,edf->erd', dh_gate, w_gate, preferred_element_type=jnp.fl...  19.7 us
    dot_general x1, matrix products, expert_grads(): jnp.einsum('erd,erf->edf', x_rows, dh_up, preferred_element_type=jnp.floa...  18.7 us
  transfers between devices with their start and end apart: 10, of which 4 were waited for; matrix products, arithmetic and copies ran while one was open for 40% of the time, Pallas kernels for 0%

commit v1 on v0

v1 whole, which is shorter than its diff:
```python
import jax
import jax.numpy as jnp
from jax import lax
from jax.sharding import PartitionSpec as P


F32 = jnp.float32
BF16 = jnp.bfloat16


def solution(mesh):
    ep_n = mesh.shape['ep']
    fs_n = mesh.shape['fsdp']
    tok_spec = P(('fsdp', 'ep'), None)
    row_spec = P('ep', 'fsdp', None)
    swap = [(i, fs_n - 1 - i) for i in range(fs_n)]

    def exchange(value):
        return lax.ppermute(value, 'fsdp', swap)

    def local_backward(grad_out, expert_idx, slot_pos, gates, x_disp, h_gate, h_up, y_disp, w_gate, w_down, w_up):
        tok_n, top_n = expert_idx.shape
        e_loc, rows_loc, width = x_disp.shape
        slot_cap = rows_loc // ep_n
        slots_n = e_loc * ep_n * slot_cap
        choices = tok_n * top_n
        z = lax.axis_index('fsdp')

        other_w_down = exchange(w_down)
        other_w_gate = exchange(w_gate)
        other_w_up = exchange(w_up)

        def whole(own, other):
            return jnp.where(z == 0, jnp.concatenate([own, other], axis=1), jnp.concatenate([other, own], axis=1))

        send_row = jnp.where(slot_pos >= 0, ((expert_idx % e_loc) * ep_n + expert_idx // e_loc) * slot_cap + slot_pos, slots_n).reshape(-1)
        src_choice = jnp.full((slots_n,), choices, jnp.int32).at[send_row].set(jnp.arange(choices, dtype=jnp.int32), mode='drop')
        send_dy = jnp.take(grad_out, src_choice // top_n, axis=0, mode='fill', fill_value=0).reshape(e_loc, ep_n, slot_cap, width)
        send_gate = jnp.take(gates.reshape(-1), src_choice, mode='fill', fill_value=0).reshape(e_loc, ep_n, slot_cap)
        dy_rows = lax.all_to_all(send_dy, 'ep', 1, 1, tiled=True).reshape(e_loc, rows_loc, width)
        gate_rows = lax.all_to_all(send_gate, 'ep', 1, 1, tiled=True).reshape(e_loc, rows_loc)

        g_rows = (dy_rows.astype(F32) * gate_rows[..., None]).astype(BF16)
        gate_pre = h_gate.astype(F32)
        up_pre = h_up.astype(F32)
        sigmoid_gate = jax.nn.sigmoid(gate_pre)
        silu_gate = gate_pre * sigmoid_gate
        act_rows = (silu_gate * up_pre).astype(BF16)

        def part(value, axis, index):
            half = value.shape[axis] // fs_n
            return lax.dynamic_slice_in_dim(value, index * half, half, axis)

        send = jnp.einsum('erf,erd->efd', part(act_rows, 2, 1 - z), g_rows, preferred_element_type=F32)
        recv_dw_down = exchange(send)

        full_w_down = whole(w_down, other_w_down)
        d_act = jnp.einsum('erd,efd->erf', g_rows, full_w_down, preferred_element_type=F32)
        dh_gate = (d_act * up_pre * sigmoid_gate * (1.0 + gate_pre * (1.0 - sigmoid_gate))).astype(BF16)
        dh_up = (d_act * silu_gate).astype(BF16)

        x_send = part(x_disp, 2, 1 - z)
        x_own = part(x_disp, 2, z)
        recv_dw_gate = exchange(jnp.einsum('erd,erf->edf', x_send, dh_gate, preferred_element_type=F32))
        recv_dw_up = exchange(jnp.einsum('erd,erf->edf', x_send, dh_up, preferred_element_type=F32))

        full_w_gate = whole(w_gate, other_w_gate)
        full_w_up = whole(w_up, other_w_up)
        dx_rows = (jnp.einsum('erf,edf->erd', dh_gate, full_w_gate, preferred_element_type=F32) + jnp.einsum('erf,edf->erd', dh_up, full_w_up, preferred_element_type=F32)).astype(BF16)
        dgate_rows = jnp.einsum('erd,erd->er', dy_rows, y_disp, preferred_element_type=F32)
        back_dx = lax.all_to_all(dx_rows.reshape(e_loc, ep_n, slot_cap, width), 'ep', 1, 1, tiled=True).reshape(slots_n, width)
        back_gate = lax.all_to_all(dgate_rows.reshape(e_loc, ep_n, slot_cap), 'ep', 1, 1, tiled=True).reshape(slots_n)
        picked = jnp.take(back_dx, send_row, axis=0, mode='fill', fill_value=0).reshape(tok_n, top_n, width)
        grad_x = jnp.sum(picked.astype(F32), axis=1).astype(BF16)
        grad_gates = jnp.take(back_gate, send_row, mode='fill', fill_value=0).reshape(tok_n, top_n)

        def combine(own, recv):
            return lax.optimization_barrier(own) + recv

        grad_w_down = combine(jnp.einsum('erf,erd->efd', part(act_rows, 2, z), g_rows, preferred_element_type=F32), recv_dw_down)
        grad_w_gate = combine(jnp.einsum('erd,erf->edf', x_own, dh_gate, preferred_element_type=F32), recv_dw_gate)
        grad_w_up = combine(jnp.einsum('erd,erf->edf', x_own, dh_up, preferred_element_type=F32), recv_dw_up)
        return grad_x, grad_gates, grad_w_gate, grad_w_down, grad_w_up

    return jax.shard_map(local_backward, mesh=mesh, in_specs=(tok_spec, tok_spec, tok_spec, tok_spec, row_spec, row_spec, row_spec, row_spec, row_spec, row_spec, row_spec), out_specs=(tok_spec, tok_spec, row_spec, row_spec, row_spec), check_vma=False)
```

time: 543 us -> 514 us (0.947)
  waiting for transfers between devices: 288 us -> 245 us
  matrix products: 135 us -> 154 us
  other arithmetic: 13.6 us -> 29.4 us
  local copies, waits for them, and re-layouts: 68.4 us -> 54.7 us
  between operations: 14.7 us -> 1.11 us
  starting transfers between devices: 18.8 us -> 26.5 us
    ppermute x0 -> x6, waiting for transfers between devices: none -> 236 us  [exchange(): return lax.ppermute(value, 'fsdp', swap)]
    reduce_scatter x3 -> x0, waiting for transfers between devices: 207 us -> none  [the longest x1 105 us: local_backward(): lax.psum_scatter(dw_down, 'fsdp', scatter_dimension=1, tiled=True)]
    all_to_all x1, waiting for transfers between devices: 45.1 us -> 0.01 us  [local_backward(): lax.all_to_all(send_dy, 'ep', 1, 1, tiled=True)]
    all_to_all x1, waiting for transfers between devices: 33.6 us -> 9.78 us  [local_backward(): lax.all_to_all(dx_rows.reshape(e_loc, ep_n, slot_cap, width), 'ep', 1, 1,...]
    dot_general x6 -> x9, matrix products: 135 us -> 154 us  [the longest x1 39.6 us: local_backward(): jnp.einsum('erd,efd->erf', g_rows, full_w_down, preferred_element_type=F32)]
    add x0 -> x3, other arithmetic: none -> 17.7 us  [combine(): return lax.optimization_barrier(own) + recv]
    unnamed x14 -> x40, local copies, waits for them, and re-layouts: 12.1 us -> 0.09 us
    ppermute x0 -> x6, starting transfers between devices: none -> 7.18 us  [exchange(): return lax.ppermute(value, 'fsdp', swap)]
  transfers between devices with their start and end apart: 10 -> 10, of which waited for: 4 -> 4; matrix products, arithmetic and copies ran while one was open for 40% -> 41% of each run, Pallas kernels for 0% -> 0%
where the time goes in v1:
time: 514 us; the launch traced here: 511 us
  waiting for transfers between devices  245 us (48%)
  matrix products  154 us (30%)
  local copies, waits for them, and re-layouts  54.7 us (11%)
  other arithmetic  29.4 us (6%)
  starting transfers between devices  26.5 us (5%)
    ppermute x6, waiting for transfers between devices, exchange(): return lax.ppermute(value, 'fsdp', swap)  236 us
    dot_general x1, matrix products, local_backward(): jnp.einsum('erd,efd->erf', g_rows, full_w_down, preferred_element_type=F32)  39.6 us
    dot_general x1, matrix products, local_backward(): jnp.einsum('erf,edf->erd', dh_gate, full_w_gate, preferred_element_type=F32)  24.5 us
    dot_general x1, matrix products, local_backward(): jnp.einsum('erf,edf->erd', dh_up, full_w_up, preferred_element_type=F32)  21.5 us
    add x3, other arithmetic, combine(): return lax.optimization_barrier(own) + recv  17.7 us
    gather x1, local copies, waits for them, and re-layouts, local_backward(): jnp.take(gates.reshape(-1), src_choice, mode='fill', fill_value=0)  13.6 us
    dot_general x1, matrix products, local_backward(): jnp.einsum('erd,erf->edf', x_send, dh_up, preferred_element_type=F32)  12.8 us
    dot_general x1, matrix products, local_backward(): jnp.einsum('erd,erf->edf', x_own, dh_gate, preferred_element_type=F32)  12.1 us
  transfers between devices with their start and end apart: 10, of which 4 were waited for; matrix products, arithmetic and copies ran while one was open for 41% of the time, Pallas kernels for 0%

profile of v1, /device:TPU:0, one launch (start us, length us, event | category | flops | bytes accessed | tf_op | source)
XLA Modules:
  0.0 511.1 jit_solution(5718850612945007749)
XLA Ops:
  0.6 0.0 copy-start
  0.6 0.0 copy-start.2
  0.7 1.5 fusion.83
  2.2 8.1 %scatter_custom_fusion = s32[2560]{0:T(1024)S(1)} fusion(s32[2048]{0:T(1024)S(1)} %bitcast.94, s32[2048]{0:T(1024)S(1)} %iota.3, s32[]{:T(128)} %constant.101.clone.1), kind=kCustom, calls=%fused_computation.88 | custom fusion | bytes 10244 | tf_op jit(solution)/shard_map/scatter | solution.py:37
  10.3 0.0 copy-done.2
  10.3 13.6 %gather_fusion.1 = f32[2560]{0:T(1024)S(1)} fusion(f32[2048]{0:T(1024)S(1)} %bitcast.85, s32[3072]{0:T(1024)S(1)} %pad_clamp_fusion), kind=kCustom, calls=%fused_computation.1 | custom fusion | bytes 30720 | tf_op jit(solution)/shard_map/jit(_take)/gather | solution.py:39
  23.9 0.7 select_n.113
  24.6 5.4 %all-to-all-start.1 = ((f32[1,8,320]{2,0,1:T(1,128)}), f32[1,8,320]{2,0,1:T(1,128)S(1)}, u32[]{:S(2)}, u32[]{:S(2)}) async-start(f32[1,8,320]{2,0,1:T(1,128)} %select_n.113), calls=%async_computation.1 | async-start | bytes 24576 | tf_op jit(solution)/shard_map/all_to_all | solution.py:41
  30.0 0.1 broadcast_in_dim.50
  30.1 0.0 copy-done
  30.1 8.5 %gather_fusion = bf16[2560,768]{1,0:T(8,128)(2,1)} fusion(bf16[2048,768]{1,0:T(8,128)(2,1)S(1)} %copy-done, s32[3072]{0:T(1024)S(1)} %pad_clamp_fusion), kind=kCustom, calls=%fused_computation | custom fusion | bytes 7874560 | tf_op jit(solution)/shard_map/jit(_take)/gather | solution.py:38
  38.6 3.7 broadcast_select_fusion
  42.4 0.0 all-to-all-done.1
  42.4 5.0 all-to-all-start
  47.3 0.0 copy-done.10
  47.3 1.6 collective-permute-start
  49.0 0.4 collective-permute-start.2
  49.4 1.6 collective-permute-start.1
  51.0 0.0 copy-done.6
  51.0 0.6 broadcast_clamp_fusion
  51.6 0.1 mul.80
  51.7 49.9 %collective-permute-done = bf16[1,1536,768]{2,1,0:T(8,128)(2,1)} collective-permute-done((bf16[1,1536,768]{2,1,0:T(8,128)(2,1)S(1)}, bf16[1,1536,768]{2,1,0:T(8,128)(2,1)}, u32[]{:S(2)}, u32[]{:S(2)}) %collective-permute-start) | collective-permute-done | bytes 2359328 | tf_op jit(solution)/shard_map/ppermute | solution.py:19
  101.6 0.0 all-to-all-done
  101.6 39.6 %fusion.2 = (bf16[1,2560,3072]{2,1,0:T(8,128)(2,1)}, bf16[2560,3072]{1,0:T(8,128)(2,1)}, bf16[1,2560,3072]{2,1,0:T(8,128)(2,1)}) fusion(bf16[1,2560,3072]{2,1,0:T(8,128)(2,1)} %param.17, bf16[1,2560,3072]{2,1,0:T(8,128)(2,1)} %param.16, bf16[1536,768]{1,0:T(8,128)(2,1)} %bitcast.6, bf16[1536,768]{1,0:T(8,128)(2,1)S(1)} %bitcast.97, pred[]{:T(512)S(6)} %eq.4, ...), kind=kOutput, calls=%fused_computation.12 | convolution fusion | flops 12240420864 | bytes 87304192 | tf_op jit(solution)/shard_map/erd,efd->erf/dot_general | solution.py:58
  141.2 0.0 slice-start
  141.2 0.0 slice-start.1
  141.2 0.0 slice-start.2
  141.2 11.7 %fusion.59 = f32[1,1536,768]{2,1,0:T(8,128)} fusion(bf16[1,2560,3072]{2,1,0:T(8,128)(2,1)} %get-tuple-element.11, s32[]{:T(128)S(6)} %select_n.124, bf16[1,2560,1,1,1,1,768]{6,1,5,4,3,2,0:T(8,128)(2,1)} %bitcast.33, f32[2560]{0:T(1024)S(1)} %mul.80), kind=kOutput, calls=%fused_computation.71 | convolution fusion | flops 6045696000 | bytes 16525316 | tf_op jit(solution)/shard_map/erf,erd->efd/dot_general | solution.py:54
  153.0 1.6 collective-permute-start.4
  154.5 12.8 %convolution_bitcast_fusion = f32[1,384,3072]{2,1,0:T(8,128)} fusion(bf16[2560,3072]{1,0:T(8,128)(2,1)} %get-tuple-element.10, bf16[1,2560,768]{2,1,0:T(8,128)(2,1)S(1)} %copy-done.3, s32[]{:T(128)S(6)} %select_n.122), kind=kOutput, calls=%fused_computation.65 | convolution fusion | flops 6039797760 | bytes 22413316 | tf_op jit(solution)/shard_map/erd,erf->edf/dot_general | solution.py:65
  167.3 0.4 collective-permute-start.5
  167.8 0.0 slice-done.3
  167.8 0.0 copy-start.5
  167.8 8.1 %fusion.50 = f32[1,384,3072]{2,1,0:T(8,128)} fusion(bf16[1,2560,3072]{2,1,0:T(8,128)(2,1)S(1)} %bitcast.87, bf16[1,2560,768]{2,1,0:T(8,128)(2,1)S(1)} %copy-done.3, s32[]{:T(128)S(6)} %select_n.122), kind=kOutput, calls=%fused_computation.64 | convolution fusion | flops 6039797760 | bytes 22413316 | tf_op jit(solution)/shard_map/erd,erf->edf/dot_general | solution.py:64
  175.9 1.6 collective-permute-start.3
  177.5 0.0 copy-done.5
  177.5 3.2 fusion.17
  180.7 0.7 reshape.293
  181.4 4.4 all-to-all-start.3
  185.8 0.0 collective-permute-done.2
  185.8 0.0 copy-done.11
  185.8 21.5 %fusion.38 = f32[2560,768]{1,0:T(8,128)} fusion(bf16[2560,3072]{1,0:T(8,128)(2,1)} %get-tuple-element.10, bf16[384,3072]{1,0:T(8,128)(2,1)} %bitcast.13, bf16[384,3072]{1,0:T(8,128)(2,1)S(1)} %bitcast.98, pred[]{:T(512)S(6)} %eq.4), kind=kOutput, calls=%fused_computation.54 | convolution fusion | flops 12100829184 | bytes 28311552 | tf_op jit(solution)/shard_map/erf,edf->erd/dot_general | solution.py:69
  207.3 0.0 collective-permute-done.1
  207.3 24.5 %add_convert_fusion = bf16[2560,768]{1,0:T(8,128)(2,1)} fusion(f32[2560,768]{1,0:T(8,128)} %fusion.38, bf16[1,2560,3072]{2,1,0:T(8,128)(2,1)} %get-tuple-element.9, bf16[384,3072]{1,0:T(8,128)(2,1)} %bitcast.10, bf16[384,3072]{1,0:T(8,128)(2,1)} %bitcast.99, pred[]{:T(512)S(6)} %eq.4), kind=kOutput, calls=%fused_computation.39 | convolution fusion | flops 12104761344 | bytes 32243712 | tf_op jit(solution)/shard_map/erf,edf->erd/dot_general | solution.py:69
  231.8 11.8 %fusion.56 = f32[1,1536,768]{2,1,0:T(8,128)} fusion(bf16[1,2560,3072]{2,1,0:T(8,128)(2,1)} %get-tuple-element.11, s32[]{:T(128)S(6)} %select_n.123, bf16[1,2560,1,1,1,1,768]{6,1,5,4,3,2,0:T(8,128)(2,1)} %bitcast.33, f32[2560]{0:T(1024)S(1)} %mul.80), kind=kOutput, calls=%fused_computation.70 | convolution fusion | flops 6045696000 | bytes 16525316 | tf_op jit(solution)/shard_map/erf,erd->efd/dot_general | solution.py:80
  243.6 0.0 all-to-all-done.3
  243.6 4.5 all-to-all-start.2
  248.1 0.0 copy-start.4
  248.1 11.9 %convolution_bitcast_fusion.1 = f32[1,384,3072]{2,1,0:T(8,128)} fusion(bf16[2560,3072]{1,0:T(8,128)(2,1)} %get-tuple-element.10, bf16[1,2560,768]{2,1,0:T(8,128)(2,1)} %param.15, s32[]{:T(128)S(6)} %select_n.121), kind=kOutput, calls=%fused_computation.66 | convolution fusion | flops 6039797760 | bytes 22413316 | tf_op jit(solution)/shard_map/erd,erf->edf/dot_general | solution.py:82
  260.0 12.1 %fusion.47 = f32[1,384,3072]{2,1,0:T(8,128)} fusion(bf16[1,2560,3072]{2,1,0:T(8,128)(2,1)} %get-tuple-element.9, bf16[1,2560,768]{2,1,0:T(8,128)(2,1)S(1)} %copy-done.4, s32[]{:T(128)S(6)} %select_n.121), kind=kOutput, calls=%fused_computation.63 | convolution fusion | flops 6039797760 | bytes 22413316 | tf_op jit(solution)/shard_map/erd,erf->edf/dot_general | solution.py:81
  272.1 0.1 reshape.294
  272.2 11.8 %gather_fusion.3 = f32[2048]{0:T(1024)S(1)} fusion(f32[2560]{0:T(1024)S(1)} %reshape.294, s32[2048]{0:T(1024)S(1)} %copy-done.8), kind=kCustom, calls=%fused_computation.3 | custom fusion | bytes 24576 | tf_op jit(solution)/shard_map/jit(_take)/gather | solution.py:75
  284.0 0.6 broadcast_select_fusion.3
  284.6 9.8 %all-to-all-done.2 = bf16[1,8,320,768]{3,2,0,1:T(8,128)(2,1)} async-done(((bf16[1,8,320,768]{3,2,0,1:T(8,128)(2,1)}), bf16[1,8,320,768]{3,2,0,1:T(8,128)(2,1)}, u32[]{:S(2)}, u32[]{:S(2)}) %all-to-all-start.2) | async-done | bytes 3932192 | tf_op jit(solution)/shard_map/all_to_all | solution.py:71
  294.4 11.1 %gather_fusion.2 = bf16[2048,768]{1,0:T(8,128)(2,1)S(1)} fusion(bf16[2560,768]{1,0:T(8,128)(2,1)} %bitcast.16, s32[2048]{0:T(1024)S(1)} %copy-done.8), kind=kCustom, calls=%fused_computation.2 | custom fusion | bytes 6299648 | tf_op jit(solution)/shard_map/jit(_take)/gather | solution.py:73
  305.5 0.0 slice-start.6
  305.5 1.9 broadcast_select_fusion.1
  307.4 0.0 collective-permute-done.4
  307.4 7.0 %add.77 = f32[1,1536,768]{2,1,0:T(8,128)} add(f32[1,1536,768]{2,1,0:T(8,128)} %fusion.56, f32[1,1536,768]{2,1,0:T(8,128)} %collective-permute-done.4) | non-fusion elementwise | flops 1179648 | bytes 14155776 | tf_op jit(solution)/shard_map/add | solution.py:78
  314.5 90.5 %collective-permute-done.5 = f32[1,384,3072]{2,1,0:T(8,128)} collective-permute-done((f32[1,384,3072]{2,1,0:T(8,128)}, f32[1,384,3072]{2,1,0:T(8,128)}, u32[]{:S(2)}, u32[]{:S(2)}) %collective-permute-start.5) | collective-permute-done | bytes 4718624 | tf_op jit(solution)/shard_map/ppermute | solution.py:19
  405.0 0.0 slice-done.6
  405.0 5.4 %add.78 = f32[1,384,3072]{2,1,0:T(8,128)} add(f32[1,384,3072]{2,1,0:T(8,128)S(1)} %bitcast.91, f32[1,384,3072]{2,1,0:T(8,128)} %collective-permute-done.5) | non-fusion elementwise | flops 1179648 | bytes 14155776 | tf_op jit(solution)/shard_map/add | solution.py:78
  410.4 95.2 %collective-permute-done.3 = f32[1,384,3072]{2,1,0:T(8,128)} collective-permute-done((f32[1,384,3072]{2,1,0:T(8,128)}, f32[1,384,3072]{2,1,0:T(8,128)}, u32[]{:S(2)}, u32[]{:S(2)}) %collective-permute-start.3) | collective-permute-done | bytes 4718624 | tf_op jit(solution)/shard_map/ppermute | solution.py:19
  505.6 5.3 %add.74 = f32[1,384,3072]{2,1,0:T(8,128)} add(f32[1,384,3072]{2,1,0:T(8,128)S(1)} %bitcast.89, f32[1,384,3072]{2,1,0:T(8,128)} %collective-permute-done.3) | non-fusion elementwise | flops 1179648 | bytes 14155776 | tf_op jit(solution)/shard_map/add | solution.py:78
  (33 shorter events, 0.1 us)
Async XLA Ops:
  0.6 29.5 %copy-start = (bf16[2048,768]{1,0:T(8,128)(2,1)S(1)}, bf16[2048,768]{1,0:T(8,128)(2,1)}, u32[]{:S(2)}) copy-start(bf16[2048,768]{1,0:T(8,128)(2,1)} %param.11) | copy-start | bytes 9437188
  0.6 9.6 %copy-start.2 = (f32[2048,1]{0,1:T(1,128)S(1)}, f32[2048,1]{0,1:T(1,128)}, u32[]{:S(2)}) copy-start(f32[2048,1]{0,1:T(1,128)} %param.14) | copy-start | bytes 24580
  2.2 48.8 %copy-start.6 = (s32[2048,1]{0,1:T(1,128)}, s32[2048,1]{0,1:T(1,128)S(1)}, u32[]{:S(2)}) copy-start(s32[2048,1]{0,1:T(1,128)S(1)} %get-tuple-element.6) | copy-start | bytes 24580
  24.6 17.8 %all-to-all-start.1 = ((f32[1,8,320]{2,0,1:T(1,128)}), f32[1,8,320]{2,0,1:T(1,128)S(1)}, u32[]{:S(2)}, u32[]{:S(2)}) async-start(f32[1,8,320]{2,0,1:T(1,128)} %select_n.113), calls=%async_computation.1 | async-start | bytes 24576 | tf_op jit(solution)/shard_map/all_to_all | solution.py:41
  42.4 5.0 copy-start.10
  42.4 59.2 %all-to-all-start = ((bf16[1,8,320,768]{3,2,0,1:T(8,128)(2,1)}), bf16[1,8,320,768]{3,2,0,1:T(8,128)(2,1)}, u32[]{:S(2)}, u32[]{:S(2)}) async-start(bf16[1,8,320,768]{3,2,0,1:T(8,128)(2,1)} %broadcast_select_fusion), calls=%async_computation | async-start | bytes 7864320 | tf_op jit(solution)/shard_map/all_to_all | solution.py:40
  47.3 54.3 %collective-permute-start = (bf16[1,1536,768]{2,1,0:T(8,128)(2,1)S(1)}, bf16[1,1536,768]{2,1,0:T(8,128)(2,1)}, u32[]{:S(2)}, u32[]{:S(2)}) collective-permute-start(bf16[1,1536,768]{2,1,0:T(8,128)(2,1)S(1)} %copy-done.10), channel_id=1, source_target_pairs={{0,8},{8,0},{1,9},{9,1},{2,10},{10,2},{3,11},{11,3},{4,12},{12,4},... | collective-permute-start | bytes 7077896 | tf_op jit(solution)/shard_map/ppermute | solution.py:19
  49.0 136.8 %collective-permute-start.2 = (bf16[1,384,3072]{2,1,0:T(8,128)(2,1)}, bf16[1,384,3072]{2,1,0:T(8,128)(2,1)}, u32[]{:S(2)}, u32[]{:S(2)}) collective-permute-start(bf16[1,384,3072]{2,1,0:T(8,128)(2,1)} %param.21), channel_id=1, source_target_pairs={{0,8},{8,0},{1,9},{9,1},{2,10},{10,2},{3,11},{11,3},{4,12},{12,4},... | collective-permute-start | bytes 7077896 | tf_op jit(solution)/shard_map/ppermute | solution.py:19
  49.4 157.9 %collective-permute-start.1 = (bf16[1,384,3072]{2,1,0:T(8,128)(2,1)}, bf16[1,384,3072]{2,1,0:T(8,128)(2,1)}, u32[]{:S(2)}, u32[]{:S(2)}) collective-permute-start(bf16[1,384,3072]{2,1,0:T(8,128)(2,1)} %param.19), channel_id=1, source_target_pairs={{0,8},{8,0},{1,9},{9,1},{2,10},{10,2},{3,11},{11,3},{4,12},{12,4},... | collective-permute-start | bytes 7077896 | tf_op jit(solution)/shard_map/ppermute | solution.py:19
  141.2 13.3 %copy-start.3 = (bf16[1,2560,768]{2,1,0:T(8,128)(2,1)S(1)}, bf16[1,2560,768]{2,1,0:T(8,128)(2,1)}, u32[]{:S(2)}) copy-start(bf16[1,2560,768]{2,1,0:T(8,128)(2,1)} %param.15) | copy-start | bytes 11796484
  141.2 26.5 %slice-start = ((s8[15728640]{0:T(1024)(128)(4,1)}), s8[4194304]{0:T(1024)(128)(4,1)S(1)}, s32[]{:S(2)}) async-start(s8[15728640]{0:T(1024)(128)(4,1)} %bitcast.86), calls=%async_computation.4 | async-start | bytes 8388608
  141.2 26.5 %slice-start.1 = ((s8[15728640]{0:T(1024)(128)(4,1)}), s8[4194304]{0:T(1024)(128)(4,1)S(1)}, s32[]{:S(2)}) async-start(s8[15728640]{0:T(1024)(128)(4,1)} %bitcast.86), calls=%async_computation.5 | async-start | bytes 8388608
  141.2 26.5 %slice-start.2 = ((s8[15728640]{0:T(1024)(128)(4,1)}), s8[4194304]{0:T(1024)(128)(4,1)S(1)}, s32[]{:S(2)}) async-start(s8[15728640]{0:T(1024)(128)(4,1)} %bitcast.86), calls=%async_computation.6 | async-start | bytes 8388608
  153.0 154.4 %collective-permute-start.4 = (f32[1,1536,768]{2,1,0:T(8,128)}, f32[1,1536,768]{2,1,0:T(8,128)}, u32[]{:S(2)}, u32[]{:S(2)}) collective-permute-start(f32[1,1536,768]{2,1,0:T(8,128)} %fusion.59), channel_id=1, source_target_pairs={{0,8},{8,0},{1,9},{9,1},{2,10},{10,2},{3,11},{11,3},{4,12},{12,4},... | collective-permute-start | bytes 14155784 | tf_op jit(solution)/shard_map/ppermute | solution.py:19
  154.5 13.2 %slice-start.3 = ((s8[15728640]{0:T(1024)(128)(4,1)}), s8[3145728]{0:T(1024)(128)(4,1)S(1)}, s32[]{:S(2)}) async-start(s8[15728640]{0:T(1024)(128)(4,1)} %bitcast.86), calls=%async_computation.7 | async-start | bytes 6291456
  167.3 237.6 %collective-permute-start.5 = (f32[1,384,3072]{2,1,0:T(8,128)}, f32[1,384,3072]{2,1,0:T(8,128)}, u32[]{:S(2)}, u32[]{:S(2)}) collective-permute-start(f32[1,384,3072]{2,1,0:T(8,128)} %convolution_bitcast_fusion), channel_id=1, source_target_pairs={{0,8},{8,0},{1,9},{9,1},{2,10},{10,2},{3,11},{11,3},{4,12},{12,4},... | collective-permute-start | bytes 14155784 | tf_op jit(solution)/shard_map/ppermute | solution.py:19
  167.8 9.7 %copy-start.5 = (bf16[1,2560,768]{2,1,0:T(8,128)(2,1)S(1)}, bf16[1,2560,768]{2,1,0:T(8,128)(2,1)}, u32[]{:S(2)}) copy-start(bf16[1,2560,768]{2,1,0:T(8,128)(2,1)} %param.18) | copy-start | bytes 11796484
  175.9 9.9 %copy-start.11 = (bf16[1,384,3072]{2,1,0:T(8,128)(2,1)S(1)}, bf16[1,384,3072]{2,1,0:T(8,128)(2,1)}, u32[]{:S(2)}) copy-start(bf16[1,384,3072]{2,1,0:T(8,128)(2,1)} %param.21) | copy-start | bytes 7077892
  175.9 329.7 %collective-permute-start.3 = (f32[1,384,3072]{2,1,0:T(8,128)}, f32[1,384,3072]{2,1,0:T(8,128)}, u32[]{:S(2)}, u32[]{:S(2)}) collective-permute-start(f32[1,384,3072]{2,1,0:T(8,128)} %fusion.50), channel_id=1, source_target_pairs={{0,8},{8,0},{1,9},{9,1},{2,10},{10,2},{3,11},{11,3},{4,12},{12,4},... | collective-permute-start | bytes 14155784 | tf_op jit(solution)/shard_map/ppermute | solution.py:19
  181.4 62.2 %all-to-all-start.3 = ((f32[1,8,320]{2,0,1:T(1,128)}), f32[1,8,320]{2,0,1:T(1,128)S(1)}, u32[]{:S(2)}, u32[]{:S(2)}) async-start(f32[1,8,320]{2,0,1:T(1,128)} %reshape.293), calls=%async_computation.3 | async-start | bytes 24576 | tf_op jit(solution)/shard_map/all_to_all | solution.py:72
  243.6 50.8 %all-to-all-start.2 = ((bf16[1,8,320,768]{3,2,0,1:T(8,128)(2,1)}), bf16[1,8,320,768]{3,2,0,1:T(8,128)(2,1)}, u32[]{:S(2)}, u32[]{:S(2)}) async-start(bf16[1,8,320,768]{3,2,0,1:T(8,128)(2,1)} %bitcast.93), calls=%async_computation.2 | async-start | bytes 7864320 | tf_op jit(solution)/shard_map/all_to_all | solution.py:71
  248.1 11.9 %copy-start.4 = (bf16[1,2560,768]{2,1,0:T(8,128)(2,1)S(1)}, bf16[1,2560,768]{2,1,0:T(8,128)(2,1)}, u32[]{:S(2)}) copy-start(bf16[1,2560,768]{2,1,0:T(8,128)(2,1)} %param.15) | copy-start | bytes 11796484
  260.0 12.2 %copy-start.8 = (s32[2048]{0:T(1024)S(1)}, s32[2048]{0:T(1024)}, u32[]{:S(2)}) copy-start(s32[2048]{0:T(1024)} %broadcast_clamp_fusion) | copy-start | bytes 24580
  272.1 11.9 %copy-start.7 = (s32[2048,1]{0,1:T(1,128)S(1)}, s32[2048,1]{0,1:T(1,128)}, u32[]{:S(2)}) copy-start(s32[2048,1]{0,1:T(1,128)} %copy-done.6) | copy-start | bytes 24580
  294.4 11.1 %copy-start.9 = (pred[2048]{0:T(1024)(128)(4,1)S(1)}, pred[2048]{0:T(1024)(128)(4,1)}, u32[]{:S(2)}) copy-start(pred[2048]{0:T(1024)(128)(4,1)} %get-tuple-element.5) | copy-start | bytes 6148
  305.5 99.5 %slice-start.6 = ((s8[4718592]{0:T(1024)(128)(4,1)}), s8[4194304]{0:T(1024)(128)(4,1)S(1)}, s32[]{:S(2)}) async-start(s8[4718592]{0:T(1024)(128)(4,1)} %bitcast.90), calls=%async_computation.10 | async-start | bytes 8388608
  307.4 97.6 %slice-start.7 = ((s8[4718592]{0:T(1024)(128)(4,1)}), s8[524288]{0:T(1024)(128)(4,1)S(1)}, s32[]{:S(2)}) async-start(s8[4718592]{0:T(1024)(128)(4,1)} %bitcast.90), calls=%async_computation.11 | async-start | bytes 1048576
  307.4 198.2 %slice-start.4 = ((s8[4718592]{0:T(1024)(128)(4,1)}), s8[4194304]{0:T(1024)(128)(4,1)S(1)}, s32[]{:S(2)}) async-start(s8[4718592]{0:T(1024)(128)(4,1)} %bitcast.88), calls=%async_computation.8 | async-start | bytes 8388608
  314.5 191.2 %slice-start.5 = ((s8[4718592]{0:T(1024)(128)(4,1)}), s8[524288]{0:T(1024)(128)(4,1)S(1)}, s32[]{:S(2)}) async-start(s8[4718592]{0:T(1024)(128)(4,1)} %bitcast.88), calls=%async_computation.9 | async-start | bytes 1048576
  405.0 105.9 %copy-start.1 = (bf16[2048,768]{1,0:T(8,128)(2,1)S(1)}, bf16[2048,768]{1,0:T(8,128)(2,1)}, u32[]{:S(2)}) copy-start(bf16[2048,768]{1,0:T(8,128)(2,1)} %param.11) | copy-start | bytes 9437188

commit v2 on v1

v2 whole, which is shorter than its diff:
```python
import jax
import jax.numpy as jnp
from jax import lax
from jax.experimental import pallas as pl
from jax.experimental.pallas import tpu as pltpu
from jax.sharding import PartitionSpec as P


F32 = jnp.float32
BF16 = jnp.bfloat16
VMEM_LIMIT = 67043328


def params(*kinds):
    return pltpu.CompilerParams(dimension_semantics=kinds, vmem_limit_bytes=VMEM_LIMIT)


def cost(flops, bytes_accessed):
    return pl.CostEstimate(flops=flops, bytes_accessed=bytes_accessed, transcendentals=0)


def hidden_grads(z, g_rows, w_own, w_other, h_gate, h_up, row_tile=512, col_tile=512):
    rows, width = g_rows.shape
    half = w_own.shape[0]
    tiles = half // col_tile
    row_steps = rows // row_tile

    def col(z_ref, h, j):
        return jnp.where(h == 0, z_ref[0], 1 - z_ref[0]) * tiles + j

    def kernel(z_ref, g_ref, own_ref, other_ref, h1_ref, h3_ref, d1_ref, d3_ref, a_ref):
        h, i = pl.program_id(0), pl.program_id(2)
        g = g_ref[pl.ds(pl.multiple_of(i * row_tile, row_tile), row_tile), :]
        w = jnp.where(h == 0, own_ref[...], other_ref[...])
        d_act = lax.dot_general(g, w, (((1,), (1,)), ((), ())), preferred_element_type=F32)
        h1 = h1_ref[...].astype(F32)
        h3 = h3_ref[...].astype(F32)
        sig = jax.nn.sigmoid(h1)
        silu = h1 * sig
        a_ref[...] = (silu * h3).astype(BF16)
        d1_ref[...] = (d_act * h3 * sig * (1.0 + h1 * (1.0 - sig))).astype(BF16)
        d3_ref[...] = (d_act * silu).astype(BF16)

    tile = pl.BlockSpec((row_tile, col_tile), lambda h, j, i, z_ref: (i, col(z_ref, h, j)))
    return pl.pallas_call(
        kernel,
        grid_spec=pltpu.PrefetchScalarGridSpec(
            num_scalar_prefetch=1,
            grid=(2, tiles, row_steps),
            in_specs=[
                pl.BlockSpec((rows, width), lambda h, j, i, z_ref: (0, 0)),
                pl.BlockSpec((col_tile, width), lambda h, j, i, z_ref: (jnp.where(h == 0, j, tiles - 1), 0)),
                pl.BlockSpec((col_tile, width), lambda h, j, i, z_ref: (jnp.where(h == 0, 0, j), 0)),
                tile, tile,
            ],
            out_specs=[tile] * 3,
        ),
        out_shape=[jax.ShapeDtypeStruct(h_gate.shape, BF16)] * 3,
        compiler_params=params('arbitrary', 'arbitrary', 'arbitrary'),
        cost_estimate=cost(2 * rows * width * 2 * half, 10 * rows * 2 * half),
    )(z, g_rows, w_own, w_other, h_gate, h_up)


def weight_grad_lhs(which, wide, rhs, halves, col_tile=512):
    rows, cols = wide.shape
    width = rhs.shape[1]
    tiles = cols // halves // col_tile

    def kernel(s_ref, l_ref, r_ref, o_ref):
        o_ref[...] = lax.dot_general(l_ref[...], r_ref[...], (((0,), (0,)), ((), ())), preferred_element_type=F32)

    return pl.pallas_call(
        kernel,
        grid_spec=pltpu.PrefetchScalarGridSpec(
            num_scalar_prefetch=1,
            grid=(tiles,),
            in_specs=[
                pl.BlockSpec((rows, col_tile), lambda j, s_ref: (0, s_ref[0] * tiles + j)),
                pl.BlockSpec((rows, width), lambda j, s_ref: (0, 0)),
            ],
            out_specs=pl.BlockSpec((col_tile, width), lambda j, s_ref: (j, 0)),
        ),
        out_shape=jax.ShapeDtypeStruct((tiles * col_tile, width), F32),
        compiler_params=params('arbitrary'),
        cost_estimate=cost(2 * rows * width * tiles * col_tile, rows * cols + 4 * width * cols),
    )(which, wide, rhs)


def weight_grad_rhs(which, x_rows, wide, halves, col_tile=512):
    rows, cols = wide.shape
    part = x_rows.shape[1] // halves

    def kernel(s_ref, l_ref, r_ref, o_ref):
        o_ref[...] = lax.dot_general(l_ref[...], r_ref[...], (((0,), (0,)), ((), ())), preferred_element_type=F32)

    return pl.pallas_call(
        kernel,
        grid_spec=pltpu.PrefetchScalarGridSpec(
            num_scalar_prefetch=1,
            grid=(cols // col_tile,),
            in_specs=[
                pl.BlockSpec((rows, part), lambda j, s_ref: (0, s_ref[0])),
                pl.BlockSpec((rows, col_tile), lambda j, s_ref: (0, j)),
            ],
            out_specs=pl.BlockSpec((part, col_tile), lambda j, s_ref: (0, j)),
        ),
        out_shape=jax.ShapeDtypeStruct((part, cols), F32),
        compiler_params=params('arbitrary'),
        cost_estimate=cost(2 * rows * part * cols, 2 * rows * cols + 4 * part * cols),
    )(which, x_rows, wide)


def row_grads(z, dh_gate, dh_up, gate_own, gate_other, up_own, up_other, row_tile=256):
    rows, cols = dh_gate.shape
    part = gate_own.shape[0]

    def kernel(z_ref, d1_ref, d3_ref, g0_ref, g1_ref, u0_ref, u1_ref, o_ref):
        h = pl.program_id(0)
        dims = (((1,), (1,)), ((), ()))

        def emit(w1_ref, w3_ref):
            acc = lax.dot_general(d1_ref[...], w1_ref[...], dims, preferred_element_type=F32)
            acc += lax.dot_general(d3_ref[...], w3_ref[...], dims, preferred_element_type=F32)
            o_ref[...] = acc.astype(BF16)

        pl.when(h == 0)(lambda: emit(g0_ref, u0_ref))
        pl.when(h == 1)(lambda: emit(g1_ref, u1_ref))

    tile = pl.BlockSpec((row_tile, cols), lambda h, i, z_ref: (i, 0))
    full = pl.BlockSpec((part, cols), lambda h, i, z_ref: (0, 0))
    return pl.pallas_call(
        kernel,
        grid_spec=pltpu.PrefetchScalarGridSpec(
            num_scalar_prefetch=1,
            grid=(2, rows // row_tile),
            in_specs=[tile, tile, full, full, full, full],
            out_specs=pl.BlockSpec((row_tile, part), lambda h, i, z_ref: (i, jnp.where(h == 0, z_ref[0], 1 - z_ref[0]))),
        ),
        out_shape=jax.ShapeDtypeStruct((rows, 2 * part), BF16),
        compiler_params=params('arbitrary', 'arbitrary'),
        cost_estimate=cost(8 * rows * cols * part, 8 * rows * cols),
    )(z, dh_gate, dh_up, gate_own, gate_other, up_own, up_other)


def add_rows(own, recv, first, tile):
    rows, width = recv.shape
    base = first // tile

    def kernel(own_ref, recv_ref, o_ref):
        o_ref[...] = own_ref[...] + recv_ref[...]

    return pl.pallas_call(
        kernel,
        grid=(rows // tile,),
        in_specs=[pl.BlockSpec((tile, width), lambda i: (base + i, 0)), pl.BlockSpec((tile, width), lambda i: (i, 0))],
        out_specs=pl.BlockSpec((tile, width), lambda i: (base + i, 0)),
        out_shape=jax.ShapeDtypeStruct(own.shape, own.dtype),
        input_output_aliases={0: 0},
        compiler_params=params('arbitrary'),
        cost_estimate=cost(rows * width, 12 * rows * width),
    )(own, recv)


def solution(mesh):
    ep_n = mesh.shape['ep']
    fs_n = mesh.shape['fsdp']
    tok_spec = P(('fsdp', 'ep'), None)
    row_spec = P('ep', 'fsdp', None)
    swap = [(i, fs_n - 1 - i) for i in range(fs_n)]

    def exchange(value):
        return lax.ppermute(value, 'fsdp', swap)

    def local_backward(grad_out, expert_idx, slot_pos, gates, x_disp, h_gate, h_up, y_disp, w_gate, w_down, w_up):
        tok_n, top_n = expert_idx.shape
        e_loc, rows_loc, width = x_disp.shape
        slot_cap = rows_loc // ep_n
        slots_n = e_loc * ep_n * slot_cap
        choices = tok_n * top_n
        x_rows, y_rows, h_gate, h_up, w_gate, w_down, w_up = (v[0] for v in (x_disp, y_disp, h_gate, h_up, w_gate, w_down, w_up))

        z = lax.axis_index('fsdp').reshape(1).astype(jnp.int32)
        other_w_down = exchange(w_down)
        other_w_gate = exchange(w_gate)
        other_w_up = exchange(w_up)

        send_row = jnp.where(slot_pos >= 0, ((expert_idx % e_loc) * ep_n + expert_idx // e_loc) * slot_cap + slot_pos, slots_n).reshape(-1)
        src_choice = jnp.full((slots_n,), choices, jnp.int32).at[send_row].set(jnp.arange(choices, dtype=jnp.int32), mode='drop')
        send_dy = jnp.take(grad_out, src_choice // top_n, axis=0, mode='fill', fill_value=0).reshape(e_loc, ep_n, slot_cap, width)
        send_gate = jnp.take(gates.reshape(-1), src_choice, mode='fill', fill_value=0).reshape(e_loc, ep_n, slot_cap)
        dy_rows = lax.all_to_all(send_dy, 'ep', 1, 1, tiled=True).reshape(rows_loc, width)
        gate_rows = lax.all_to_all(send_gate, 'ep', 1, 1, tiled=True).reshape(rows_loc)
        g_rows = (dy_rows.astype(F32) * gate_rows[:, None]).astype(BF16)

        dh_gate, dh_up, act = hidden_grads(z, g_rows, w_down, other_w_down, h_gate, h_up)
        send = weight_grad_lhs(1 - z, act, g_rows, fs_n)
        recv_down = exchange(send)
        send = weight_grad_rhs(1 - z, x_rows, dh_gate, fs_n)
        recv_gate = exchange(send)
        send = weight_grad_rhs(1 - z, x_rows, dh_up, fs_n)
        step = send.shape[0] // 16
        cuts = (0, 12 * step, 15 * step, 16 * step)
        recv_up = [exchange(send[lo:hi]) for lo, hi in zip(cuts, cuts[1:])]

        dx_rows = row_grads(z, dh_gate, dh_up, w_gate, other_w_gate, w_up, other_w_up)
        dgate_rows = jnp.einsum('rd,rd->r', dy_rows, y_rows, preferred_element_type=F32)
        back_dx = lax.all_to_all(dx_rows.reshape(e_loc, ep_n, slot_cap, width), 'ep', 1, 1, tiled=True).reshape(slots_n, width)
        back_gate = lax.all_to_all(dgate_rows.reshape(e_loc, ep_n, slot_cap), 'ep', 1, 1, tiled=True).reshape(slots_n)
        picked = jnp.take(back_dx, send_row, axis=0, mode='fill', fill_value=0).reshape(tok_n, top_n, width)
        grad_x = jnp.sum(picked.astype(F32), axis=1).astype(BF16)
        grad_gates = jnp.take(back_gate, send_row, mode='fill', fill_value=0).reshape(tok_n, top_n)

        grad_w_down = weight_grad_lhs(z, act, g_rows, fs_n)
        grad_w_gate = weight_grad_rhs(z, x_rows, dh_gate, fs_n)
        grad_w_up = weight_grad_rhs(z, x_rows, dh_up, fs_n)
        grad_w_down = add_rows(grad_w_down, recv_down, 0, 128)
        grad_w_gate = add_rows(grad_w_gate, recv_gate, 0, 2 * step)
        for n, recv in enumerate(recv_up):
            grad_w_up = add_rows(grad_w_up, recv, cuts[n], step)
        return grad_x, grad_gates, grad_w_gate[None], grad_w_down[None], grad_w_up[None]

    return jax.shard_map(local_backward, mesh=mesh, in_specs=(tok_spec, tok_spec, tok_spec, tok_spec, row_spec, row_spec, row_spec, row_spec, row_spec, row_spec, row_spec), out_specs=(tok_spec, tok_spec, row_spec, row_spec, row_spec), check_vma=False)
```

time: 514 us -> 531 us (1.033)
  Pallas kernels: 0 us -> 192 us
  matrix products: 154 us -> 0 us
  waiting for transfers between devices: 245 us -> 228 us
  other arithmetic: 29.4 us -> 15.1 us
  local copies, waits for them, and re-layouts: 54.7 us -> 62.9 us
    pallas_call x0 -> x13, Pallas kernels: none -> 192 us  [the longest x4 50.1 us: weight_grad_rhs(): pl.pallas_call(kernel, grid_spec=pltpu.PrefetchScalarGridSpec(num_scalar_...]
    dot_general x9 -> x0, matrix products: 154 us -> none  [the longest x1 39.6 us: local_backward(): jnp.einsum('erd,efd->erf', g_rows, full_w_down, preferred_element_type=F32)]
    ppermute x6 -> x8, waiting for transfers between devices: 236 us -> 186 us  [exchange(): return lax.ppermute(value, 'fsdp', swap)]
    all_to_all x2, waiting for transfers between devices: 0.01 us -> 42.5 us  [the longest x1 42.5 us: local_backward(): lax.all_to_all(send_dy, 'ep', 1, 1, tiled=True).reshape(rows_loc, width)]
    add x3 -> x0, other arithmetic: 17.7 us -> none  [combine(): return lax.optimization_barrier(own) + recv]
    all_to_all x1, waiting for transfers between devices: 9.78 us -> 0.01 us  [local_backward(): lax.all_to_all(dx_rows.reshape(e_loc, ep_n, slot_cap, width), 'ep', 1, 1,...]
    slice x0 -> x3, local copies, waits for them, and re-layouts: none -> 8.03 us  [local_backward(): recv_up = [exchange(send[lo:hi]) for lo, hi in zip(cuts, cuts[1:])]]
  transfers between devices with their start and end apart: 10 -> 12, of which waited for: 4 -> 4; matrix products, arithmetic and copies ran while one was open for 41% -> 10% of each run, Pallas kernels for 0% -> 35%
where the time goes in v2:
time: 531 us; the launch traced here: 527 us
  waiting for transfers between devices  228 us (43%)
  Pallas kernels  192 us (36%)
  local copies, waits for them, and re-layouts  62.9 us (12%)
  starting transfers between devices  28 us (5%)
  other arithmetic  15.1 us (3%)
    ppermute x8, waiting for transfers between devices, exchange(): return lax.ppermute(value, 'fsdp', swap)  186 us
    pallas_call x4, Pallas kernels, weight_grad_rhs(): pl.pallas_call(kernel, grid_spec=pltpu.PrefetchScalarGridSpec(num_scalar_...  50.1 us
    pallas_call x1, Pallas kernels, hidden_grads(): pl.pallas_call(kernel, grid_spec=pltpu.PrefetchScalarGridSpec(num_scalar_...  46.2 us
    pallas_call x1, Pallas kernels, row_grads(): pl.pallas_call(kernel, grid_spec=pltpu.PrefetchScalarGridSpec(num_scalar_...  43.2 us
    all_to_all x1, waiting for transfers between devices, local_backward(): lax.all_to_all(send_dy, 'ep', 1, 1, tiled=True).reshape(rows_loc, width)  42.5 us
    pallas_call x5, Pallas kernels, add_rows(): pl.pallas_call(kernel, grid=(rows // tile,), in_specs=[pl.BlockSpec((tile...  31 us
    pallas_call x2, Pallas kernels, weight_grad_lhs(): pl.pallas_call(kernel, grid_spec=pltpu.PrefetchScalarGridSpec(num_scalar_...  21.8 us
    gather x1, local copies, waits for them, and re-layouts, local_backward(): jnp.take(gates.reshape(-1), src_choice, mode='fill', fill_value=0)  13.6 us
  transfers between devices with their start and end apart: 12, of which 4 were waited for; matrix products, arithmetic and copies ran while one was open for 10% of the time, Pallas kernels for 35%

profile of v2, /device:TPU:0, one launch (start us, length us, event | category | flops | bytes accessed | tf_op | source)
XLA Modules:
  0.0 527.4 jit_solution(13380411011791260579)
XLA Ops:
  0.6 0.0 copy-start
  0.6 1.3 fusion.4
  2.0 8.1 %scatter_custom_fusion = s32[2560]{0:T(1024)S(1)} fusion(s32[2048]{0:T(1024)S(1)} %bitcast.36, s32[2048]{0:T(1024)S(1)} %iota.3, s32[]{:T(128)} %constant.98.clone.1), kind=kCustom, calls=%fused_computation.18 | custom fusion | bytes 10244 | tf_op jit(solution)/shard_map/scatter | solution.py:188
  10.1 0.0 copy-done.2
  10.1 0.0 copy-done
  10.1 0.0 copy-start.1
  10.1 13.6 %gather_fusion.1 = f32[2560]{0:T(1024)S(1)} fusion(f32[2048]{0:T(1024)S(1)} %bitcast.26, s32[3072]{0:T(1024)S(1)} %pad_clamp_fusion), kind=kCustom, calls=%fused_computation.1 | custom fusion | bytes 30720 | tf_op jit(solution)/shard_map/jit(_take)/gather | solution.py:190
  23.7 0.7 select_n.72
  24.4 5.4 %all-to-all-start.1 = ((f32[1,8,320]{2,0,1:T(1,128)}), f32[1,8,320]{2,0,1:T(1,128)S(1)}, u32[]{:S(2)}, u32[]{:S(2)}) async-start(f32[1,8,320]{2,0,1:T(1,128)} %select_n.72), calls=%async_computation.1 | async-start | bytes 24576 | tf_op jit(solution)/shard_map/all_to_all | solution.py:192
  29.9 0.1 broadcast_in_dim.59
  29.9 0.0 copy-done.1
  29.9 8.5 %gather_fusion = bf16[2560,768]{1,0:T(8,128)(2,1)} fusion(bf16[2048,768]{1,0:T(8,128)(2,1)S(1)} %copy-done.1, s32[3072]{0:T(1024)S(1)} %pad_clamp_fusion), kind=kCustom, calls=%fused_computation | custom fusion | bytes 7874560 | tf_op jit(solution)/shard_map/jit(_take)/gather | solution.py:189
  38.4 3.7 broadcast_select_fusion
  42.2 0.0 all-to-all-done.1
  42.2 4.7 all-to-all-start
  46.9 1.6 collective-permute-start
  48.5 0.4 collective-permute-start.1
  48.9 1.6 collective-permute-start.2
  50.5 0.1 mul.21
  50.6 42.5 %all-to-all-done = bf16[1,8,320,768]{3,2,0,1:T(8,128)(2,1)} async-done(((bf16[1,8,320,768]{3,2,0,1:T(8,128)(2,1)}), bf16[1,8,320,768]{3,2,0,1:T(8,128)(2,1)}, u32[]{:S(2)}, u32[]{:S(2)}) %all-to-all-start) | async-done | bytes 3932192 | tf_op jit(solution)/shard_map/all_to_all | solution.py:191
  93.2 6.2 %fusion.1 = (f32[2560]{0:T(1024)S(1)}, bf16[2560,768]{1,0:T(8,128)(2,1)}) fusion(bf16[1,2560,768]{2,1,0:T(8,128)(2,1)} %param.18, bf16[1,8,320,768]{3,2,0,1:T(8,128)(2,1)} %all-to-all-done, f32[2560]{0:T(1024)S(1)} %mul.21), kind=kLoop, calls=%fused_computation.8 | loop fusion | flops 11793920 | bytes 11816960 | tf_op jit(solution)/shard_map/rd,rd->r/dot_general | solution.py:206
  99.3 0.7 reshape.103
  100.0 4.0 all-to-all-start.3
  103.9 0.0 collective-permute-done.other_ref
  104.0 46.2 %shard_map.146 = (bf16[2560,3072]{1,0:T(8,128)(2,1)}, bf16[2560,3072]{1,0:T(8,128)(2,1)}, bf16[2560,3072]{1,0:T(8,128)(2,1)}) custom-call(s32[1]{0:T(128)} %bitcast.z_ref.s_ref, bf16[2560,768]{1,0:T(8,128)(2,1)} %get-tuple-element.16.g_ref.r_ref, bf16[1536,768]{1,0:T(8,128)(2,1)} %bitcast.41, bf16[1536,768]{1,0:T(8,128)(2,1)} %collective-permute-done.other_ref, ...), custom_call_target="tpu_custom_call" | custom-call | flops 12079595520 | bytes 78643200 | tf_op jit(solution)/shard_map/pallas_call | solution.py:45
  150.1 12.6 %shard_map.149 = f32[384,3072]{1,0:T(8,128)} custom-call(s32[1]{0:T(128)S(6)} %sub.10.s_ref, bf16[2560,768]{1,0:T(8,128)(2,1)} %bitcast.28, bf16[2560,3072]{1,0:T(8,128)(2,1)} %get-tuple-element.8.d1_ref.r_ref), custom_call_target="tpu_custom_call" | custom-call | flops 6039797760 | bytes 20447232 | tf_op jit(solution)/shard_map/pallas_call | solution.py:96
  162.7 1.6 collective-permute-start.3
  164.3 10.9 %shard_map.152 = f32[1536,768]{1,0:T(8,128)} custom-call(s32[1]{0:T(128)S(6)} %sub.10.s_ref, bf16[2560,3072]{1,0:T(8,128)(2,1)} %get-tuple-element.10.l_ref, bf16[2560,768]{1,0:T(8,128)(2,1)} %get-tuple-element.16.g_ref.r_ref), custom_call_target="tpu_custom_call" | custom-call | flops 6039797760 | bytes 17301504 | tf_op jit(solution)/shard_map/pallas_call | solution.py:72
  175.2 0.4 collective-permute-start.4
  175.6 0.0 collective-permute-done.1.g1_ref
  175.6 26.6 %collective-permute-done.2.u1_ref = bf16[384,3072]{1,0:T(8,128)(2,1)} collective-permute-done((bf16[384,3072]{1,0:T(8,128)(2,1)}, bf16[384,3072]{1,0:T(8,128)(2,1)}, u32[]{:S(2)}, u32[]{:S(2)}) %collective-permute-start.2) | collective-permute-done | bytes 2359328 | tf_op jit(solution)/shard_map/ppermute | solution.py:172
  202.2 43.2 %shard_map.147 = bf16[2560,768]{1,0:T(8,128)(2,1)} custom-call(s32[1]{0:T(128)} %bitcast.z_ref.s_ref, bf16[2560,3072]{1,0:T(8,128)(2,1)} %get-tuple-element.8.d1_ref.r_ref, bf16[2560,3072]{1,0:T(8,128)(2,1)} %get-tuple-element.9.d3_ref.r_ref, bf16[384,3072]{1,0:T(8,128)(2,1)} %bitcast.44, bf16[384,3072]{1,0:T(8,128)(2,1)} %collective-permute-done.1.g1_ref, ...), custom_call_target="tpu_custom_call" | custom-call | flops 24159191040 | bytes 62914560 | tf_op jit(solution)/shard_map/pallas_call | solution.py:131
  245.4 0.0 all-to-all-done.3
  245.4 4.7 all-to-all-start.2
  250.1 12.5 %shard_map.155 = f32[384,3072]{1,0:T(8,128)} custom-call(s32[1]{0:T(128)S(6)} %sub.10.s_ref, bf16[2560,768]{1,0:T(8,128)(2,1)} %bitcast.29, bf16[2560,3072]{1,0:T(8,128)(2,1)} %get-tuple-element.9.d3_ref.r_ref), custom_call_target="tpu_custom_call" | custom-call | flops 6039797760 | bytes 20447232 | tf_op jit(solution)/shard_map/pallas_call | solution.py:96
  262.7 4.2 slice.20
  266.8 1.6 collective-permute-start.5
  268.4 0.0 copy-done.3
  268.4 0.6 broadcast_clamp_fusion
  269.0 1.7 slice.22
  270.7 2.2 slice.21
  272.9 0.5 collective-permute-start.7
  273.3 1.6 collective-permute-start.6
  274.9 12.5 %shard_map.154.own_ref = f32[384,3072]{1,0:T(8,128)} custom-call(s32[1]{0:T(128)} %bitcast.z_ref.s_ref, bf16[2560,768]{1,0:T(8,128)(2,1)} %bitcast.30, bf16[2560,3072]{1,0:T(8,128)(2,1)} %get-tuple-element.9.d3_ref.r_ref), custom_call_target="tpu_custom_call" | custom-call | flops 6039797760 | bytes 20447232 | tf_op jit(solution)/shard_map/pallas_call | solution.py:96
  287.4 10.9 %shard_map.151.own_ref = f32[1536,768]{1,0:T(8,128)} custom-call(s32[1]{0:T(128)} %bitcast.z_ref.s_ref, bf16[2560,3072]{1,0:T(8,128)(2,1)} %get-tuple-element.10.l_ref, bf16[2560,768]{1,0:T(8,128)(2,1)} %get-tuple-element.16.g_ref.r_ref), custom_call_target="tpu_custom_call" | custom-call | flops 6039797760 | bytes 17301504 | tf_op jit(solution)/shard_map/pallas_call | solution.py:72
  298.3 12.5 %shard_map.148.own_ref = f32[384,3072]{1,0:T(8,128)} custom-call(s32[1]{0:T(128)} %bitcast.z_ref.s_ref, bf16[2560,768]{1,0:T(8,128)(2,1)} %bitcast.31, bf16[2560,3072]{1,0:T(8,128)(2,1)} %get-tuple-element.8.d1_ref.r_ref), custom_call_target="tpu_custom_call" | custom-call | flops 6039797760 | bytes 20447232 | tf_op jit(solution)/shard_map/pallas_call | solution.py:96
  310.8 0.7 reduce.3
  311.5 0.1 reshape.104
  311.6 12.0 %gather_fusion.3 = f32[2048]{0:T(1024)S(1)} fusion(f32[2560]{0:T(1024)S(1)} %reshape.104, s32[2048]{0:T(1024)} %broadcast_clamp_fusion), kind=kCustom, calls=%fused_computation.3 | custom fusion | bytes 24576 | tf_op jit(solution)/shard_map/jit(_take)/gather | solution.py:211
  323.6 0.6 broadcast_select_fusion.3
  324.3 0.0 all-to-all-done.2
  324.3 11.1 %gather_fusion.2 = bf16[2048,768]{1,0:T(8,128)(2,1)S(1)} fusion(bf16[2560,768]{1,0:T(8,128)(2,1)} %bitcast.13, s32[2048]{0:T(1024)S(1)} %copy-done.5), kind=kCustom, calls=%fused_computation.2 | custom fusion | bytes 6299648 | tf_op jit(solution)/shard_map/jit(_take)/gather | solution.py:209
  335.4 0.0 copy-done.6
  335.4 1.9 broadcast_select_fusion.1
  337.3 143.1 %collective-permute-done.5.recv_ref = f32[288,3072]{1,0:T(8,128)} collective-permute-done((f32[288,3072]{1,0:T(8,128)}, f32[288,3072]{1,0:T(8,128)}, u32[]{:S(2)}, u32[]{:S(2)}) %collective-permute-start.5) | collective-permute-done | bytes 3538976 | tf_op jit(solution)/shard_map/ppermute | solution.py:172
  480.3 8.7 %shard_map.156.own_ref = f32[384,3072]{1,0:T(8,128)} custom-call(f32[384,3072]{1,0:T(8,128)} %shard_map.154.own_ref, f32[288,3072]{1,0:T(8,128)} %collective-permute-done.5.recv_ref), custom_call_target="tpu_custom_call", output_to_operand_aliasing={{}: (0, {})} | custom-call | flops 884736 | bytes 10616832 | tf_op jit(solution)/shard_map/pallas_call | solution.py:152
  489.0 16.0 %collective-permute-done.6.recv_ref = f32[72,3072]{1,0:T(8,128)} collective-permute-done((f32[72,3072]{1,0:T(8,128)}, f32[72,3072]{1,0:T(8,128)}, u32[]{:S(2)}, u32[]{:S(2)}) %collective-permute-start.6) | collective-permute-done | bytes 884768 | tf_op jit(solution)/shard_map/ppermute | solution.py:172
  505.1 3.1 shard_map.157.own_ref
  508.2 0.0 collective-permute-done.7.recv_ref
  508.2 1.8 shard_map.158
  510.0 0.0 collective-permute-done.3.recv_ref
  510.0 7.9 %shard_map.150 = f32[384,3072]{1,0:T(8,128)} custom-call(f32[384,3072]{1,0:T(8,128)} %shard_map.148.own_ref, f32[384,3072]{1,0:T(8,128)} %collective-permute-done.3.recv_ref), custom_call_target="tpu_custom_call", output_to_operand_aliasing={{}: (0, {})} | custom-call | flops 1179648 | bytes 14155776 | tf_op jit(solution)/shard_map/pallas_call | solution.py:152
  517.9 0.0 collective-permute-done.4.recv_ref
  517.9 9.4 %shard_map.153 = f32[1536,768]{1,0:T(8,128)} custom-call(f32[1536,768]{1,0:T(8,128)} %shard_map.151.own_ref, f32[1536,768]{1,0:T(8,128)} %collective-permute-done.4.recv_ref), custom_call_target="tpu_custom_call", output_to_operand_aliasing={{}: (0, {})} | custom-call | flops 1179648 | bytes 14155776 | tf_op jit(solution)/shard_map/pallas_call | solution.py:152
  (14 shorter events, 0.1 us)
Async XLA Ops:
  0.6 9.5 %copy-start = (f32[2048,1]{0,1:T(1,128)S(1)}, f32[2048,1]{0,1:T(1,128)}, u32[]{:S(2)}) copy-start(f32[2048,1]{0,1:T(1,128)} %param.14) | copy-start | bytes 24580
  2.0 8.1 %copy-start.2 = (s32[2048,1]{0,1:T(1,128)}, s32[2048,1]{0,1:T(1,128)S(1)}, u32[]{:S(2)}) copy-start(s32[2048,1]{0,1:T(1,128)S(1)} %get-tuple-element.12) | copy-start | bytes 24580
  10.1 19.9 %copy-start.1 = (bf16[2048,768]{1,0:T(8,128)(2,1)S(1)}, bf16[2048,768]{1,0:T(8,128)(2,1)}, u32[]{:S(2)}) copy-start(bf16[2048,768]{1,0:T(8,128)(2,1)} %param.11) | copy-start | bytes 9437188
  24.4 17.8 %all-to-all-start.1 = ((f32[1,8,320]{2,0,1:T(1,128)}), f32[1,8,320]{2,0,1:T(1,128)S(1)}, u32[]{:S(2)}, u32[]{:S(2)}) async-start(f32[1,8,320]{2,0,1:T(1,128)} %select_n.72), calls=%async_computation.1 | async-start | bytes 24576 | tf_op jit(solution)/shard_map/all_to_all | solution.py:192
  42.2 4.7 copy-start.7
  42.2 51.0 %all-to-all-start = ((bf16[1,8,320,768]{3,2,0,1:T(8,128)(2,1)}), bf16[1,8,320,768]{3,2,0,1:T(8,128)(2,1)}, u32[]{:S(2)}, u32[]{:S(2)}) async-start(bf16[1,8,320,768]{3,2,0,1:T(8,128)(2,1)} %broadcast_select_fusion), calls=%async_computation | async-start | bytes 7864320 | tf_op jit(solution)/shard_map/all_to_all | solution.py:191
  46.9 57.1 %collective-permute-start = (bf16[1536,768]{1,0:T(8,128)(2,1)S(1)}, bf16[1536,768]{1,0:T(8,128)(2,1)}, u32[]{:S(2)}, u32[]{:S(2)}) collective-permute-start(bf16[1536,768]{1,0:T(8,128)(2,1)S(1)} %bitcast.42), channel_id=1, source_target_pairs={{0,8},{8,0},{1,9},{9,1},{2,10},{10,2},{3,11},{11,3},{4,12},{12,4},... | collective-permute-start | bytes 7077896 | tf_op jit(solution)/shard_map/ppermute | solution.py:172
  48.5 127.1 %collective-permute-start.1 = (bf16[384,3072]{1,0:T(8,128)(2,1)}, bf16[384,3072]{1,0:T(8,128)(2,1)}, u32[]{:S(2)}, u32[]{:S(2)}) collective-permute-start(bf16[384,3072]{1,0:T(8,128)(2,1)} %bitcast.43), channel_id=1, source_target_pairs={{0,8},{8,0},{1,9},{9,1},{2,10},{10,2},{3,11},{11,3},{4,12},{12,4},... | collective-permute-start | bytes 7077896 | tf_op jit(solution)/shard_map/ppermute | solution.py:172
  48.9 153.3 %collective-permute-start.2 = (bf16[384,3072]{1,0:T(8,128)(2,1)}, bf16[384,3072]{1,0:T(8,128)(2,1)}, u32[]{:S(2)}, u32[]{:S(2)}) collective-permute-start(bf16[384,3072]{1,0:T(8,128)(2,1)} %bitcast.45), channel_id=1, source_target_pairs={{0,8},{8,0},{1,9},{9,1},{2,10},{10,2},{3,11},{11,3},{4,12},{12,4},... | collective-permute-start | bytes 7077896 | tf_op jit(solution)/shard_map/ppermute | solution.py:172
  100.0 145.4 %all-to-all-start.3 = ((f32[1,8,320]{2,0,1:T(1,128)}), f32[1,8,320]{2,0,1:T(1,128)}, u32[]{:S(2)}, u32[]{:S(2)}) async-start(f32[1,8,320]{2,0,1:T(1,128)} %reshape.103), calls=%async_computation.3 | async-start | bytes 24576 | tf_op jit(solution)/shard_map/all_to_all | solution.py:208
  162.7 347.3 %collective-permute-start.3 = (f32[384,3072]{1,0:T(8,128)}, f32[384,3072]{1,0:T(8,128)}, u32[]{:S(2)}, u32[]{:S(2)}) collective-permute-start(f32[384,3072]{1,0:T(8,128)} %shard_map.149), channel_id=1, source_target_pairs={{0,8},{8,0},{1,9},{9,1},{2,10},{10,2},{3,11},{11,3},{4,12},{12,4},... | collective-permute-start | bytes 14155784 | tf_op jit(solution)/shard_map/ppermute | solution.py:172
  175.2 342.8 %collective-permute-start.4 = (f32[1536,768]{1,0:T(8,128)}, f32[1536,768]{1,0:T(8,128)}, u32[]{:S(2)}, u32[]{:S(2)}) collective-permute-start(f32[1536,768]{1,0:T(8,128)} %shard_map.152), channel_id=1, source_target_pairs={{0,8},{8,0},{1,9},{9,1},{2,10},{10,2},{3,11},{11,3},{4,12},{12,4},... | collective-permute-start | bytes 14155784 | tf_op jit(solution)/shard_map/ppermute | solution.py:172
  245.4 78.8 %all-to-all-start.2 = ((bf16[1,8,320,768]{3,2,0,1:T(8,128)(2,1)}), bf16[1,8,320,768]{3,2,0,1:T(8,128)(2,1)}, u32[]{:S(2)}, u32[]{:S(2)}) async-start(bf16[1,8,320,768]{3,2,0,1:T(8,128)(2,1)} %bitcast.35), calls=%async_computation.2 | async-start | bytes 7864320 | tf_op jit(solution)/shard_map/all_to_all | solution.py:207
  262.7 5.8 %copy-start.3 = (s32[2048,1]{0,1:T(1,128)S(1)}, s32[2048,1]{0,1:T(1,128)}, u32[]{:S(2)}) copy-start(s32[2048,1]{0,1:T(1,128)} %copy-done.2) | copy-start | bytes 24580
  266.8 213.5 %collective-permute-start.5 = (f32[288,3072]{1,0:T(8,128)}, f32[288,3072]{1,0:T(8,128)}, u32[]{:S(2)}, u32[]{:S(2)}) collective-permute-start(f32[288,3072]{1,0:T(8,128)} %slice.20), channel_id=1, source_target_pairs={{0,8},{8,0},{1,9},{9,1},{2,10},{10,2},{3,11},{11,3},{4,12},{12,4},... | collective-permute-start | bytes 10616840 | tf_op jit(solution)/shard_map/ppermute | solution.py:172
  272.9 235.3 %collective-permute-start.7 = (f32[24,3072]{1,0:T(8,128)}, f32[24,3072]{1,0:T(8,128)}, u32[]{:S(2)}, u32[]{:S(2)}) collective-permute-start(f32[24,3072]{1,0:T(8,128)} %slice.22), channel_id=1, source_target_pairs={{0,8},{8,0},{1,9},{9,1},{2,10},{10,2},{3,11},{11,3},{4,12},{12,4},... | collective-permute-start | bytes 884744 | tf_op jit(solution)/shard_map/ppermute | solution.py:172
  273.3 231.7 %collective-permute-start.6 = (f32[72,3072]{1,0:T(8,128)}, f32[72,3072]{1,0:T(8,128)}, u32[]{:S(2)}, u32[]{:S(2)}) collective-permute-start(f32[72,3072]{1,0:T(8,128)} %slice.21), channel_id=1, source_target_pairs={{0,8},{8,0},{1,9},{9,1},{2,10},{10,2},{3,11},{11,3},{4,12},{12,4},... | collective-permute-start | bytes 2654216 | tf_op jit(solution)/shard_map/ppermute | solution.py:172
  311.6 12.0 %copy-start.4 = (s32[2048,1]{0,1:T(1,128)S(1)}, s32[2048,1]{0,1:T(1,128)}, u32[]{:S(2)}) copy-start(s32[2048,1]{0,1:T(1,128)} %copy-done.2) | copy-start | bytes 24580
  311.6 12.7 %copy-start.5 = (s32[2048]{0:T(1024)S(1)}, s32[2048]{0:T(1024)}, u32[]{:S(2)}) copy-start(s32[2048]{0:T(1024)} %broadcast_clamp_fusion) | copy-start | bytes 24580
  324.3 11.1 %copy-start.6 = (pred[2048]{0:T(1024)(128)(4,1)S(1)}, pred[2048]{0:T(1024)(128)(4,1)}, u32[]{:S(2)}) copy-start(pred[2048]{0:T(1024)(128)(4,1)} %get-tuple-element.11) | copy-start | bytes 6148

commit v3 on v2

--- a/solution.py
+++ b/solution.py
@@ -28,7 +28,7 @@
     def col(z_ref, h, j):
         return jnp.where(h == 0, z_ref[0], 1 - z_ref[0]) * tiles + j
 
-    def kernel(z_ref, g_ref, own_ref, other_ref, h1_ref, h3_ref, d1_ref, d3_ref, a_ref):
+    def kernel(z_ref, g_ref, own_ref, other_ref, h1_ref, h3_ref, d1_ref, d3_ref):
         h, i = pl.program_id(0), pl.program_id(2)
         g = g_ref[pl.ds(pl.multiple_of(i * row_tile, row_tile), row_tile), :]
         w = jnp.where(h == 0, own_ref[...], other_ref[...])
@@ -37,7 +37,6 @@
         h3 = h3_ref[...].astype(F32)
         sig = jax.nn.sigmoid(h1)
         silu = h1 * sig
-        a_ref[...] = (silu * h3).astype(BF16)
         d1_ref[...] = (d_act * h3 * sig * (1.0 + h1 * (1.0 - sig))).astype(BF16)
         d3_ref[...] = (d_act * silu).astype(BF16)
 
@@ -53,37 +52,47 @@
                 pl.BlockSpec((col_tile, width), lambda h, j, i, z_ref: (jnp.where(h == 0, 0, j), 0)),
                 tile, tile,
             ],
-            out_specs=[tile] * 3,
-        ),
-        out_shape=[jax.ShapeDtypeStruct(h_gate.shape, BF16)] * 3,
+            out_specs=[tile] * 2,
+        ),
+        out_shape=[jax.ShapeDtypeStruct(h_gate.shape, BF16)] * 2,
         compiler_params=params('arbitrary', 'arbitrary', 'arbitrary'),
-        cost_estimate=cost(2 * rows * width * 2 * half, 10 * rows * 2 * half),
+        cost_estimate=cost(2 * rows * width * 2 * half, 8 * rows * 2 * half),
     )(z, g_rows, w_own, w_other, h_gate, h_up)
 
 
-def weight_grad_lhs(which, wide, rhs, halves, col_tile=512):
-    rows, cols = wide.shape
-    width = rhs.shape[1]
+def down_grad(which, h_gate, h_up, g_rows, halves, row_tile=512, col_tile=512):
+    rows, cols = h_gate.shape
+    width = g_rows.shape[1]
     tiles = cols // halves // col_tile
 
-    def kernel(s_ref, l_ref, r_ref, o_ref):
-        o_ref[...] = lax.dot_general(l_ref[...], r_ref[...], (((0,), (0,)), ((), ())), preferred_element_type=F32)
-
-    return pl.pallas_call(
-        kernel,
-        grid_spec=pltpu.PrefetchScalarGridSpec(
-            num_scalar_prefetch=1,
-            grid=(tiles,),
-            in_specs=[
-                pl.BlockSpec((rows, col_tile), lambda j, s_ref: (0, s_ref[0] * tiles + j)),
-                pl.BlockSpec((rows, width), lambda j, s_ref: (0, 0)),
-            ],
-            out_specs=pl.BlockSpec((col_tile, width), lambda j, s_ref: (j, 0)),
+    def kernel(s_ref, h1_ref, h3_ref, g_ref, o_ref):
+        i = pl.program_id(1)
+        h1 = h1_ref[...].astype(F32)
+        act = (h1 * jax.nn.sigmoid(h1) * h3_ref[...].astype(F32)).astype(BF16)
+        g = g_ref[pl.ds(pl.multiple_of(i * row_tile, row_tile), row_tile), :]
+        term = lax.dot_general(act, g, (((0,), (0,)), ((), ())), preferred_element_type=F32)
+
+        @pl.when(i == 0)
+        def _():
+            o_ref[...] = term
+
+        @pl.when(i > 0)
+        def _():
+            o_ref[...] += term
+
+    tile = pl.BlockSpec((row_tile, col_tile), lambda j, i, s_ref: (i, s_ref[0] * tiles + j))
+    return pl.pallas_call(
+        kernel,
+        grid_spec=pltpu.PrefetchScalarGridSpec(
+            num_scalar_prefetch=1,
+            grid=(tiles, rows // row_tile),
+            in_specs=[tile, tile, pl.BlockSpec((rows, width), lambda j, i, s_ref: (0, 0))],
+            out_specs=pl.BlockSpec((col_tile, width), lambda j, i, s_ref: (j, 0)),
         ),
         out_shape=jax.ShapeDtypeStruct((tiles * col_tile, width), F32),
-        compiler_params=params('arbitrary'),
-        cost_estimate=cost(2 * rows * width * tiles * col_tile, rows * cols + 4 * width * cols),
-    )(which, wide, rhs)
+        compiler_params=params('arbitrary', 'arbitrary'),
+        cost_estimate=cost(2 * rows * width * tiles * col_tile, 4 * rows * cols),
+    )(which, h_gate, h_up, g_rows)
 
 
 def weight_grad_rhs(which, x_rows, wide, halves, col_tile=512):
@@ -192,14 +201,15 @@
         gate_rows = lax.all_to_all(send_gate, 'ep', 1, 1, tiled=True).reshape(rows_loc)
         g_rows = (dy_rows.astype(F32) * gate_rows[:, None]).astype(BF16)
 
-        dh_gate, dh_up, act = hidden_grads(z, g_rows, w_down, other_w_down, h_gate, h_up)
-        send = weight_grad_lhs(1 - z, act, g_rows, fs_n)
+        send = down_grad(1 - z, h_gate, h_up, g_rows, fs_n)
         recv_down = exchange(send)
+        dh_gate, dh_up = hidden_grads(z, g_rows, w_down, other_w_down, h_gate, h_up)
         send = weight_grad_rhs(1 - z, x_rows, dh_gate, fs_n)
         recv_gate = exchange(send)
         send = weight_grad_rhs(1 - z, x_rows, dh_up, fs_n)
         step = send.shape[0] // 16
-        cuts = (0, 12 * step, 15 * step, 16 * step)
+        cuts = (0, 12 * step, 15 * step, 15 * step + 2 * step // 3, 16 * step)
+        tiles = (4 * step, 3 * step, step // 3, step // 3)
         recv_up = [exchange(send[lo:hi]) for lo, hi in zip(cuts, cuts[1:])]
 
         dx_rows = row_grads(z, dh_gate, dh_up, w_gate, other_w_gate, w_up, other_w_up)
@@ -210,13 +220,13 @@
         grad_x = jnp.sum(picked.astype(F32), axis=1).astype(BF16)
         grad_gates = jnp.take(back_gate, send_row, mode='fill', fill_value=0).reshape(tok_n, top_n)
 
-        grad_w_down = weight_grad_lhs(z, act, g_rows, fs_n)
+        grad_w_down = down_grad(z, h_gate, h_up, g_rows, fs_n)
         grad_w_gate = weight_grad_rhs(z, x_rows, dh_gate, fs_n)
         grad_w_up = weight_grad_rhs(z, x_rows, dh_up, fs_n)
-        grad_w_down = add_rows(grad_w_down, recv_down, 0, 128)
-        grad_w_gate = add_rows(grad_w_gate, recv_gate, 0, 2 * step)
+        grad_w_down = add_rows(grad_w_down, recv_down, 0, 384)
+        grad_w_gate = add_rows(grad_w_gate, recv_gate, 0, 4 * step)
         for n, recv in enumerate(recv_up):
-            grad_w_up = add_rows(grad_w_up, recv, cuts[n], step)
+            grad_w_up = add_rows(grad_w_up, recv, cuts[n], tiles[n])
         return grad_x, grad_gates, grad_w_gate[None], grad_w_down[None], grad_w_up[None]
 
     return jax.shard_map(local_backward, mesh=mesh, in_specs=(tok_spec, tok_spec, tok_spec, tok_spec, row_spec, row_spec, row_spec, row_spec, row_spec, row_spec, row_spec), out_specs=(tok_spec, tok_spec, row_spec, row_spec, row_spec), check_vma=False)

time: 531 us -> 522 us (0.983)
  waiting for transfers between devices: 228 us -> 209 us
  Pallas kernels: 192 us -> 201 us
    pallas_call x2, Pallas kernels: 21.8 us -> 41.7 us  [down_grad(): pl.pallas_call(kernel, grid_spec=pltpu.PrefetchScalarGridSpec(num_scalar_...]
    ppermute x8 -> x9, waiting for transfers between devices: 186 us -> 166 us  [exchange(): return lax.ppermute(value, 'fsdp', swap)]
    pallas_call x5 -> x6, Pallas kernels: 31 us -> 23.5 us  [add_rows(): pl.pallas_call(kernel, grid=(rows // tile,), in_specs=[pl.BlockSpec((tile...]
    ppermute x8 -> x9, starting transfers between devices: 9.26 us -> 10.9 us  [exchange(): return lax.ppermute(value, 'fsdp', swap)]
  transfers between devices with their start and end apart: 12 -> 13, of which waited for: 4 -> 5; matrix products, arithmetic and copies ran while one was open for 10% -> 11% of each run, Pallas kernels for 35% -> 37%
where the time goes in v3:
time: 522 us; the launch traced here: 519 us
  waiting for transfers between devices  209 us (40%)
  Pallas kernels  201 us (39%)
  local copies, waits for them, and re-layouts  64.4 us (12%)
  starting transfers between devices  29.6 us (6%)
  other arithmetic  15.2 us (3%)
    ppermute x9, waiting for transfers between devices, exchange(): return lax.ppermute(value, 'fsdp', swap)  166 us
    pallas_call x4, Pallas kernels, weight_grad_rhs(): pl.pallas_call(kernel, grid_spec=pltpu.PrefetchScalarGridSpec(num_scalar_...  50.1 us
    pallas_call x1, Pallas kernels, row_grads(): pl.pallas_call(kernel, grid_spec=pltpu.PrefetchScalarGridSpec(num_scalar_...  43.2 us
    all_to_all x1, waiting for transfers between devices, local_backward(): lax.all_to_all(send_dy, 'ep', 1, 1, tiled=True).reshape(rows_loc, width)  42.5 us
    pallas_call x1, Pallas kernels, hidden_grads(): pl.pallas_call(kernel, grid_spec=pltpu.PrefetchScalarGridSpec(num_scalar_...  42.1 us
    pallas_call x2, Pallas kernels, down_grad(): pl.pallas_call(kernel, grid_spec=pltpu.PrefetchScalarGridSpec(num_scalar_...  41.7 us
    pallas_call x6, Pallas kernels, add_rows(): pl.pallas_call(kernel, grid=(rows // tile,), in_specs=[pl.BlockSpec((tile...  23.5 us
    gather x1, local copies, waits for them, and re-layouts, local_backward(): jnp.take(gates.reshape(-1), src_choice, mode='fill', fill_value=0)  13.6 us
  transfers between devices with their start and end apart: 13, of which 5 were waited for; matrix products, arithmetic and copies ran while one was open for 11% of the time, Pallas kernels for 37%

profile of v3, /device:TPU:0, one launch (start us, length us, event | category | flops | bytes accessed | tf_op | source)
XLA Modules:
  0.0 519.1 jit_solution(3999080455946031136)
XLA Ops:
  0.6 0.0 copy-start
  0.6 1.3 fusion.4
  2.0 8.1 %scatter_custom_fusion = s32[2560]{0:T(1024)S(1)} fusion(s32[2048]{0:T(1024)S(1)} %bitcast.41, s32[2048]{0:T(1024)S(1)} %iota.3, s32[]{:T(128)} %constant.98.clone.1), kind=kCustom, calls=%fused_computation.18 | custom fusion | bytes 10244 | tf_op jit(solution)/shard_map/scatter | solution.py:197
  10.1 0.0 copy-start.1
  10.1 13.6 %gather_fusion.1 = f32[2560]{0:T(1024)S(1)} fusion(f32[2048]{0:T(1024)S(1)} %bitcast.25, s32[3072]{0:T(1024)S(1)} %pad_clamp_fusion), kind=kCustom, calls=%fused_computation.1 | custom fusion | bytes 30720 | tf_op jit(solution)/shard_map/jit(_take)/gather | solution.py:199
  23.8 0.7 select_n.72
  24.4 5.4 %all-to-all-start.1 = ((f32[1,8,320]{2,0,1:T(1,128)}), f32[1,8,320]{2,0,1:T(1,128)S(1)}, u32[]{:S(2)}, u32[]{:S(2)}) async-start(f32[1,8,320]{2,0,1:T(1,128)} %select_n.72), calls=%async_computation.1 | async-start | bytes 24576 | tf_op jit(solution)/shard_map/all_to_all | solution.py:201
  29.9 8.5 %gather_fusion = bf16[2560,768]{1,0:T(8,128)(2,1)} fusion(bf16[2048,768]{1,0:T(8,128)(2,1)S(1)} %copy-done.1, s32[3072]{0:T(1024)S(1)} %pad_clamp_fusion), kind=kCustom, calls=%fused_computation | custom fusion | bytes 7874560 | tf_op jit(solution)/shard_map/jit(_take)/gather | solution.py:198
  38.4 0.1 broadcast_in_dim.59
  38.5 3.7 broadcast_select_fusion
  42.2 0.0 all-to-all-done.1
  42.2 4.7 all-to-all-start
  46.9 1.6 collective-permute-start
  48.5 0.4 collective-permute-start.1
  49.0 1.6 collective-permute-start.2
  50.6 0.1 mul.21
  50.6 42.5 %all-to-all-done = bf16[1,8,320,768]{3,2,0,1:T(8,128)(2,1)} async-done(((bf16[1,8,320,768]{3,2,0,1:T(8,128)(2,1)}), bf16[1,8,320,768]{3,2,0,1:T(8,128)(2,1)}, u32[]{:S(2)}, u32[]{:S(2)}) %all-to-all-start) | async-done | bytes 3932192 | tf_op jit(solution)/shard_map/all_to_all | solution.py:200
  93.2 6.2 %fusion.1 = (f32[2560]{0:T(1024)S(1)}, bf16[2560,768]{1,0:T(8,128)(2,1)}) fusion(bf16[1,2560,768]{2,1,0:T(8,128)(2,1)} %param.18, bf16[1,8,320,768]{3,2,0,1:T(8,128)(2,1)} %all-to-all-done, f32[2560]{0:T(1024)S(1)} %mul.21), kind=kLoop, calls=%fused_computation.8 | loop fusion | flops 11793920 | bytes 11816960 | tf_op jit(solution)/shard_map/rd,rd->r/dot_general | solution.py:216
  99.4 0.7 reshape.103
  100.1 3.9 all-to-all-start.3
  104.0 0.0 collective-permute-done.other_ref
  104.0 42.1 %shard_map.146 = (bf16[2560,3072]{1,0:T(8,128)(2,1)}, bf16[2560,3072]{1,0:T(8,128)(2,1)}) custom-call(s32[1]{0:T(128)} %bitcast.z_ref.s_ref, bf16[2560,768]{1,0:T(8,128)(2,1)} %get-tuple-element.14.g_ref, bf16[1536,768]{1,0:T(8,128)(2,1)} %bitcast.44, bf16[1536,768]{1,0:T(8,128)(2,1)} %collective-permute-done.other_ref, bf16[2560,3072]{1,0:T(8,128)(2,1)} %bitcast.27, ...), custom_call_target="tpu_custom_call" | custom-call | flops 12079595520 | bytes 62914560 | tf_op jit(solution)/shard_map/pallas_call | solution.py:44
  146.1 12.5 %shard_map.149 = f32[384,3072]{1,0:T(8,128)} custom-call(s32[1]{0:T(128)S(6)} %sub.10.s_ref, bf16[2560,768]{1,0:T(8,128)(2,1)} %bitcast.33, bf16[2560,3072]{1,0:T(8,128)(2,1)} %get-tuple-element.7.d1_ref.r_ref), custom_call_target="tpu_custom_call" | custom-call | flops 6039797760 | bytes 20447232 | tf_op jit(solution)/shard_map/pallas_call | solution.py:105
  158.7 1.6 collective-permute-start.3
  160.3 20.9 %shard_map.152 = f32[1536,768]{1,0:T(8,128)} custom-call(s32[1]{0:T(128)S(6)} %sub.10.s_ref, bf16[2560,3072]{1,0:T(8,128)(2,1)} %bitcast.28, bf16[2560,3072]{1,0:T(8,128)(2,1)} %bitcast.31, bf16[2560,768]{1,0:T(8,128)(2,1)} %get-tuple-element.14.g_ref), custom_call_target="tpu_custom_call" | custom-call | flops 6039797760 | bytes 31457280 | tf_op jit(solution)/shard_map/pallas_call | solution.py:84
  181.1 0.4 collective-permute-start.4
  181.5 12.5 %shard_map.155 = f32[384,3072]{1,0:T(8,128)} custom-call(s32[1]{0:T(128)S(6)} %sub.10.s_ref, bf16[2560,768]{1,0:T(8,128)(2,1)} %bitcast.34, bf16[2560,3072]{1,0:T(8,128)(2,1)} %get-tuple-element.8.d3_ref.r_ref), custom_call_target="tpu_custom_call" | custom-call | flops 6039797760 | bytes 20447232 | tf_op jit(solution)/shard_map/pallas_call | solution.py:105
  194.0 4.2 slice.24
  198.2 1.6 collective-permute-start.5
  199.8 0.0 collective-permute-done.1.g1_ref
  199.8 2.4 collective-permute-done.2.u1_ref
  202.3 43.2 %shard_map.147 = bf16[2560,768]{1,0:T(8,128)(2,1)} custom-call(s32[1]{0:T(128)} %bitcast.z_ref.s_ref, bf16[2560,3072]{1,0:T(8,128)(2,1)} %get-tuple-element.7.d1_ref.r_ref, bf16[2560,3072]{1,0:T(8,128)(2,1)} %get-tuple-element.8.d3_ref.r_ref, bf16[384,3072]{1,0:T(8,128)(2,1)} %bitcast.47, bf16[384,3072]{1,0:T(8,128)(2,1)} %collective-permute-done.1.g1_ref, ...), custom_call_target="tpu_custom_call" | custom-call | flops 24159191040 | bytes 62914560 | tf_op jit(solution)/shard_map/pallas_call | solution.py:140
  245.5 0.0 all-to-all-done.3
  245.5 4.7 all-to-all-start.2
  250.2 0.6 broadcast_clamp_fusion
  250.8 2.2 slice.25
  253.0 1.6 slice.26
  254.6 1.5 slice.27
  256.1 1.6 collective-permute-start.6
  257.7 0.5 collective-permute-start.7
  258.1 12.5 %shard_map.148.own_ref = f32[384,3072]{1,0:T(8,128)} custom-call(s32[1]{0:T(128)} %bitcast.z_ref.s_ref, bf16[2560,768]{1,0:T(8,128)(2,1)} %bitcast.35, bf16[2560,3072]{1,0:T(8,128)(2,1)} %get-tuple-element.7.d1_ref.r_ref), custom_call_target="tpu_custom_call" | custom-call | flops 6039797760 | bytes 20447232 | tf_op jit(solution)/shard_map/pallas_call | solution.py:105
  270.7 20.9 %shard_map.151.own_ref = f32[1536,768]{1,0:T(8,128)} custom-call(s32[1]{0:T(128)} %bitcast.z_ref.s_ref, bf16[2560,3072]{1,0:T(8,128)(2,1)} %bitcast.29, bf16[2560,3072]{1,0:T(8,128)(2,1)} %bitcast.32, bf16[2560,768]{1,0:T(8,128)(2,1)} %get-tuple-element.14.g_ref), custom_call_target="tpu_custom_call" | custom-call | flops 6039797760 | bytes 31457280 | tf_op jit(solution)/shard_map/pallas_call | solution.py:84
  291.5 12.5 %shard_map.154.own_ref = f32[384,3072]{1,0:T(8,128)} custom-call(s32[1]{0:T(128)} %bitcast.z_ref.s_ref, bf16[2560,768]{1,0:T(8,128)(2,1)} %bitcast.36, bf16[2560,3072]{1,0:T(8,128)(2,1)} %get-tuple-element.8.d3_ref.r_ref), custom_call_target="tpu_custom_call" | custom-call | flops 6039797760 | bytes 20447232 | tf_op jit(solution)/shard_map/pallas_call | solution.py:105
  304.0 0.7 reduce.3
  304.8 0.1 reshape.104
  304.8 12.0 %gather_fusion.3 = f32[2048]{0:T(1024)S(1)} fusion(f32[2560]{0:T(1024)S(1)} %reshape.104, s32[2048]{0:T(1024)} %broadcast_clamp_fusion), kind=kCustom, calls=%fused_computation.3 | custom fusion | bytes 24576 | tf_op jit(solution)/shard_map/jit(_take)/gather | solution.py:221
  316.9 0.6 broadcast_select_fusion.3
  317.5 0.0 all-to-all-done.2
  317.5 0.0 copy-done.5
  317.5 11.1 %gather_fusion.2 = bf16[2048,768]{1,0:T(8,128)(2,1)S(1)} fusion(bf16[2560,768]{1,0:T(8,128)(2,1)} %bitcast.13, s32[2048]{0:T(1024)S(1)} %copy-done.5), kind=kCustom, calls=%fused_computation.2 | custom fusion | bytes 6299648 | tf_op jit(solution)/shard_map/jit(_take)/gather | solution.py:219
  328.6 151.7 %collective-permute-done.5.recv_ref = f32[288,3072]{1,0:T(8,128)} collective-permute-done((f32[288,3072]{1,0:T(8,128)}, f32[288,3072]{1,0:T(8,128)}, u32[]{:S(2)}, u32[]{:S(2)}) %collective-permute-start.5) | collective-permute-done | bytes 3538976 | tf_op jit(solution)/shard_map/ppermute | solution.py:181
  480.3 1.6 collective-permute-start.8
  481.9 1.9 broadcast_select_fusion.1
  483.8 5.5 %shard_map.156.own_ref = f32[384,3072]{1,0:T(8,128)} custom-call(f32[384,3072]{1,0:T(8,128)} %shard_map.154.own_ref, f32[288,3072]{1,0:T(8,128)} %collective-permute-done.5.recv_ref), custom_call_target="tpu_custom_call", output_to_operand_aliasing={{}: (0, {})} | custom-call | flops 884736 | bytes 10616832 | tf_op jit(solution)/shard_map/pallas_call | solution.py:161
  489.3 10.0 %collective-permute-done.6.recv_ref = f32[72,3072]{1,0:T(8,128)} collective-permute-done((f32[72,3072]{1,0:T(8,128)}, f32[72,3072]{1,0:T(8,128)}, u32[]{:S(2)}, u32[]{:S(2)}) %collective-permute-start.6) | collective-permute-done | bytes 884768 | tf_op jit(solution)/shard_map/ppermute | solution.py:181
  499.3 2.4 shard_map.157.own_ref
  501.7 1.8 collective-permute-done.7.recv_ref
  503.5 1.7 shard_map.158.own_ref
  505.2 0.0 collective-permute-done.8.recv_ref
  505.2 1.6 shard_map.159
  506.8 0.0 collective-permute-done.3.recv_ref
  506.8 6.1 %shard_map.150 = f32[384,3072]{1,0:T(8,128)} custom-call(f32[384,3072]{1,0:T(8,128)} %shard_map.148.own_ref, f32[384,3072]{1,0:T(8,128)} %collective-permute-done.3.recv_ref), custom_call_target="tpu_custom_call", output_to_operand_aliasing={{}: (0, {})} | custom-call | flops 1179648 | bytes 14155776 | tf_op jit(solution)/shard_map/pallas_call | solution.py:161
  513.0 0.0 collective-permute-done.4.recv_ref
  513.0 6.2 %shard_map.153 = f32[1536,768]{1,0:T(8,128)} custom-call(f32[1536,768]{1,0:T(8,128)} %shard_map.151.own_ref, f32[1536,768]{1,0:T(8,128)} %collective-permute-done.4.recv_ref), custom_call_target="tpu_custom_call", output_to_operand_aliasing={{}: (0, {})} | custom-call | flops 1179648 | bytes 14155776 | tf_op jit(solution)/shard_map/pallas_call | solution.py:161
  (18 shorter events, 0.1 us)
Async XLA Ops:
  0.6 9.5 %copy-start = (f32[2048,1]{0,1:T(1,128)S(1)}, f32[2048,1]{0,1:T(1,128)}, u32[]{:S(2)}) copy-start(f32[2048,1]{0,1:T(1,128)} %param.14) | copy-start | bytes 24580
  2.0 8.1 %copy-start.2 = (s32[2048,1]{0,1:T(1,128)}, s32[2048,1]{0,1:T(1,128)S(1)}, u32[]{:S(2)}) copy-start(s32[2048,1]{0,1:T(1,128)S(1)} %get-tuple-element.10) | copy-start | bytes 24580
  10.1 19.8 %copy-start.1 = (bf16[2048,768]{1,0:T(8,128)(2,1)S(1)}, bf16[2048,768]{1,0:T(8,128)(2,1)}, u32[]{:S(2)}) copy-start(bf16[2048,768]{1,0:T(8,128)(2,1)} %param.11) | copy-start | bytes 9437188
  24.4 17.8 %all-to-all-start.1 = ((f32[1,8,320]{2,0,1:T(1,128)}), f32[1,8,320]{2,0,1:T(1,128)S(1)}, u32[]{:S(2)}, u32[]{:S(2)}) async-start(f32[1,8,320]{2,0,1:T(1,128)} %select_n.72), calls=%async_computation.1 | async-start | bytes 24576 | tf_op jit(solution)/shard_map/all_to_all | solution.py:201
  42.2 4.7 copy-start.7
  42.2 51.0 %all-to-all-start = ((bf16[1,8,320,768]{3,2,0,1:T(8,128)(2,1)}), bf16[1,8,320,768]{3,2,0,1:T(8,128)(2,1)}, u32[]{:S(2)}, u32[]{:S(2)}) async-start(bf16[1,8,320,768]{3,2,0,1:T(8,128)(2,1)} %broadcast_select_fusion), calls=%async_computation | async-start | bytes 7864320 | tf_op jit(solution)/shard_map/all_to_all | solution.py:200
  46.9 57.1 %collective-permute-start = (bf16[1536,768]{1,0:T(8,128)(2,1)S(1)}, bf16[1536,768]{1,0:T(8,128)(2,1)}, u32[]{:S(2)}, u32[]{:S(2)}) collective-permute-start(bf16[1536,768]{1,0:T(8,128)(2,1)S(1)} %bitcast.45), channel_id=1, source_target_pairs={{0,8},{8,0},{1,9},{9,1},{2,10},{10,2},{3,11},{11,3},{4,12},{12,4},... | collective-permute-start | bytes 7077896 | tf_op jit(solution)/shard_map/ppermute | solution.py:181
  48.5 151.3 %collective-permute-start.1 = (bf16[384,3072]{1,0:T(8,128)(2,1)}, bf16[384,3072]{1,0:T(8,128)(2,1)}, u32[]{:S(2)}, u32[]{:S(2)}) collective-permute-start(bf16[384,3072]{1,0:T(8,128)(2,1)} %bitcast.46), channel_id=1, source_target_pairs={{0,8},{8,0},{1,9},{9,1},{2,10},{10,2},{3,11},{11,3},{4,12},{12,4},... | collective-permute-start | bytes 7077896 | tf_op jit(solution)/shard_map/ppermute | solution.py:181
  49.0 153.3 %collective-permute-start.2 = (bf16[384,3072]{1,0:T(8,128)(2,1)}, bf16[384,3072]{1,0:T(8,128)(2,1)}, u32[]{:S(2)}, u32[]{:S(2)}) collective-permute-start(bf16[384,3072]{1,0:T(8,128)(2,1)} %bitcast.48), channel_id=1, source_target_pairs={{0,8},{8,0},{1,9},{9,1},{2,10},{10,2},{3,11},{11,3},{4,12},{12,4},... | collective-permute-start | bytes 7077896 | tf_op jit(solution)/shard_map/ppermute | solution.py:181
  100.1 145.4 %all-to-all-start.3 = ((f32[1,8,320]{2,0,1:T(1,128)}), f32[1,8,320]{2,0,1:T(1,128)}, u32[]{:S(2)}, u32[]{:S(2)}) async-start(f32[1,8,320]{2,0,1:T(1,128)} %reshape.103), calls=%async_computation.3 | async-start | bytes 24576 | tf_op jit(solution)/shard_map/all_to_all | solution.py:218
  158.7 348.1 %collective-permute-start.3 = (f32[384,3072]{1,0:T(8,128)}, f32[384,3072]{1,0:T(8,128)}, u32[]{:S(2)}, u32[]{:S(2)}) collective-permute-start(f32[384,3072]{1,0:T(8,128)} %shard_map.149), channel_id=1, source_target_pairs={{0,8},{8,0},{1,9},{9,1},{2,10},{10,2},{3,11},{11,3},{4,12},{12,4},... | collective-permute-start | bytes 14155784 | tf_op jit(solution)/shard_map/ppermute | solution.py:181
  181.1 331.8 %collective-permute-start.4 = (f32[1536,768]{1,0:T(8,128)}, f32[1536,768]{1,0:T(8,128)}, u32[]{:S(2)}, u32[]{:S(2)}) collective-permute-start(f32[1536,768]{1,0:T(8,128)} %shard_map.152), channel_id=1, source_target_pairs={{0,8},{8,0},{1,9},{9,1},{2,10},{10,2},{3,11},{11,3},{4,12},{12,4},... | collective-permute-start | bytes 14155784 | tf_op jit(solution)/shard_map/ppermute | solution.py:181
  198.2 282.1 %collective-permute-start.5 = (f32[288,3072]{1,0:T(8,128)}, f32[288,3072]{1,0:T(8,128)}, u32[]{:S(2)}, u32[]{:S(2)}) collective-permute-start(f32[288,3072]{1,0:T(8,128)} %slice.24), channel_id=1, source_target_pairs={{0,8},{8,0},{1,9},{9,1},{2,10},{10,2},{3,11},{11,3},{4,12},{12,4},... | collective-permute-start | bytes 10616840 | tf_op jit(solution)/shard_map/ppermute | solution.py:181
  245.5 4.7 copy-start.3
  245.5 72.1 %all-to-all-start.2 = ((bf16[1,8,320,768]{3,2,0,1:T(8,128)(2,1)}), bf16[1,8,320,768]{3,2,0,1:T(8,128)(2,1)}, u32[]{:S(2)}, u32[]{:S(2)}) async-start(bf16[1,8,320,768]{3,2,0,1:T(8,128)(2,1)} %bitcast.40), calls=%async_computation.2 | async-start | bytes 7864320 | tf_op jit(solution)/shard_map/all_to_all | solution.py:217
  256.1 243.2 %collective-permute-start.6 = (f32[72,3072]{1,0:T(8,128)}, f32[72,3072]{1,0:T(8,128)}, u32[]{:S(2)}, u32[]{:S(2)}) collective-permute-start(f32[72,3072]{1,0:T(8,128)} %slice.25), channel_id=1, source_target_pairs={{0,8},{8,0},{1,9},{9,1},{2,10},{10,2},{3,11},{11,3},{4,12},{12,4},... | collective-permute-start | bytes 2654216 | tf_op jit(solution)/shard_map/ppermute | solution.py:181
  257.7 245.8 %collective-permute-start.7 = (f32[16,3072]{1,0:T(8,128)}, f32[16,3072]{1,0:T(8,128)}, u32[]{:S(2)}, u32[]{:S(2)}) collective-permute-start(f32[16,3072]{1,0:T(8,128)} %slice.26), channel_id=1, source_target_pairs={{0,8},{8,0},{1,9},{9,1},{2,10},{10,2},{3,11},{11,3},{4,12},{12,4},... | collective-permute-start | bytes 589832 | tf_op jit(solution)/shard_map/ppermute | solution.py:181
  304.8 12.0 %copy-start.4 = (s32[2048,1]{0,1:T(1,128)S(1)}, s32[2048,1]{0,1:T(1,128)}, u32[]{:S(2)}) copy-start(s32[2048,1]{0,1:T(1,128)} %copy-done.2) | copy-start | bytes 24580
  304.8 12.7 %copy-start.5 = (s32[2048]{0:T(1024)S(1)}, s32[2048]{0:T(1024)}, u32[]{:S(2)}) copy-start(s32[2048]{0:T(1024)} %broadcast_clamp_fusion) | copy-start | bytes 24580
  317.5 164.4 %copy-start.6 = (pred[2048]{0:T(1024)(128)(4,1)S(1)}, pred[2048]{0:T(1024)(128)(4,1)}, u32[]{:S(2)}) copy-start(pred[2048]{0:T(1024)(128)(4,1)} %get-tuple-element.9) | copy-start | bytes 6148
  480.3 24.9 %collective-permute-start.8 = (f32[8,3072]{1,0:T(8,128)}, f32[8,3072]{1,0:T(8,128)}, u32[]{:S(2)}, u32[]{:S(2)}) collective-permute-start(f32[8,3072]{1,0:T(8,128)} %slice.27), channel_id=1, source_target_pairs={{0,8},{8,0},{1,9},{9,1},{2,10},{10,2},{3,11},{11,3},{4,12},{12,4},... | collective-permute-start | bytes 294920 | tf_op jit(solution)/shard_map/ppermute | solution.py:181

commit v4 on v3

--- a/solution.py
+++ b/solution.py
@@ -8,7 +8,7 @@
 
 F32 = jnp.float32
 BF16 = jnp.bfloat16
-VMEM_LIMIT = 67043328
+VMEM_LIMIT = 58 * 1024 * 1024
 
 
 def params(*kinds):
@@ -170,6 +170,56 @@
     )(own, recv)
 
 
+def add_piece(own, recv, first):
+    rows, width = recv.shape
+
+    def kernel(own_ref, recv_ref, o_ref, here, there, sem):
+        place = pl.ds(first, rows)
+        ins = (pltpu.make_async_copy(own_ref.at[place], here, sem.at[0]), pltpu.make_async_copy(recv_ref, there, sem.at[1]))
+        for copy in ins:
+            copy.start()
+        for copy in ins:
+            copy.wait()
+        here[...] += there[...]
+        out = pltpu.make_async_copy(here, o_ref.at[place], sem.at[2])
+        out.start()
+        out.wait()
+
+    return pl.pallas_call(
+        kernel,
+        in_specs=[pl.BlockSpec(memory_space=pl.ANY)] * 2,
+        out_specs=pl.BlockSpec(memory_space=pl.ANY),
+        out_shape=jax.ShapeDtypeStruct(own.shape, own.dtype),
+        scratch_shapes=[pltpu.VMEM((rows, width), F32)] * 2 + [pltpu.SemaphoreType.DMA((3,))],
+        input_output_aliases={0: 0},
+        compiler_params=params(),
+        cost_estimate=cost(rows * width, 12 * rows * width),
+    )(own, recv)
+
+
+def add_last(own, tail, recv):
+    rows, width = recv.shape
+    first = own.shape[0] - rows
+
+    def kernel(own_ref, tail_ref, recv_ref, o_ref, total, sem):
+        total[...] = tail_ref[...] + recv_ref[...]
+        out = pltpu.make_async_copy(total, o_ref.at[pl.ds(first, rows)], sem)
+        out.start()
+        out.wait()
+
+    vmem = pl.BlockSpec(memory_space=pltpu.VMEM)
+    return pl.pallas_call(
+        kernel,
+        in_specs=[pl.BlockSpec(memory_space=pl.ANY), vmem, vmem],
+        out_specs=pl.BlockSpec(memory_space=pl.ANY),
+        out_shape=jax.ShapeDtypeStruct(own.shape, own.dtype),
+        scratch_shapes=[pltpu.VMEM((rows, width), F32), pltpu.SemaphoreType.DMA],
+        input_output_aliases={0: 0},
+        compiler_params=pltpu.CompilerParams(vmem_limit_bytes=4 * 1024 * 1024),
+        cost_estimate=cost(rows * width, 12 * rows * width),
+    )(own, pltpu.with_memory_space_constraint(tail, pltpu.VMEM), pltpu.with_memory_space_constraint(recv, pltpu.VMEM))
+
+
 def solution(mesh):
     ep_n = mesh.shape['ep']
     fs_n = mesh.shape['fsdp']
@@ -208,8 +258,7 @@
         recv_gate = exchange(send)
         send = weight_grad_rhs(1 - z, x_rows, dh_up, fs_n)
         step = send.shape[0] // 16
-        cuts = (0, 12 * step, 15 * step, 15 * step + 2 * step // 3, 16 * step)
-        tiles = (4 * step, 3 * step, step // 3, step // 3)
+        cuts = (0, 12 * step, 15 * step + step // 3, 16 * step)
         recv_up = [exchange(send[lo:hi]) for lo, hi in zip(cuts, cuts[1:])]
 
         dx_rows = row_grads(z, dh_gate, dh_up, w_gate, other_w_gate, w_up, other_w_up)
@@ -225,8 +274,10 @@
         grad_w_up = weight_grad_rhs(z, x_rows, dh_up, fs_n)
         grad_w_down = add_rows(grad_w_down, recv_down, 0, 384)
         grad_w_gate = add_rows(grad_w_gate, recv_gate, 0, 4 * step)
-        for n, recv in enumerate(recv_up):
-            grad_w_up = add_rows(grad_w_up, recv, cuts[n], tiles[n])
+        tail = grad_w_up[cuts[2]:]
+        for n, recv in enumerate(recv_up[:-1]):
+            grad_w_up = add_piece(grad_w_up, recv, cuts[n])
+        grad_w_up = add_last(grad_w_up, tail, recv_up[-1])
         return grad_x, grad_gates, grad_w_gate[None], grad_w_down[None], grad_w_up[None]
 
     return jax.shard_map(local_backward, mesh=mesh, in_specs=(tok_spec, tok_spec, tok_spec, tok_spec, row_spec, row_spec, row_spec, row_spec, row_spec, row_spec, row_spec), out_specs=(tok_spec, tok_spec, row_spec, row_spec, row_spec), check_vma=False)

time: 522 us -> 521 us (level)
    pallas_call x6 -> x2, Pallas kernels: 23.5 us -> 12.5 us  [add_rows(): pl.pallas_call(kernel, grid=(rows // tile,), in_specs=[pl.BlockSpec((tile...]
    pallas_call x0 -> x3, Pallas kernels: none -> 8.52 us  [the longest x2 7.81 us: add_piece(): pl.pallas_call(kernel, in_specs=[pl.BlockSpec(memory_space=pl.ANY)] * 2,...]
    ppermute x9 -> x8, waiting for transfers between devices: 166 us -> 169 us  [exchange(): return lax.ppermute(value, 'fsdp', swap)]
    ppermute x9 -> x8, starting transfers between devices: 10.9 us -> 9.3 us  [exchange(): return lax.ppermute(value, 'fsdp', swap)]
  transfers between devices with their start and end apart: 13 -> 12, of which waited for: 5 -> 5; matrix products, arithmetic and copies ran while one was open for 11% -> 11% of each run, Pallas kernels for 37% -> 37%
where the time goes in v4:
time: 521 us; the launch traced here: 518 us
  waiting for transfers between devices  212 us (41%)
  Pallas kernels  198 us (38%)
  local copies, waits for them, and re-layouts  64.6 us (12%)
  starting transfers between devices  27.4 us (5%)
  other arithmetic  14.9 us (3%)
    ppermute x8, waiting for transfers between devices, exchange(): return lax.ppermute(value, 'fsdp', swap)  169 us
    pallas_call x4, Pallas kernels, weight_grad_rhs(): pl.pallas_call(kernel, grid_spec=pltpu.PrefetchScalarGridSpec(num_scalar_...  50.1 us
    pallas_call x1, Pallas kernels, row_grads(): pl.pallas_call(kernel, grid_spec=pltpu.PrefetchScalarGridSpec(num_scalar_...  43.2 us
    all_to_all x1, waiting for transfers between devices, local_backward(): lax.all_to_all(send_dy, 'ep', 1, 1, tiled=True).reshape(rows_loc, width)  42.5 us
    pallas_call x1, Pallas kernels, hidden_grads(): pl.pallas_call(kernel, grid_spec=pltpu.PrefetchScalarGridSpec(num_scalar_...  42.1 us
    pallas_call x2, Pallas kernels, down_grad(): pl.pallas_call(kernel, grid_spec=pltpu.PrefetchScalarGridSpec(num_scalar_...  41.7 us
    gather x1, local copies, waits for them, and re-layouts, local_backward(): jnp.take(gates.reshape(-1), src_choice, mode='fill', fill_value=0)  13.6 us
    gather x1, local copies, waits for them, and re-layouts, local_backward(): jnp.take(back_dx, send_row, axis=0, mode='fill', fill_value=0)  12.7 us
  transfers between devices with their start and end apart: 12, of which 5 were waited for; matrix products, arithmetic and copies ran while one was open for 11% of the time, Pallas kernels for 37%

profile of v4, /device:TPU:0, one launch (start us, length us, event | category | flops | bytes accessed | tf_op | source)
XLA Modules:
  0.0 517.8 jit_solution(3382675450368567315)
XLA Ops:
  0.6 0.0 copy-start
  0.6 0.0 copy-start.2
  0.7 0.9 fusion.4
  1.6 8.1 %scatter_custom_fusion = s32[2560]{0:T(1024)S(1)} fusion(s32[2048]{0:T(1024)S(1)} %bitcast.41, s32[2048]{0:T(1024)S(1)} %iota.3, s32[]{:T(128)} %constant.98.clone.1), kind=kCustom, calls=%fused_computation.18 | custom fusion | bytes 10244 | tf_op jit(solution)/shard_map/scatter | solution.py:247
  9.7 0.0 copy-done.2
  9.7 13.6 %gather_fusion.1 = f32[2560]{0:T(1024)S(1)} fusion(f32[2048]{0:T(1024)S(1)} %bitcast.25, s32[3072]{0:T(1024)S(1)} %pad_clamp_fusion), kind=kCustom, calls=%fused_computation.1 | custom fusion | bytes 30720 | tf_op jit(solution)/shard_map/jit(_take)/gather | solution.py:249
  23.3 0.7 select_n.72
  24.0 5.4 %all-to-all-start.1 = ((f32[1,8,320]{2,0,1:T(1,128)}), f32[1,8,320]{2,0,1:T(1,128)S(1)}, u32[]{:S(2)}, u32[]{:S(2)}) async-start(f32[1,8,320]{2,0,1:T(1,128)} %select_n.72), calls=%async_computation.1 | async-start | bytes 24576 | tf_op jit(solution)/shard_map/all_to_all | solution.py:251
  29.4 0.0 copy-done
  29.5 8.5 %gather_fusion = bf16[2560,768]{1,0:T(8,128)(2,1)} fusion(bf16[2048,768]{1,0:T(8,128)(2,1)S(1)} %copy-done, s32[3072]{0:T(1024)S(1)} %pad_clamp_fusion), kind=kCustom, calls=%fused_computation | custom fusion | bytes 7874560 | tf_op jit(solution)/shard_map/jit(_take)/gather | solution.py:248
  38.0 0.1 broadcast_in_dim.59
  38.0 3.7 broadcast_select_fusion
  41.8 0.0 all-to-all-done.1
  41.8 4.7 all-to-all-start
  46.5 0.0 copy-done.4
  46.5 1.6 collective-permute-start
  48.1 0.4 collective-permute-start.1
  48.5 1.6 collective-permute-start.2
  50.2 0.1 mul.21
  50.2 42.5 %all-to-all-done = bf16[1,8,320,768]{3,2,0,1:T(8,128)(2,1)} async-done(((bf16[1,8,320,768]{3,2,0,1:T(8,128)(2,1)}), bf16[1,8,320,768]{3,2,0,1:T(8,128)(2,1)}, u32[]{:S(2)}, u32[]{:S(2)}) %all-to-all-start) | async-done | bytes 3932192 | tf_op jit(solution)/shard_map/all_to_all | solution.py:250
  92.8 6.2 %fusion.1 = (f32[2560]{0:T(1024)S(1)}, bf16[2560,768]{1,0:T(8,128)(2,1)}) fusion(bf16[1,2560,768]{2,1,0:T(8,128)(2,1)} %param.18, bf16[1,8,320,768]{3,2,0,1:T(8,128)(2,1)} %all-to-all-done, f32[2560]{0:T(1024)S(1)} %mul.21), kind=kLoop, calls=%fused_computation.8 | loop fusion | flops 11793920 | bytes 11816960 | tf_op jit(solution)/shard_map/rd,rd->r/dot_general | solution.py:265
  99.0 0.7 reshape.103
  99.6 3.3 all-to-all-start.3
  103.0 0.0 collective-permute-done.other_ref
  103.0 42.1 %shard_map.146 = (bf16[2560,3072]{1,0:T(8,128)(2,1)}, bf16[2560,3072]{1,0:T(8,128)(2,1)}) custom-call(s32[1]{0:T(128)} %bitcast.z_ref.s_ref, bf16[2560,768]{1,0:T(8,128)(2,1)} %get-tuple-element.14.g_ref, bf16[1536,768]{1,0:T(8,128)(2,1)} %bitcast.44, bf16[1536,768]{1,0:T(8,128)(2,1)} %collective-permute-done.other_ref, bf16[2560,3072]{1,0:T(8,128)(2,1)} %bitcast.27, ...), custom_call_target="tpu_custom_call" | custom-call | flops 12079595520 | bytes 62914560 | tf_op jit(solution)/shard_map/pallas_call | solution.py:44
  145.1 12.5 %shard_map.149 = f32[384,3072]{1,0:T(8,128)} custom-call(s32[1]{0:T(128)S(6)} %sub.10.s_ref, bf16[2560,768]{1,0:T(8,128)(2,1)} %bitcast.33, bf16[2560,3072]{1,0:T(8,128)(2,1)} %get-tuple-element.7.d1_ref.r_ref), custom_call_target="tpu_custom_call" | custom-call | flops 6039797760 | bytes 20447232 | tf_op jit(solution)/shard_map/pallas_call | solution.py:105
  157.7 1.7 collective-permute-start.3
  159.4 20.9 %shard_map.152 = f32[1536,768]{1,0:T(8,128)} custom-call(s32[1]{0:T(128)S(6)} %sub.10.s_ref, bf16[2560,3072]{1,0:T(8,128)(2,1)} %bitcast.28, bf16[2560,3072]{1,0:T(8,128)(2,1)} %bitcast.31, bf16[2560,768]{1,0:T(8,128)(2,1)} %get-tuple-element.14.g_ref), custom_call_target="tpu_custom_call" | custom-call | flops 6039797760 | bytes 31457280 | tf_op jit(solution)/shard_map/pallas_call | solution.py:84
  180.2 0.3 collective-permute-start.4
  180.6 0.0 collective-permute-done.1.g1_ref
  180.6 21.3 %collective-permute-done.2.u1_ref = bf16[384,3072]{1,0:T(8,128)(2,1)} collective-permute-done((bf16[384,3072]{1,0:T(8,128)(2,1)}, bf16[384,3072]{1,0:T(8,128)(2,1)}, u32[]{:S(2)}, u32[]{:S(2)}) %collective-permute-start.2) | collective-permute-done | bytes 2359328 | tf_op jit(solution)/shard_map/ppermute | solution.py:231
  201.9 43.2 %shard_map.147 = bf16[2560,768]{1,0:T(8,128)(2,1)} custom-call(s32[1]{0:T(128)} %bitcast.z_ref.s_ref, bf16[2560,3072]{1,0:T(8,128)(2,1)} %get-tuple-element.7.d1_ref.r_ref, bf16[2560,3072]{1,0:T(8,128)(2,1)} %get-tuple-element.8.d3_ref.r_ref, bf16[384,3072]{1,0:T(8,128)(2,1)} %bitcast.47, bf16[384,3072]{1,0:T(8,128)(2,1)} %collective-permute-done.1.g1_ref, ...), custom_call_target="tpu_custom_call" | custom-call | flops 24159191040 | bytes 62914560 | tf_op jit(solution)/shard_map/pallas_call | solution.py:140
  245.0 0.0 all-to-all-done.3
  245.0 4.7 all-to-all-start.2
  249.8 12.5 %shard_map.155 = f32[384,3072]{1,0:T(8,128)} custom-call(s32[1]{0:T(128)S(6)} %sub.10.s_ref, bf16[2560,768]{1,0:T(8,128)(2,1)} %bitcast.34, bf16[2560,3072]{1,0:T(8,128)(2,1)} %get-tuple-element.8.d3_ref.r_ref), custom_call_target="tpu_custom_call" | custom-call | flops 6039797760 | bytes 20447232 | tf_op jit(solution)/shard_map/pallas_call | solution.py:105
  262.3 4.2 slice.24
  266.5 1.6 collective-permute-start.5
  268.1 1.3 slice.25
  269.3 0.9 slice.27
  270.3 12.5 %shard_map.154.own_ref = f32[384,3072]{1,0:T(8,128)} custom-call(s32[1]{0:T(128)} %bitcast.z_ref.s_ref, bf16[2560,768]{1,0:T(8,128)(2,1)} %bitcast.35, bf16[2560,3072]{1,0:T(8,128)(2,1)} %get-tuple-element.8.d3_ref.r_ref), custom_call_target="tpu_custom_call" | custom-call | flops 6039797760 | bytes 20447232 | tf_op jit(solution)/shard_map/pallas_call | solution.py:105
  282.8 0.9 slice.26.tail_ref
  283.8 0.5 collective-permute-start.6
  284.2 1.6 collective-permute-start.7
  285.8 12.5 %shard_map.148.own_ref = f32[384,3072]{1,0:T(8,128)} custom-call(s32[1]{0:T(128)} %bitcast.z_ref.s_ref, bf16[2560,768]{1,0:T(8,128)(2,1)} %bitcast.36, bf16[2560,3072]{1,0:T(8,128)(2,1)} %get-tuple-element.7.d1_ref.r_ref), custom_call_target="tpu_custom_call" | custom-call | flops 6039797760 | bytes 20447232 | tf_op jit(solution)/shard_map/pallas_call | solution.py:105
  298.3 20.9 %shard_map.151.own_ref = f32[1536,768]{1,0:T(8,128)} custom-call(s32[1]{0:T(128)} %bitcast.z_ref.s_ref, bf16[2560,3072]{1,0:T(8,128)(2,1)} %bitcast.29, bf16[2560,3072]{1,0:T(8,128)(2,1)} %bitcast.32, bf16[2560,768]{1,0:T(8,128)(2,1)} %get-tuple-element.14.g_ref), custom_call_target="tpu_custom_call" | custom-call | flops 6039797760 | bytes 31457280 | tf_op jit(solution)/shard_map/pallas_call | solution.py:84
  319.2 0.1 reshape.104
  319.3 11.8 %gather_fusion.3 = f32[2048]{0:T(1024)S(1)} fusion(f32[2560]{0:T(1024)S(1)} %reshape.104, s32[2048]{0:T(1024)S(1)} %broadcast_clamp_fusion), kind=kCustom, calls=%fused_computation.3 | custom fusion | bytes 24576 | tf_op jit(solution)/shard_map/jit(_take)/gather | solution.py:270
  331.1 0.6 broadcast_select_fusion.3
  331.7 0.0 all-to-all-done.2
  331.7 12.7 %gather_fusion.2 = bf16[2048,768]{1,0:T(8,128)(2,1)} fusion(bf16[2560,768]{1,0:T(8,128)(2,1)} %bitcast.13, s32[2048]{0:T(1024)S(1)} %broadcast_clamp_fusion), kind=kCustom, calls=%fused_computation.2 | custom fusion | bytes 6299648 | tf_op jit(solution)/shard_map/jit(_take)/gather | solution.py:268
  344.4 3.3 broadcast_select_fusion.1
  347.7 132.3 %collective-permute-done.5.recv_ref = f32[288,3072]{1,0:T(8,128)} collective-permute-done((f32[288,3072]{1,0:T(8,128)}, f32[288,3072]{1,0:T(8,128)}, u32[]{:S(2)}, u32[]{:S(2)}) %collective-permute-start.5) | collective-permute-done | bytes 3538976 | tf_op jit(solution)/shard_map/ppermute | solution.py:231
  479.9 5.3 %shard_map.156.own_ref = f32[384,3072]{1,0:T(8,128)} custom-call(f32[384,3072]{1,0:T(8,128)} %shard_map.154.own_ref, f32[288,3072]{1,0:T(8,128)} %collective-permute-done.5.recv_ref), custom_call_target="tpu_custom_call", output_to_operand_aliasing={{}: (0, {})} | custom-call | flops 884736 | bytes 10616832 | tf_op jit(solution)/shard_map/pallas_call | solution.py:188
  485.2 15.7 %collective-permute-done.6.recv_ref = f32[80,3072]{1,0:T(8,128)S(1)} collective-permute-done((f32[80,3072]{1,0:T(8,128)S(1)}, f32[80,3072]{1,0:T(8,128)S(1)}, u32[]{:S(2)}, u32[]{:S(2)}) %collective-permute-start.6) | collective-permute-done | bytes 983072 | tf_op jit(solution)/shard_map/ppermute | solution.py:231
  500.9 0.9 copy-done.3
  501.8 2.6 shard_map.157.own_ref
  504.4 0.2 collective-permute-done.7.recv_ref
  504.6 0.7 shard_map.158
  505.3 0.0 collective-permute-done.3.recv_ref
  505.3 0.0 copy-start.1
  505.3 6.3 %shard_map.150 = f32[384,3072]{1,0:T(8,128)} custom-call(f32[384,3072]{1,0:T(8,128)} %shard_map.148.own_ref, f32[384,3072]{1,0:T(8,128)} %collective-permute-done.3.recv_ref), custom_call_target="tpu_custom_call", output_to_operand_aliasing={{}: (0, {})} | custom-call | flops 1179648 | bytes 14155776 | tf_op jit(solution)/shard_map/pallas_call | solution.py:161
  511.6 0.0 collective-permute-done.4.recv_ref
  511.6 6.2 %shard_map.153 = f32[1536,768]{1,0:T(8,128)} custom-call(f32[1536,768]{1,0:T(8,128)} %shard_map.151.own_ref, f32[1536,768]{1,0:T(8,128)} %collective-permute-done.4.recv_ref), custom_call_target="tpu_custom_call", output_to_operand_aliasing={{}: (0, {})} | custom-call | flops 1179648 | bytes 14155776 | tf_op jit(solution)/shard_map/pallas_call | solution.py:161
  517.8 0.0 copy-done.1
  (9 shorter events, 0.1 us)
Async XLA Ops:
  0.6 28.8 %copy-start = (bf16[2048,768]{1,0:T(8,128)(2,1)S(1)}, bf16[2048,768]{1,0:T(8,128)(2,1)}, u32[]{:S(2)}) copy-start(bf16[2048,768]{1,0:T(8,128)(2,1)} %param.11) | copy-start | bytes 9437188
  0.6 9.0 %copy-start.2 = (f32[2048,1]{0,1:T(1,128)S(1)}, f32[2048,1]{0,1:T(1,128)}, u32[]{:S(2)}) copy-start(f32[2048,1]{0,1:T(1,128)} %param.14) | copy-start | bytes 24580
  24.0 17.8 %all-to-all-start.1 = ((f32[1,8,320]{2,0,1:T(1,128)}), f32[1,8,320]{2,0,1:T(1,128)S(1)}, u32[]{:S(2)}, u32[]{:S(2)}) async-start(f32[1,8,320]{2,0,1:T(1,128)} %select_n.72), calls=%async_computation.1 | async-start | bytes 24576 | tf_op jit(solution)/shard_map/all_to_all | solution.py:251
  41.8 4.7 copy-start.4
  41.8 51.0 %all-to-all-start = ((bf16[1,8,320,768]{3,2,0,1:T(8,128)(2,1)}), bf16[1,8,320,768]{3,2,0,1:T(8,128)(2,1)}, u32[]{:S(2)}, u32[]{:S(2)}) async-start(bf16[1,8,320,768]{3,2,0,1:T(8,128)(2,1)} %broadcast_select_fusion), calls=%async_computation | async-start | bytes 7864320 | tf_op jit(solution)/shard_map/all_to_all | solution.py:250
  46.5 56.5 %collective-permute-start = (bf16[1536,768]{1,0:T(8,128)(2,1)S(1)}, bf16[1536,768]{1,0:T(8,128)(2,1)}, u32[]{:S(2)}, u32[]{:S(2)}) collective-permute-start(bf16[1536,768]{1,0:T(8,128)(2,1)S(1)} %bitcast.45), channel_id=1, source_target_pairs={{0,8},{8,0},{1,9},{9,1},{2,10},{10,2},{3,11},{11,3},{4,12},{12,4},... | collective-permute-start | bytes 7077896 | tf_op jit(solution)/shard_map/ppermute | solution.py:231
  48.1 132.5 %collective-permute-start.1 = (bf16[384,3072]{1,0:T(8,128)(2,1)}, bf16[384,3072]{1,0:T(8,128)(2,1)}, u32[]{:S(2)}, u32[]{:S(2)}) collective-permute-start(bf16[384,3072]{1,0:T(8,128)(2,1)} %bitcast.46), channel_id=1, source_target_pairs={{0,8},{8,0},{1,9},{9,1},{2,10},{10,2},{3,11},{11,3},{4,12},{12,4},... | collective-permute-start | bytes 7077896 | tf_op jit(solution)/shard_map/ppermute | solution.py:231
  48.5 153.3 %collective-permute-start.2 = (bf16[384,3072]{1,0:T(8,128)(2,1)}, bf16[384,3072]{1,0:T(8,128)(2,1)}, u32[]{:S(2)}, u32[]{:S(2)}) collective-permute-start(bf16[384,3072]{1,0:T(8,128)(2,1)} %bitcast.48), channel_id=1, source_target_pairs={{0,8},{8,0},{1,9},{9,1},{2,10},{10,2},{3,11},{11,3},{4,12},{12,4},... | collective-permute-start | bytes 7077896 | tf_op jit(solution)/shard_map/ppermute | solution.py:231
  99.6 145.4 %all-to-all-start.3 = ((f32[1,8,320]{2,0,1:T(1,128)}), f32[1,8,320]{2,0,1:T(1,128)S(1)}, u32[]{:S(2)}, u32[]{:S(2)}) async-start(f32[1,8,320]{2,0,1:T(1,128)} %reshape.103), calls=%async_computation.3 | async-start | bytes 24576 | tf_op jit(solution)/shard_map/all_to_all | solution.py:267
  157.7 347.6 %collective-permute-start.3 = (f32[384,3072]{1,0:T(8,128)}, f32[384,3072]{1,0:T(8,128)}, u32[]{:S(2)}, u32[]{:S(2)}) collective-permute-start(f32[384,3072]{1,0:T(8,128)} %shard_map.149), channel_id=1, source_target_pairs={{0,8},{8,0},{1,9},{9,1},{2,10},{10,2},{3,11},{11,3},{4,12},{12,4},... | collective-permute-start | bytes 14155784 | tf_op jit(solution)/shard_map/ppermute | solution.py:231
  180.2 331.4 %collective-permute-start.4 = (f32[1536,768]{1,0:T(8,128)}, f32[1536,768]{1,0:T(8,128)}, u32[]{:S(2)}, u32[]{:S(2)}) collective-permute-start(f32[1536,768]{1,0:T(8,128)} %shard_map.152), channel_id=1, source_target_pairs={{0,8},{8,0},{1,9},{9,1},{2,10},{10,2},{3,11},{11,3},{4,12},{12,4},... | collective-permute-start | bytes 14155784 | tf_op jit(solution)/shard_map/ppermute | solution.py:231
  245.0 86.7 %all-to-all-start.2 = ((bf16[1,8,320,768]{3,2,0,1:T(8,128)(2,1)}), bf16[1,8,320,768]{3,2,0,1:T(8,128)(2,1)}, u32[]{:S(2)}, u32[]{:S(2)}) async-start(bf16[1,8,320,768]{3,2,0,1:T(8,128)(2,1)} %bitcast.40), calls=%async_computation.2 | async-start | bytes 7864320 | tf_op jit(solution)/shard_map/all_to_all | solution.py:266
  266.5 213.4 %collective-permute-start.5 = (f32[288,3072]{1,0:T(8,128)}, f32[288,3072]{1,0:T(8,128)}, u32[]{:S(2)}, u32[]{:S(2)}) collective-permute-start(f32[288,3072]{1,0:T(8,128)} %slice.24), channel_id=1, source_target_pairs={{0,8},{8,0},{1,9},{9,1},{2,10},{10,2},{3,11},{11,3},{4,12},{12,4},... | collective-permute-start | bytes 10616840 | tf_op jit(solution)/shard_map/ppermute | solution.py:231
  283.8 217.1 %collective-permute-start.6 = (f32[80,3072]{1,0:T(8,128)S(1)}, f32[80,3072]{1,0:T(8,128)S(1)}, u32[]{:S(2)}, u32[]{:S(2)}) collective-permute-start(f32[80,3072]{1,0:T(8,128)S(1)} %slice.25), channel_id=1, source_target_pairs={{0,8},{8,0},{1,9},{9,1},{2,10},{10,2},{3,11},{11,3},{4,12},{12,4},... | collective-permute-start | bytes 2949128 | tf_op jit(solution)/shard_map/ppermute | solution.py:231
  284.2 220.3 %collective-permute-start.7 = (f32[16,3072]{1,0:T(8,128)S(1)}, f32[16,3072]{1,0:T(8,128)S(1)}, u32[]{:S(2)}, u32[]{:S(2)}) collective-permute-start(f32[16,3072]{1,0:T(8,128)S(1)} %slice.27), channel_id=1, source_target_pairs={{0,8},{8,0},{1,9},{9,1},{2,10},{10,2},{3,11},{11,3},{4,12},{12,4},... | collective-permute-start | bytes 589832 | tf_op jit(solution)/shard_map/ppermute | solution.py:231
  500.9 0.9 copy-start.3
  505.3 12.5 %copy-start.1 = (bf16[2048,768]{1,0:T(8,128)(2,1)S(1)}, bf16[2048,768]{1,0:T(8,128)(2,1)}, u32[]{:S(2)}) copy-start(bf16[2048,768]{1,0:T(8,128)(2,1)} %param.11) | copy-start | bytes 9437188

commit v5 on v4

--- a/solution.py
+++ b/solution.py
@@ -230,6 +230,22 @@
     def exchange(value):
         return lax.ppermute(value, 'fsdp', swap)
 
+    near = 2
+    far = range(1, ep_n // near)
+
+    def send(value, moves):
+        return lax.ppermute(value, ('fsdp', 'ep'), [(a * ep_n + b, c * ep_n + d) for (a, b), (c, d) in moves])
+
+    def detour(value):
+        cols = value.shape[1] // len(far)
+        grid = [(f, c) for f in range(fs_n) for c in range(near)]
+        rest = [((f, e), (fs_n - 1 - f, e)) for f in range(fs_n) for e in range(near, ep_n)]
+        out = [send(value[:, (k - 1) * cols:k * cols], [((f, c), (f, near * k + c)) for f, c in grid]) for k in far]
+        crossed = send(sum(out[1:], out[0]), rest)
+        direct = send(value, rest)
+        back = [send(crossed, [((f, near * k + c), (f, c)) for f, c in grid]) for k in far]
+        return direct, jnp.concatenate(back, axis=1)
+
     def local_backward(grad_out, expert_idx, slot_pos, gates, x_disp, h_gate, h_up, y_disp, w_gate, w_down, w_up):
         tok_n, top_n = expert_idx.shape
         e_loc, rows_loc, width = x_disp.shape
@@ -251,15 +267,17 @@
         gate_rows = lax.all_to_all(send_gate, 'ep', 1, 1, tiled=True).reshape(rows_loc)
         g_rows = (dy_rows.astype(F32) * gate_rows[:, None]).astype(BF16)
 
-        send = down_grad(1 - z, h_gate, h_up, g_rows, fs_n)
-        recv_down = exchange(send)
+        part = down_grad(1 - z, h_gate, h_up, g_rows, fs_n)
+        recv_down = exchange(part)
         dh_gate, dh_up = hidden_grads(z, g_rows, w_down, other_w_down, h_gate, h_up)
-        send = weight_grad_rhs(1 - z, x_rows, dh_gate, fs_n)
-        recv_gate = exchange(send)
-        send = weight_grad_rhs(1 - z, x_rows, dh_up, fs_n)
-        step = send.shape[0] // 16
-        cuts = (0, 12 * step, 15 * step + step // 3, 16 * step)
-        recv_up = [exchange(send[lo:hi]) for lo, hi in zip(cuts, cuts[1:])]
+        part = weight_grad_rhs(1 - z, x_rows, dh_gate, fs_n)
+        recv_gate = exchange(part)
+        send_up = weight_grad_rhs(1 - z, x_rows, dh_up, fs_n)
+        step = send_up.shape[0] // 16
+        cuts = (0, 12 * step, 15 * step, 15 * step + step // 3, 16 * step)
+        piece = [send_up[lo:hi] for lo, hi in zip(cuts, cuts[1:])]
+        direct, around = detour(piece[2])
+        recv_up = [exchange(piece[0]), exchange(piece[1]), exchange(piece[3])]
 
         dx_rows = row_grads(z, dh_gate, dh_up, w_gate, other_w_gate, w_up, other_w_up)
         dgate_rows = jnp.einsum('rd,rd->r', dy_rows, y_rows, preferred_element_type=F32)
@@ -274,9 +292,10 @@
         grad_w_up = weight_grad_rhs(z, x_rows, dh_up, fs_n)
         grad_w_down = add_rows(grad_w_down, recv_down, 0, 384)
         grad_w_gate = add_rows(grad_w_gate, recv_gate, 0, 4 * step)
-        tail = grad_w_up[cuts[2]:]
-        for n, recv in enumerate(recv_up[:-1]):
-            grad_w_up = add_piece(grad_w_up, recv, cuts[n])
+        tail = grad_w_up[cuts[3]:]
+        grad_w_up = add_piece(grad_w_up, recv_up[0], cuts[0])
+        grad_w_up = add_piece(grad_w_up, direct + around, cuts[2])
+        grad_w_up = add_piece(grad_w_up, recv_up[1], cuts[1])
         grad_w_up = add_last(grad_w_up, tail, recv_up[-1])
         return grad_x, grad_gates, grad_w_gate[None], grad_w_down[None], grad_w_up[None]
 

time: 521 us -> 559 us (1.073)
  waiting for transfers between devices: 212 us -> 234 us
  starting transfers between devices: 27.4 us -> 40.1 us
    ppermute x0 -> x8, waiting for transfers between devices: none -> 188 us  [send(): lax.ppermute(value, ('fsdp', 'ep'), [(a * ep_n + b, c * ep_n + d) for (a,...]
    ppermute x8, waiting for transfers between devices: 169 us -> 3.02 us  [exchange(): return lax.ppermute(value, 'fsdp', swap)]
    ppermute x0 -> x8, starting transfers between devices: none -> 12.7 us  [send(): lax.ppermute(value, ('fsdp', 'ep'), [(a * ep_n + b, c * ep_n + d) for (a,...]
  transfers between devices with their start and end apart: 12 -> 20, of which waited for: 5 -> 5; matrix products, arithmetic and copies ran while one was open for 11% -> 10% of each run, Pallas kernels for 37% -> 35%
where the time goes in v5:
time: 559 us; the launch traced here: 556 us
  waiting for transfers between devices  234 us (42%)
  Pallas kernels  200 us (36%)
  local copies, waits for them, and re-layouts  66.1 us (12%)
  starting transfers between devices  40.1 us (7%)
  other arithmetic  15.5 us (3%)
    ppermute x8, waiting for transfers between devices, send(): lax.ppermute(value, ('fsdp', 'ep'), [(a * ep_n + b, c * ep_n + d) for (a,...  188 us
    pallas_call x4, Pallas kernels, weight_grad_rhs(): pl.pallas_call(kernel, grid_spec=pltpu.PrefetchScalarGridSpec(num_scalar_...  50.1 us
    pallas_call x1, Pallas kernels, row_grads(): pl.pallas_call(kernel, grid_spec=pltpu.PrefetchScalarGridSpec(num_scalar_...  43.4 us
    all_to_all x1, waiting for transfers between devices, local_backward(): lax.all_to_all(send_dy, 'ep', 1, 1, tiled=True).reshape(rows_loc, width)  42.5 us
    pallas_call x1, Pallas kernels, hidden_grads(): pl.pallas_call(kernel, grid_spec=pltpu.PrefetchScalarGridSpec(num_scalar_...  42.2 us
    pallas_call x2, Pallas kernels, down_grad(): pl.pallas_call(kernel, grid_spec=pltpu.PrefetchScalarGridSpec(num_scalar_...  41.8 us
    gather x1, local copies, waits for them, and re-layouts, local_backward(): jnp.take(gates.reshape(-1), src_choice, mode='fill', fill_value=0)  13.6 us
    gather x1, local copies, waits for them, and re-layouts, local_backward(): jnp.take(back_dx, send_row, axis=0, mode='fill', fill_value=0)  12.7 us
  transfers between devices with their start and end apart: 20, of which 5 were waited for; matrix products, arithmetic and copies ran while one was open for 10% of the time, Pallas kernels for 35%

profile of v5, /device:TPU:0, one launch (start us, length us, event | category | flops | bytes accessed | tf_op | source)
XLA Modules:
  0.0 556.3 jit_solution(378767865080893942)
XLA Ops:
  0.6 0.0 copy-start
  0.7 0.9 fusion.4
  1.6 8.1 %scatter_custom_fusion = s32[2560]{0:T(1024)S(1)} fusion(s32[2048]{0:T(1024)S(1)} %bitcast.41, s32[2048]{0:T(1024)S(1)} %iota.3, s32[]{:T(128)} %constant.98.clone.1), kind=kCustom, calls=%fused_computation.20 | custom fusion | bytes 10244 | tf_op jit(solution)/shard_map/scatter | solution.py:263
  9.7 13.6 %gather_fusion.1 = f32[2560]{0:T(1024)S(1)} fusion(f32[2048]{0:T(1024)S(1)} %bitcast.25, s32[3072]{0:T(1024)S(1)} %pad_clamp_fusion), kind=kCustom, calls=%fused_computation.1 | custom fusion | bytes 30720 | tf_op jit(solution)/shard_map/jit(_take)/gather | solution.py:265
  23.3 0.7 select_n.72
  24.0 5.4 all-to-all-start.1
  29.5 8.5 %gather_fusion = bf16[2560,768]{1,0:T(8,128)(2,1)} fusion(bf16[2048,768]{1,0:T(8,128)(2,1)S(1)} %copy-done, s32[3072]{0:T(1024)S(1)} %pad_clamp_fusion), kind=kCustom, calls=%fused_computation | custom fusion | bytes 7874560 | tf_op jit(solution)/shard_map/jit(_take)/gather | solution.py:264
  38.0 0.1 broadcast_in_dim.59
  38.0 3.7 broadcast_select_fusion
  41.8 4.7 all-to-all-start
  46.5 1.6 collective-permute-start
  48.1 0.4 collective-permute-start.1
  48.5 1.6 collective-permute-start.2
  50.2 0.1 mul.21
  50.2 42.5 %all-to-all-done = bf16[1,8,320,768]{3,2,0,1:T(8,128)(2,1)} async-done(((bf16[1,8,320,768]{3,2,0,1:T(8,128)(2,1)}), bf16[1,8,320,768]{3,2,0,1:T(8,128)(2,1)}, u32[]{:S(2)}, u32[]{:S(2)}) %all-to-all-start) | async-done | bytes 3932192 | tf_op jit(solution)/shard_map/all_to_all | solution.py:266
  92.8 6.2 %fusion.1 = (f32[2560]{0:T(1024)S(1)}, bf16[2560,768]{1,0:T(8,128)(2,1)}) fusion(bf16[1,2560,768]{2,1,0:T(8,128)(2,1)} %param.18, bf16[1,8,320,768]{3,2,0,1:T(8,128)(2,1)} %all-to-all-done, f32[2560]{0:T(1024)S(1)} %mul.21), kind=kLoop, calls=%fused_computation.8 | loop fusion | flops 11793920 | bytes 11816960 | tf_op jit(solution)/shard_map/rd,rd->r/dot_general | solution.py:283
  98.9 0.7 reshape.103
  99.6 3.3 all-to-all-start.3
  102.9 42.2 %shard_map.146 = (bf16[2560,3072]{1,0:T(8,128)(2,1)}, bf16[2560,3072]{1,0:T(8,128)(2,1)}) custom-call(s32[1]{0:T(128)} %bitcast.z_ref.s_ref, bf16[2560,768]{1,0:T(8,128)(2,1)} %get-tuple-element.17.g_ref, bf16[1536,768]{1,0:T(8,128)(2,1)} %bitcast.44, bf16[1536,768]{1,0:T(8,128)(2,1)} %collective-permute-done.other_ref, bf16[2560,3072]{1,0:T(8,128)(2,1)} %bitcast.27, ...), custom_call_target="tpu_custom_call" | custom-call | flops 12079595520 | bytes 62914560 | tf_op jit(solution)/shard_map/pallas_call | solution.py:44
  145.1 12.6 %shard_map.149 = f32[384,3072]{1,0:T(8,128)} custom-call(s32[1]{0:T(128)S(6)} %sub.10.s_ref, bf16[2560,768]{1,0:T(8,128)(2,1)} %bitcast.33, bf16[2560,3072]{1,0:T(8,128)(2,1)} %get-tuple-element.7.d1_ref.r_ref), custom_call_target="tpu_custom_call" | custom-call | flops 6039797760 | bytes 20447232 | tf_op jit(solution)/shard_map/pallas_call | solution.py:105
  157.7 1.5 collective-permute-start.3
  159.2 20.9 %shard_map.152 = f32[1536,768]{1,0:T(8,128)} custom-call(s32[1]{0:T(128)S(6)} %sub.10.s_ref, bf16[2560,3072]{1,0:T(8,128)(2,1)} %bitcast.28, bf16[2560,3072]{1,0:T(8,128)(2,1)} %bitcast.31, bf16[2560,768]{1,0:T(8,128)(2,1)} %get-tuple-element.17.g_ref), custom_call_target="tpu_custom_call" | custom-call | flops 6039797760 | bytes 31457280 | tf_op jit(solution)/shard_map/pallas_call | solution.py:84
  180.1 0.5 collective-permute-start.4
  180.6 12.5 %shard_map.155 = f32[384,3072]{1,0:T(8,128)} custom-call(s32[1]{0:T(128)S(6)} %sub.10.s_ref, bf16[2560,768]{1,0:T(8,128)(2,1)} %bitcast.34, bf16[2560,3072]{1,0:T(8,128)(2,1)} %get-tuple-element.8.d3_ref.r_ref), custom_call_target="tpu_custom_call" | custom-call | flops 6039797760 | bytes 20447232 | tf_op jit(solution)/shard_map/pallas_call | solution.py:105
  193.2 4.1 slice.43
  197.3 1.5 collective-permute-start.5
  198.9 3.0 collective-permute-done.2.u1_ref
  201.9 43.4 %shard_map.147 = bf16[2560,768]{1,0:T(8,128)(2,1)} custom-call(s32[1]{0:T(128)} %bitcast.z_ref.s_ref, bf16[2560,3072]{1,0:T(8,128)(2,1)} %get-tuple-element.7.d1_ref.r_ref, bf16[2560,3072]{1,0:T(8,128)(2,1)} %get-tuple-element.8.d3_ref.r_ref, bf16[384,3072]{1,0:T(8,128)(2,1)} %bitcast.47, bf16[384,3072]{1,0:T(8,128)(2,1)} %collective-permute-done.1.g1_ref, ...), custom_call_target="tpu_custom_call" | custom-call | flops 24159191040 | bytes 62914560 | tf_op jit(solution)/shard_map/pallas_call | solution.py:140
  245.2 4.5 all-to-all-start.2
  249.7 0.8 fusion.5
  250.5 4.7 collective-permute-start.9
  255.3 1.3 collective-permute-start.7
  256.6 37.3 %collective-permute-done.9 = f32[8,1024]{1,0:T(8,128)S(1)} collective-permute-done((f32[8,1024]{1,0:T(8,128)S(1)}, f32[8,1024]{1,0:T(8,128)S(1)}, u32[]{:S(2)}, u32[]{:S(2)}) %collective-permute-start.9) | collective-permute-done | bytes 32800 | tf_op jit(solution)/shard_map/ppermute | solution.py:237
  293.9 1.5 collective-permute-start.8
  295.3 12.5 %shard_map.148.own_ref = f32[384,3072]{1,0:T(8,128)} custom-call(s32[1]{0:T(128)} %bitcast.z_ref.s_ref, bf16[2560,768]{1,0:T(8,128)(2,1)} %bitcast.35, bf16[2560,3072]{1,0:T(8,128)(2,1)} %get-tuple-element.7.d1_ref.r_ref), custom_call_target="tpu_custom_call" | custom-call | flops 6039797760 | bytes 20447232 | tf_op jit(solution)/shard_map/pallas_call | solution.py:105
  307.9 0.7 collective-permute-start.10
  308.6 20.9 %shard_map.151.own_ref = f32[1536,768]{1,0:T(8,128)} custom-call(s32[1]{0:T(128)} %bitcast.z_ref.s_ref, bf16[2560,3072]{1,0:T(8,128)(2,1)} %bitcast.29, bf16[2560,3072]{1,0:T(8,128)(2,1)} %bitcast.32, bf16[2560,768]{1,0:T(8,128)(2,1)} %get-tuple-element.17.g_ref), custom_call_target="tpu_custom_call" | custom-call | flops 6039797760 | bytes 31457280 | tf_op jit(solution)/shard_map/pallas_call | solution.py:84
  329.5 0.9 slice.44
  330.4 0.7 collective-permute-start.6
  331.0 1.3 collective-permute-start.13
  332.3 12.5 %shard_map.154.own_ref = f32[384,3072]{1,0:T(8,128)} custom-call(s32[1]{0:T(128)} %bitcast.z_ref.s_ref, bf16[2560,768]{1,0:T(8,128)(2,1)} %bitcast.36, bf16[2560,3072]{1,0:T(8,128)(2,1)} %get-tuple-element.8.d3_ref.r_ref), custom_call_target="tpu_custom_call" | custom-call | flops 6039797760 | bytes 20447232 | tf_op jit(solution)/shard_map/pallas_call | solution.py:105
  344.9 1.2 slice.48
  346.1 0.9 slice.50
  347.0 0.9 slice.49.tail_ref
  348.0 0.1 reshape.104
  348.1 11.8 %gather_fusion.3 = f32[2048]{0:T(1024)S(1)} fusion(f32[2560]{0:T(1024)S(1)} %reshape.104, s32[2048]{0:T(1024)S(1)} %broadcast_clamp_fusion), kind=kCustom, calls=%fused_computation.3 | custom fusion | bytes 24576 | tf_op jit(solution)/shard_map/jit(_take)/gather | solution.py:288
  359.9 1.3 collective-permute-start.12
  361.2 125.4 %collective-permute-done.13 = f32[8,1024]{1,0:T(8,128)S(1)} collective-permute-done((f32[8,1024]{1,0:T(8,128)S(1)}, f32[8,1024]{1,0:T(8,128)S(1)}, u32[]{:S(2)}, u32[]{:S(2)}) %collective-permute-start.13) | collective-permute-done | bytes 32800 | tf_op jit(solution)/shard_map/ppermute | solution.py:237
  486.5 1.3 collective-permute-start.11
  487.8 0.6 broadcast_select_fusion.3
  488.5 25.4 %collective-permute-done.12 = f32[8,1024]{1,0:T(8,128)S(1)} collective-permute-done((f32[8,1024]{1,0:T(8,128)S(1)}, f32[8,1024]{1,0:T(8,128)S(1)}, u32[]{:S(2)}, u32[]{:S(2)}) %collective-permute-start.12) | collective-permute-done | bytes 32800 | tf_op jit(solution)/shard_map/ppermute | solution.py:237
  513.9 1.6 collective-permute-start.14
  515.5 0.7 collective-permute-start.15
  516.1 0.7 maximum_add_fusion.recv_ref
  516.8 12.7 %gather_fusion.2 = bf16[2048,768]{1,0:T(8,128)(2,1)} fusion(bf16[2560,768]{1,0:T(8,128)(2,1)} %bitcast.13, s32[2048]{0:T(1024)S(1)} %broadcast_clamp_fusion), kind=kCustom, calls=%fused_computation.2 | custom fusion | bytes 6299648 | tf_op jit(solution)/shard_map/jit(_take)/gather | solution.py:286
  529.5 5.3 shard_map.156.own_ref
  534.8 3.3 broadcast_select_fusion.1
  538.0 1.6 shard_map.157.own_ref
  539.7 0.9 copy-done.3
  540.6 2.5 shard_map.158.own_ref
  543.1 0.7 shard_map.159
  543.8 0.0 copy-start.1
  543.8 6.3 %shard_map.150 = f32[384,3072]{1,0:T(8,128)} custom-call(f32[384,3072]{1,0:T(8,128)} %shard_map.148.own_ref, f32[384,3072]{1,0:T(8,128)} %collective-permute-done.3.recv_ref), custom_call_target="tpu_custom_call", output_to_operand_aliasing={{}: (0, {})} | custom-call | flops 1179648 | bytes 14155776 | tf_op jit(solution)/shard_map/pallas_call | solution.py:161
  550.1 6.2 %shard_map.153 = f32[1536,768]{1,0:T(8,128)} custom-call(f32[1536,768]{1,0:T(8,128)} %shard_map.151.own_ref, f32[1536,768]{1,0:T(8,128)} %collective-permute-done.4.recv_ref), custom_call_target="tpu_custom_call", output_to_operand_aliasing={{}: (0, {})} | custom-call | flops 1179648 | bytes 14155776 | tf_op jit(solution)/shard_map/pallas_call | solution.py:161
  (30 shorter events, 0.2 us)
Async XLA Ops:
  0.6 28.8 %copy-start = (bf16[2048,768]{1,0:T(8,128)(2,1)S(1)}, bf16[2048,768]{1,0:T(8,128)(2,1)}, u32[]{:S(2)}) copy-start(bf16[2048,768]{1,0:T(8,128)(2,1)} %param.11) | copy-start | bytes 9437188
  0.6 9.0 %copy-start.2 = (f32[2048,1]{0,1:T(1,128)S(1)}, f32[2048,1]{0,1:T(1,128)}, u32[]{:S(2)}) copy-start(f32[2048,1]{0,1:T(1,128)} %param.14) | copy-start | bytes 24580
  24.0 17.8 %all-to-all-start.1 = ((f32[1,8,320]{2,0,1:T(1,128)}), f32[1,8,320]{2,0,1:T(1,128)S(1)}, u32[]{:S(2)}, u32[]{:S(2)}) async-start(f32[1,8,320]{2,0,1:T(1,128)} %select_n.72), calls=%async_computation.1 | async-start | bytes 24576 | tf_op jit(solution)/shard_map/all_to_all | solution.py:267
  41.8 4.7 copy-start.4
  41.8 51.0 %all-to-all-start = ((bf16[1,8,320,768]{3,2,0,1:T(8,128)(2,1)}), bf16[1,8,320,768]{3,2,0,1:T(8,128)(2,1)}, u32[]{:S(2)}, u32[]{:S(2)}) async-start(bf16[1,8,320,768]{3,2,0,1:T(8,128)(2,1)} %broadcast_select_fusion), calls=%async_computation | async-start | bytes 7864320 | tf_op jit(solution)/shard_map/all_to_all | solution.py:266
  46.5 56.5 %collective-permute-start = (bf16[1536,768]{1,0:T(8,128)(2,1)S(1)}, bf16[1536,768]{1,0:T(8,128)(2,1)}, u32[]{:S(2)}, u32[]{:S(2)}) collective-permute-start(bf16[1536,768]{1,0:T(8,128)(2,1)S(1)} %bitcast.45), channel_id=1, source_target_pairs={{0,8},{8,0},{1,9},{9,1},{2,10},{10,2},{3,11},{11,3},{4,12},{12,4},... | collective-permute-start | bytes 7077896 | tf_op jit(solution)/shard_map/ppermute | solution.py:231
  48.1 150.8 %collective-permute-start.1 = (bf16[384,3072]{1,0:T(8,128)(2,1)}, bf16[384,3072]{1,0:T(8,128)(2,1)}, u32[]{:S(2)}, u32[]{:S(2)}) collective-permute-start(bf16[384,3072]{1,0:T(8,128)(2,1)} %bitcast.46), channel_id=1, source_target_pairs={{0,8},{8,0},{1,9},{9,1},{2,10},{10,2},{3,11},{11,3},{4,12},{12,4},... | collective-permute-start | bytes 7077896 | tf_op jit(solution)/shard_map/ppermute | solution.py:231
  48.5 153.3 %collective-permute-start.2 = (bf16[384,3072]{1,0:T(8,128)(2,1)}, bf16[384,3072]{1,0:T(8,128)(2,1)}, u32[]{:S(2)}, u32[]{:S(2)}) collective-permute-start(bf16[384,3072]{1,0:T(8,128)(2,1)} %bitcast.48), channel_id=1, source_target_pairs={{0,8},{8,0},{1,9},{9,1},{2,10},{10,2},{3,11},{11,3},{4,12},{12,4},... | collective-permute-start | bytes 7077896 | tf_op jit(solution)/shard_map/ppermute | solution.py:231
  99.6 145.6 %all-to-all-start.3 = ((f32[1,8,320]{2,0,1:T(1,128)}), f32[1,8,320]{2,0,1:T(1,128)S(1)}, u32[]{:S(2)}, u32[]{:S(2)}) async-start(f32[1,8,320]{2,0,1:T(1,128)} %reshape.103), calls=%async_computation.3 | async-start | bytes 24576 | tf_op jit(solution)/shard_map/all_to_all | solution.py:285
  157.7 386.1 %collective-permute-start.3 = (f32[384,3072]{1,0:T(8,128)}, f32[384,3072]{1,0:T(8,128)}, u32[]{:S(2)}, u32[]{:S(2)}) collective-permute-start(f32[384,3072]{1,0:T(8,128)} %shard_map.149), channel_id=1, source_target_pairs={{0,8},{8,0},{1,9},{9,1},{2,10},{10,2},{3,11},{11,3},{4,12},{12,4},... | collective-permute-start | bytes 14155784 | tf_op jit(solution)/shard_map/ppermute | solution.py:231
  180.1 370.0 %collective-permute-start.4 = (f32[1536,768]{1,0:T(8,128)}, f32[1536,768]{1,0:T(8,128)}, u32[]{:S(2)}, u32[]{:S(2)}) collective-permute-start(f32[1536,768]{1,0:T(8,128)} %shard_map.152), channel_id=1, source_target_pairs={{0,8},{8,0},{1,9},{9,1},{2,10},{10,2},{3,11},{11,3},{4,12},{12,4},... | collective-permute-start | bytes 14155784 | tf_op jit(solution)/shard_map/ppermute | solution.py:231
  197.3 332.2 %collective-permute-start.5 = (f32[288,3072]{1,0:T(8,128)}, f32[288,3072]{1,0:T(8,128)}, u32[]{:S(2)}, u32[]{:S(2)}) collective-permute-start(f32[288,3072]{1,0:T(8,128)} %slice.43), channel_id=1, source_target_pairs={{0,8},{8,0},{1,9},{9,1},{2,10},{10,2},{3,11},{11,3},{4,12},{12,4},... | collective-permute-start | bytes 10616840 | tf_op jit(solution)/shard_map/ppermute | solution.py:231
  245.2 271.6 %all-to-all-start.2 = ((bf16[1,8,320,768]{3,2,0,1:T(8,128)(2,1)}), bf16[1,8,320,768]{3,2,0,1:T(8,128)(2,1)}, u32[]{:S(2)}, u32[]{:S(2)}) async-start(bf16[1,8,320,768]{3,2,0,1:T(8,128)(2,1)} %bitcast.40), calls=%async_computation.2 | async-start | bytes 7864320 | tf_op jit(solution)/shard_map/all_to_all | solution.py:284
  250.5 43.3 %collective-permute-start.9 = (f32[8,1024]{1,0:T(8,128)S(1)}, f32[8,1024]{1,0:T(8,128)S(1)}, u32[]{:S(2)}, u32[]{:S(2)}) collective-permute-start(f32[8,1024]{1,0:T(8,128)S(1)} %get-tuple-element.14), channel_id=1, source_target_pairs={{0,6},{1,7},{8,14},{9,15}} | collective-permute-start | bytes 98312 | tf_op jit(solution)/shard_map/ppermute | solution.py:237
  255.3 52.6 %collective-permute-start.7 = (f32[8,1024]{1,0:T(8,128)S(1)}, f32[8,1024]{1,0:T(8,128)S(1)}, u32[]{:S(2)}, u32[]{:S(2)}) collective-permute-start(f32[8,1024]{1,0:T(8,128)S(1)} %get-tuple-element.15), channel_id=1, source_target_pairs={{0,2},{1,3},{8,10},{9,11}} | collective-permute-start | bytes 98312 | tf_op jit(solution)/shard_map/ppermute | solution.py:237
  293.9 14.0 %collective-permute-start.8 = (f32[8,1024]{1,0:T(8,128)S(1)}, f32[8,1024]{1,0:T(8,128)S(1)}, u32[]{:S(2)}, u32[]{:S(2)}) collective-permute-start(f32[8,1024]{1,0:T(8,128)S(1)} %get-tuple-element.13), channel_id=1, source_target_pairs={{0,4},{1,5},{8,12},{9,13}} | collective-permute-start | bytes 98312 | tf_op jit(solution)/shard_map/ppermute | solution.py:237
  307.9 23.1 %collective-permute-start.10 = (f32[8,1024]{1,0:T(8,128)S(1)}, f32[8,1024]{1,0:T(8,128)S(1)}, u32[]{:S(2)}, u32[]{:S(2)}) collective-permute-start(f32[8,1024]{1,0:T(8,128)S(1)} %add_add_fusion), channel_id=1, source_target_pairs={{2,10},{3,11},{4,12},{5,13},{6,14},{7,15},{10,2},{11,3},{12,4},{13... | collective-permute-start | bytes 98312 | tf_op jit(solution)/shard_map/ppermute | solution.py:237
  330.4 29.5 %collective-permute-start.6 = (f32[8,3072]{1,0:T(8,128)S(1)}, f32[8,3072]{1,0:T(8,128)S(1)}, u32[]{:S(2)}, u32[]{:S(2)}) collective-permute-start(f32[8,3072]{1,0:T(8,128)S(1)} %slice.44), channel_id=1, source_target_pairs={{2,10},{3,11},{4,12},{5,13},{6,14},{7,15},{10,2},{11,3},{12,4},{13... | collective-permute-start | bytes 294920 | tf_op jit(solution)/shard_map/ppermute | solution.py:237
  331.0 155.5 %collective-permute-start.13 = (f32[8,1024]{1,0:T(8,128)S(1)}, f32[8,1024]{1,0:T(8,128)S(1)}, u32[]{:S(2)}, u32[]{:S(2)}) collective-permute-start(f32[8,1024]{1,0:T(8,128)S(1)} %collective-permute-done.10), channel_id=1, source_target_pairs={{6,0},{7,1},{14,8},{15,9}} | collective-permute-start | bytes 98312 | tf_op jit(solution)/shard_map/ppermute | solution.py:237
  359.9 154.0 %collective-permute-start.12 = (f32[8,1024]{1,0:T(8,128)S(1)}, f32[8,1024]{1,0:T(8,128)S(1)}, u32[]{:S(2)}, u32[]{:S(2)}) collective-permute-start(f32[8,1024]{1,0:T(8,128)S(1)} %collective-permute-done.10), channel_id=1, source_target_pairs={{4,0},{5,1},{12,8},{13,9}} | collective-permute-start | bytes 98312 | tf_op jit(solution)/shard_map/ppermute | solution.py:237
  486.5 28.9 %collective-permute-start.11 = (f32[8,1024]{1,0:T(8,128)S(1)}, f32[8,1024]{1,0:T(8,128)S(1)}, u32[]{:S(2)}, u32[]{:S(2)}) collective-permute-start(f32[8,1024]{1,0:T(8,128)S(1)} %collective-permute-done.10), channel_id=1, source_target_pairs={{2,0},{3,1},{10,8},{11,9}} | collective-permute-start | bytes 98312 | tf_op jit(solution)/shard_map/ppermute | solution.py:237
  513.9 25.8 %collective-permute-start.14 = (f32[72,3072]{1,0:T(8,128)S(1)}, f32[72,3072]{1,0:T(8,128)S(1)}, u32[]{:S(2)}, u32[]{:S(2)}) collective-permute-start(f32[72,3072]{1,0:T(8,128)S(1)} %slice.48), channel_id=1, source_target_pairs={{0,8},{8,0},{1,9},{9,1},{2,10},{10,2},{3,11},{11,3},{4,12},{12,4},... | collective-permute-start | bytes 2654216 | tf_op jit(solution)/shard_map/ppermute | solution.py:231
  515.5 27.6 %collective-permute-start.15 = (f32[16,3072]{1,0:T(8,128)S(1)}, f32[16,3072]{1,0:T(8,128)S(1)}, u32[]{:S(2)}, u32[]{:S(2)}) collective-permute-start(f32[16,3072]{1,0:T(8,128)S(1)} %slice.50), channel_id=1, source_target_pairs={{0,8},{8,0},{1,9},{9,1},{2,10},{10,2},{3,11},{11,3},{4,12},{12,4},... | collective-permute-start | bytes 589832 | tf_op jit(solution)/shard_map/ppermute | solution.py:231
  539.7 0.9 copy-start.3
  543.8 12.5 %copy-start.1 = (bf16[2048,768]{1,0:T(8,128)(2,1)S(1)}, bf16[2048,768]{1,0:T(8,128)(2,1)}, u32[]{:S(2)}) copy-start(bf16[2048,768]{1,0:T(8,128)(2,1)} %param.11) | copy-start | bytes 9437188

commit v6 on v5

--- a/solution.py
+++ b/solution.py
@@ -231,20 +231,31 @@
         return lax.ppermute(value, 'fsdp', swap)
 
     near = 2
-    far = range(1, ep_n // near)
+    chips = ep_n // near
+    odd = [near * k + 1 for k in range(chips)]
 
     def send(value, moves):
-        return lax.ppermute(value, ('fsdp', 'ep'), [(a * ep_n + b, c * ep_n + d) for (a, b), (c, d) in moves])
-
-    def detour(value):
-        cols = value.shape[1] // len(far)
-        grid = [(f, c) for f in range(fs_n) for c in range(near)]
-        rest = [((f, e), (fs_n - 1 - f, e)) for f in range(fs_n) for e in range(near, ep_n)]
-        out = [send(value[:, (k - 1) * cols:k * cols], [((f, c), (f, near * k + c)) for f, c in grid]) for k in far]
-        crossed = send(sum(out[1:], out[0]), rest)
-        direct = send(value, rest)
-        back = [send(crossed, [((f, near * k + c), (f, c)) for f, c in grid]) for k in far]
-        return direct, jnp.concatenate(back, axis=1)
+        return lax.ppermute(value, ('fsdp', 'ep'), [(f * ep_n + a, g * ep_n + b) for f in range(fs_n) for a, b, g in moves(f)])
+
+    def within(pairs):
+        return lambda f: [(a, b, f) for a, b in pairs]
+
+    def across(devices):
+        return lambda f: [(e, e, fs_n - 1 - f) for e in devices]
+
+    def balanced(value):
+        third = value.shape[1] * 5 // 24
+        cut = value.shape[1] - 3 * third
+        side, long = value[:, :cut], value[:, cut:]
+        handed = send(side, within([(e - 1, e) for e in odd]))
+        parts = [send(long[:, n * third:(n + 1) * third], within([(0, e)])) for n, e in enumerate(odd[1:])]
+        handed = send(handed, across(odd))
+        passed = send(sum(parts[1:], parts[0]), across(odd[1:]))
+        own_side = send(side, across(odd))
+        own_long = send(long, across(range(1, ep_n)))
+        handed = send(handed, within([(e, e - 1) for e in odd]))
+        back = [send(passed, within([(e, 0)])) for e in odd[1:]]
+        return own_side, handed, own_long, back
 
     def local_backward(grad_out, expert_idx, slot_pos, gates, x_disp, h_gate, h_up, y_disp, w_gate, w_down, w_up):
         tok_n, top_n = expert_idx.shape
@@ -276,7 +287,7 @@
         step = send_up.shape[0] // 16
         cuts = (0, 12 * step, 15 * step, 15 * step + step // 3, 16 * step)
         piece = [send_up[lo:hi] for lo, hi in zip(cuts, cuts[1:])]
-        direct, around = detour(piece[2])
+        own_side, handed, own_long, back = balanced(piece[2])
         recv_up = [exchange(piece[0]), exchange(piece[1]), exchange(piece[3])]
 
         dx_rows = row_grads(z, dh_gate, dh_up, w_gate, other_w_gate, w_up, other_w_up)
@@ -294,7 +305,8 @@
         grad_w_gate = add_rows(grad_w_gate, recv_gate, 0, 4 * step)
         tail = grad_w_up[cuts[3]:]
         grad_w_up = add_piece(grad_w_up, recv_up[0], cuts[0])
-        grad_w_up = add_piece(grad_w_up, direct + around, cuts[2])
+        band = jnp.concatenate([own_side + handed, own_long + jnp.concatenate(back, axis=1)], axis=1)
+        grad_w_up = add_piece(grad_w_up, band, cuts[2])
         grad_w_up = add_piece(grad_w_up, recv_up[1], cuts[1])
         grad_w_up = add_last(grad_w_up, tail, recv_up[-1])
         return grad_x, grad_gates, grad_w_gate[None], grad_w_down[None], grad_w_up[None]

time: 559 us -> 564 us (level)
    ppermute x8 -> x12, starting transfers between devices: 12.7 us -> 16.3 us  [send(): lax.ppermute(value, ('fsdp', 'ep'), [(f * ep_n + a, g * ep_n + b) for f i...]
    ppermute x8 -> x12, waiting for transfers between devices: 188 us -> 190 us  [send(): lax.ppermute(value, ('fsdp', 'ep'), [(f * ep_n + a, g * ep_n + b) for f i...]
  transfers between devices with their start and end apart: 20 -> 24, of which waited for: 5 -> 7; matrix products, arithmetic and copies ran while one was open for 10% -> 10% of each run, Pallas kernels for 35% -> 35%
where the time goes in v6:
time: 564 us; the launch traced here: 561 us
  waiting for transfers between devices  235 us (42%)
  Pallas kernels  200 us (35%)
  local copies, waits for them, and re-layouts  66.8 us (12%)
  starting transfers between devices  42.4 us (8%)
  other arithmetic  15.5 us (3%)
    ppermute x12, waiting for transfers between devices, send(): lax.ppermute(value, ('fsdp', 'ep'), [(f * ep_n + a, g * ep_n + b) for f i...  190 us
    pallas_call x4, Pallas kernels, weight_grad_rhs(): pl.pallas_call(kernel, grid_spec=pltpu.PrefetchScalarGridSpec(num_scalar_...  50.1 us
    pallas_call x1, Pallas kernels, row_grads(): pl.pallas_call(kernel, grid_spec=pltpu.PrefetchScalarGridSpec(num_scalar_...  43.4 us
    all_to_all x1, waiting for transfers between devices, local_backward(): lax.all_to_all(send_dy, 'ep', 1, 1, tiled=True).reshape(rows_loc, width)  42.5 us
    pallas_call x1, Pallas kernels, hidden_grads(): pl.pallas_call(kernel, grid_spec=pltpu.PrefetchScalarGridSpec(num_scalar_...  42.2 us
    pallas_call x2, Pallas kernels, down_grad(): pl.pallas_call(kernel, grid_spec=pltpu.PrefetchScalarGridSpec(num_scalar_...  41.8 us
    ppermute x12, starting transfers between devices, send(): lax.ppermute(value, ('fsdp', 'ep'), [(f * ep_n + a, g * ep_n + b) for f i...  16.3 us
    gather x1, local copies, waits for them, and re-layouts, local_backward(): jnp.take(gates.reshape(-1), src_choice, mode='fill', fill_value=0)  13.6 us
  transfers between devices with their start and end apart: 24, of which 7 were waited for; matrix products, arithmetic and copies ran while one was open for 10% of the time, Pallas kernels for 35%

profile of v6, /device:TPU:0, one launch (start us, length us, event | category | flops | bytes accessed | tf_op | source)
XLA Modules:
  0.0 560.8 jit_solution(17920040280201729156)
XLA Ops:
  0.7 0.9 fusion.4
  1.6 8.1 %scatter_custom_fusion = s32[2560]{0:T(1024)S(1)} fusion(s32[2048]{0:T(1024)S(1)} %bitcast.41, s32[2048]{0:T(1024)S(1)} %iota.3, s32[]{:T(128)} %constant.98.clone.1), kind=kCustom, calls=%fused_computation.21 | custom fusion | bytes 10244 | tf_op jit(solution)/shard_map/scatter | solution.py:274
  9.7 13.6 %gather_fusion.1 = f32[2560]{0:T(1024)S(1)} fusion(f32[2048]{0:T(1024)S(1)} %bitcast.25, s32[3072]{0:T(1024)S(1)} %pad_clamp_fusion), kind=kCustom, calls=%fused_computation.1 | custom fusion | bytes 30720 | tf_op jit(solution)/shard_map/jit(_take)/gather | solution.py:276
  23.3 0.7 select_n.72
  24.0 5.4 all-to-all-start.1
  29.5 8.5 %gather_fusion = bf16[2560,768]{1,0:T(8,128)(2,1)} fusion(bf16[2048,768]{1,0:T(8,128)(2,1)S(1)} %copy-done, s32[3072]{0:T(1024)S(1)} %pad_clamp_fusion), kind=kCustom, calls=%fused_computation | custom fusion | bytes 7874560 | tf_op jit(solution)/shard_map/jit(_take)/gather | solution.py:275
  38.0 3.7 broadcast_select_fusion
  41.8 4.7 all-to-all-start
  46.5 1.6 collective-permute-start
  48.6 1.6 collective-permute-start.2
  50.2 42.5 %all-to-all-done = bf16[1,8,320,768]{3,2,0,1:T(8,128)(2,1)} async-done(((bf16[1,8,320,768]{3,2,0,1:T(8,128)(2,1)}), bf16[1,8,320,768]{3,2,0,1:T(8,128)(2,1)}, u32[]{:S(2)}, u32[]{:S(2)}) %all-to-all-start) | async-done | bytes 3932192 | tf_op jit(solution)/shard_map/all_to_all | solution.py:277
  92.8 6.2 %fusion.1 = (f32[2560]{0:T(1024)S(1)}, bf16[2560,768]{1,0:T(8,128)(2,1)}) fusion(bf16[1,2560,768]{2,1,0:T(8,128)(2,1)} %param.18, bf16[1,8,320,768]{3,2,0,1:T(8,128)(2,1)} %all-to-all-done, f32[2560]{0:T(1024)S(1)} %mul.21), kind=kLoop, calls=%fused_computation.8 | loop fusion | flops 11793920 | bytes 11816960 | tf_op jit(solution)/shard_map/rd,rd->r/dot_general | solution.py:294
  98.9 0.7 reshape.103
  99.6 3.3 all-to-all-start.3
  103.0 42.2 %shard_map.146 = (bf16[2560,3072]{1,0:T(8,128)(2,1)}, bf16[2560,3072]{1,0:T(8,128)(2,1)}) custom-call(s32[1]{0:T(128)} %bitcast.z_ref.s_ref, bf16[2560,768]{1,0:T(8,128)(2,1)} %get-tuple-element.17.g_ref, bf16[1536,768]{1,0:T(8,128)(2,1)} %bitcast.44, bf16[1536,768]{1,0:T(8,128)(2,1)} %collective-permute-done.other_ref, bf16[2560,3072]{1,0:T(8,128)(2,1)} %bitcast.27, ...), custom_call_target="tpu_custom_call" | custom-call | flops 12079595520 | bytes 62914560 | tf_op jit(solution)/shard_map/pallas_call | solution.py:44
  145.1 12.5 %shard_map.149 = f32[384,3072]{1,0:T(8,128)} custom-call(s32[1]{0:T(128)S(6)} %sub.10.s_ref, bf16[2560,768]{1,0:T(8,128)(2,1)} %bitcast.33, bf16[2560,3072]{1,0:T(8,128)(2,1)} %get-tuple-element.7.d1_ref.r_ref), custom_call_target="tpu_custom_call" | custom-call | flops 6039797760 | bytes 20447232 | tf_op jit(solution)/shard_map/pallas_call | solution.py:105
  157.7 1.6 collective-permute-start.3
  159.3 20.9 %shard_map.152 = f32[1536,768]{1,0:T(8,128)} custom-call(s32[1]{0:T(128)S(6)} %sub.10.s_ref, bf16[2560,3072]{1,0:T(8,128)(2,1)} %bitcast.28, bf16[2560,3072]{1,0:T(8,128)(2,1)} %bitcast.31, bf16[2560,768]{1,0:T(8,128)(2,1)} %get-tuple-element.17.g_ref), custom_call_target="tpu_custom_call" | custom-call | flops 6039797760 | bytes 31457280 | tf_op jit(solution)/shard_map/pallas_call | solution.py:84
  180.6 12.5 %shard_map.155 = f32[384,3072]{1,0:T(8,128)} custom-call(s32[1]{0:T(128)S(6)} %sub.10.s_ref, bf16[2560,768]{1,0:T(8,128)(2,1)} %bitcast.34, bf16[2560,3072]{1,0:T(8,128)(2,1)} %get-tuple-element.8.d3_ref.r_ref), custom_call_target="tpu_custom_call" | custom-call | flops 6039797760 | bytes 20447232 | tf_op jit(solution)/shard_map/pallas_call | solution.py:105
  193.1 4.2 slice.50
  197.3 1.6 collective-permute-start.5
  198.9 3.0 collective-permute-done.2.u1_ref
  201.9 43.4 %shard_map.147 = bf16[2560,768]{1,0:T(8,128)(2,1)} custom-call(s32[1]{0:T(128)} %bitcast.z_ref.s_ref, bf16[2560,3072]{1,0:T(8,128)(2,1)} %get-tuple-element.7.d1_ref.r_ref, bf16[2560,3072]{1,0:T(8,128)(2,1)} %get-tuple-element.8.d3_ref.r_ref, bf16[384,3072]{1,0:T(8,128)(2,1)} %bitcast.47, bf16[384,3072]{1,0:T(8,128)(2,1)} %collective-permute-done.1.g1_ref, ...), custom_call_target="tpu_custom_call" | custom-call | flops 24159191040 | bytes 62914560 | tf_op jit(solution)/shard_map/pallas_call | solution.py:140
  245.2 4.5 all-to-all-start.2
  249.8 0.8 fusion.5
  250.5 4.4 collective-permute-start.13
  255.0 1.3 collective-permute-start.11
  256.3 36.9 %collective-permute-done.13 = f32[8,640]{1,0:T(8,128)S(1)} collective-permute-done((f32[8,640]{1,0:T(8,128)S(1)}, f32[8,640]{1,0:T(8,128)S(1)}, u32[]{:S(2)}, u32[]{:S(2)}) %collective-permute-start.13) | collective-permute-done | bytes 20512 | tf_op jit(solution)/shard_map/ppermute | solution.py:238
  293.2 1.5 collective-permute-start.12
  294.7 12.5 %shard_map.148.own_ref = f32[384,3072]{1,0:T(8,128)} custom-call(s32[1]{0:T(128)} %bitcast.z_ref.s_ref, bf16[2560,768]{1,0:T(8,128)(2,1)} %bitcast.35, bf16[2560,3072]{1,0:T(8,128)(2,1)} %get-tuple-element.7.d1_ref.r_ref), custom_call_target="tpu_custom_call" | custom-call | flops 6039797760 | bytes 20447232 | tf_op jit(solution)/shard_map/pallas_call | solution.py:105
  307.2 0.8 slice.52
  308.0 0.8 slice.51
  308.8 0.7 collective-permute-start.10
  309.5 1.3 collective-permute-start.7
  310.8 0.8 collective-permute-done.7
  311.6 0.7 collective-permute-start.14
  312.3 20.9 %shard_map.151.own_ref = f32[1536,768]{1,0:T(8,128)} custom-call(s32[1]{0:T(128)} %bitcast.z_ref.s_ref, bf16[2560,3072]{1,0:T(8,128)(2,1)} %bitcast.29, bf16[2560,3072]{1,0:T(8,128)(2,1)} %bitcast.32, bf16[2560,768]{1,0:T(8,128)(2,1)} %get-tuple-element.17.g_ref), custom_call_target="tpu_custom_call" | custom-call | flops 6039797760 | bytes 31457280 | tf_op jit(solution)/shard_map/pallas_call | solution.py:84
  333.2 1.3 collective-permute-start.17
  334.5 1.3 collective-permute-start.16
  335.8 12.5 %shard_map.154.own_ref = f32[384,3072]{1,0:T(8,128)} custom-call(s32[1]{0:T(128)} %bitcast.z_ref.s_ref, bf16[2560,768]{1,0:T(8,128)(2,1)} %bitcast.36, bf16[2560,3072]{1,0:T(8,128)(2,1)} %get-tuple-element.8.d3_ref.r_ref), custom_call_target="tpu_custom_call" | custom-call | flops 6039797760 | bytes 20447232 | tf_op jit(solution)/shard_map/pallas_call | solution.py:105
  348.3 1.2 slice.56
  349.5 0.9 slice.58
  350.5 0.9 slice.57.tail_ref
  351.5 11.8 %gather_fusion.3 = f32[2048]{0:T(1024)S(1)} fusion(f32[2560]{0:T(1024)S(1)} %reshape.104, s32[2048]{0:T(1024)S(1)} %broadcast_clamp_fusion), kind=kCustom, calls=%fused_computation.3 | custom fusion | bytes 24576 | tf_op jit(solution)/shard_map/jit(_take)/gather | solution.py:299
  363.3 122.0 %collective-permute-done.17 = f32[8,640]{1,0:T(8,128)S(1)} collective-permute-done((f32[8,640]{1,0:T(8,128)S(1)}, f32[8,640]{1,0:T(8,128)S(1)}, u32[]{:S(2)}, u32[]{:S(2)}) %collective-permute-start.17) | collective-permute-done | bytes 20512 | tf_op jit(solution)/shard_map/ppermute | solution.py:238
  485.3 0.7 collective-permute-start.8
  485.9 1.3 collective-permute-start.15
  487.2 0.6 broadcast_select_fusion.3
  487.9 28.6 %collective-permute-done.15 = f32[8,640]{1,0:T(8,128)S(1)} collective-permute-done((f32[8,640]{1,0:T(8,128)S(1)}, f32[8,640]{1,0:T(8,128)S(1)}, u32[]{:S(2)}, u32[]{:S(2)}) %collective-permute-start.15) | collective-permute-done | bytes 20512 | tf_op jit(solution)/shard_map/ppermute | solution.py:238
  516.5 0.7 collective-permute-start.6
  517.1 1.3 collective-permute-start.9
  518.5 0.5 collective-permute-start.18
  519.0 1.3 collective-permute-done.9
  520.2 0.5 collective-permute-start.19
  520.7 0.7 pad_maximum_fusion.recv_ref
  521.4 12.7 %gather_fusion.2 = bf16[2048,768]{1,0:T(8,128)(2,1)} fusion(bf16[2560,768]{1,0:T(8,128)(2,1)} %bitcast.13, s32[2048]{0:T(1024)S(1)} %broadcast_clamp_fusion), kind=kCustom, calls=%fused_computation.2 | custom fusion | bytes 6299648 | tf_op jit(solution)/shard_map/jit(_take)/gather | solution.py:297
  534.0 5.3 shard_map.156.own_ref
  539.3 3.3 broadcast_select_fusion.1
  542.6 1.6 shard_map.157.own_ref
  544.2 0.9 copy-done.3
  545.1 2.5 shard_map.158.own_ref
  547.6 0.7 shard_map.159
  548.4 6.3 %shard_map.150 = f32[384,3072]{1,0:T(8,128)} custom-call(f32[384,3072]{1,0:T(8,128)} %shard_map.148.own_ref, f32[384,3072]{1,0:T(8,128)} %collective-permute-done.3.recv_ref), custom_call_target="tpu_custom_call", output_to_operand_aliasing={{}: (0, {})} | custom-call | flops 1179648 | bytes 14155776 | tf_op jit(solution)/shard_map/pallas_call | solution.py:161
  554.7 6.2 %shard_map.153 = f32[1536,768]{1,0:T(8,128)} custom-call(f32[1536,768]{1,0:T(8,128)} %shard_map.151.own_ref, f32[1536,768]{1,0:T(8,128)} %collective-permute-done.4.recv_ref), custom_call_target="tpu_custom_call", output_to_operand_aliasing={{}: (0, {})} | custom-call | flops 1179648 | bytes 14155776 | tf_op jit(solution)/shard_map/pallas_call | solution.py:161
  (41 shorter events, 1.3 us)
Async XLA Ops:
  0.6 28.8 %copy-start = (bf16[2048,768]{1,0:T(8,128)(2,1)S(1)}, bf16[2048,768]{1,0:T(8,128)(2,1)}, u32[]{:S(2)}) copy-start(bf16[2048,768]{1,0:T(8,128)(2,1)} %param.11) | copy-start | bytes 9437188
  0.6 9.0 %copy-start.2 = (f32[2048,1]{0,1:T(1,128)S(1)}, f32[2048,1]{0,1:T(1,128)}, u32[]{:S(2)}) copy-start(f32[2048,1]{0,1:T(1,128)} %param.14) | copy-start | bytes 24580
  24.0 17.8 %all-to-all-start.1 = ((f32[1,8,320]{2,0,1:T(1,128)}), f32[1,8,320]{2,0,1:T(1,128)S(1)}, u32[]{:S(2)}, u32[]{:S(2)}) async-start(f32[1,8,320]{2,0,1:T(1,128)} %select_n.72), calls=%async_computation.1 | async-start | bytes 24576 | tf_op jit(solution)/shard_map/all_to_all | solution.py:278
  41.8 4.7 copy-start.4
  41.8 51.0 %all-to-all-start = ((bf16[1,8,320,768]{3,2,0,1:T(8,128)(2,1)}), bf16[1,8,320,768]{3,2,0,1:T(8,128)(2,1)}, u32[]{:S(2)}, u32[]{:S(2)}) async-start(bf16[1,8,320,768]{3,2,0,1:T(8,128)(2,1)} %broadcast_select_fusion), calls=%async_computation | async-start | bytes 7864320 | tf_op jit(solution)/shard_map/all_to_all | solution.py:277
  46.5 56.5 %collective-permute-start = (bf16[1536,768]{1,0:T(8,128)(2,1)S(1)}, bf16[1536,768]{1,0:T(8,128)(2,1)}, u32[]{:S(2)}, u32[]{:S(2)}) collective-permute-start(bf16[1536,768]{1,0:T(8,128)(2,1)S(1)} %bitcast.45), channel_id=1, source_target_pairs={{0,8},{8,0},{1,9},{9,1},{2,10},{10,2},{3,11},{11,3},{4,12},{12,4},... | collective-permute-start | bytes 7077896 | tf_op jit(solution)/shard_map/ppermute | solution.py:231
  48.1 150.8 %collective-permute-start.1 = (bf16[384,3072]{1,0:T(8,128)(2,1)}, bf16[384,3072]{1,0:T(8,128)(2,1)}, u32[]{:S(2)}, u32[]{:S(2)}) collective-permute-start(bf16[384,3072]{1,0:T(8,128)(2,1)} %bitcast.46), channel_id=1, source_target_pairs={{0,8},{8,0},{1,9},{9,1},{2,10},{10,2},{3,11},{11,3},{4,12},{12,4},... | collective-permute-start | bytes 7077896 | tf_op jit(solution)/shard_map/ppermute | solution.py:231
  48.6 153.3 %collective-permute-start.2 = (bf16[384,3072]{1,0:T(8,128)(2,1)}, bf16[384,3072]{1,0:T(8,128)(2,1)}, u32[]{:S(2)}, u32[]{:S(2)}) collective-permute-start(bf16[384,3072]{1,0:T(8,128)(2,1)} %bitcast.48), channel_id=1, source_target_pairs={{0,8},{8,0},{1,9},{9,1},{2,10},{10,2},{3,11},{11,3},{4,12},{12,4},... | collective-permute-start | bytes 7077896 | tf_op jit(solution)/shard_map/ppermute | solution.py:231
  99.6 145.6 %all-to-all-start.3 = ((f32[1,8,320]{2,0,1:T(1,128)}), f32[1,8,320]{2,0,1:T(1,128)S(1)}, u32[]{:S(2)}, u32[]{:S(2)}) async-start(f32[1,8,320]{2,0,1:T(1,128)} %reshape.103), calls=%async_computation.3 | async-start | bytes 24576 | tf_op jit(solution)/shard_map/all_to_all | solution.py:296
  157.7 390.7 %collective-permute-start.3 = (f32[384,3072]{1,0:T(8,128)}, f32[384,3072]{1,0:T(8,128)}, u32[]{:S(2)}, u32[]{:S(2)}) collective-permute-start(f32[384,3072]{1,0:T(8,128)} %shard_map.149), channel_id=1, source_target_pairs={{0,8},{8,0},{1,9},{9,1},{2,10},{10,2},{3,11},{11,3},{4,12},{12,4},... | collective-permute-start | bytes 14155784 | tf_op jit(solution)/shard_map/ppermute | solution.py:231
  180.2 374.5 %collective-permute-start.4 = (f32[1536,768]{1,0:T(8,128)}, f32[1536,768]{1,0:T(8,128)}, u32[]{:S(2)}, u32[]{:S(2)}) collective-permute-start(f32[1536,768]{1,0:T(8,128)} %shard_map.152), channel_id=1, source_target_pairs={{0,8},{8,0},{1,9},{9,1},{2,10},{10,2},{3,11},{11,3},{4,12},{12,4},... | collective-permute-start | bytes 14155784 | tf_op jit(solution)/shard_map/ppermute | solution.py:231
  197.3 336.8 %collective-permute-start.5 = (f32[288,3072]{1,0:T(8,128)}, f32[288,3072]{1,0:T(8,128)}, u32[]{:S(2)}, u32[]{:S(2)}) collective-permute-start(f32[288,3072]{1,0:T(8,128)} %slice.50), channel_id=1, source_target_pairs={{0,8},{8,0},{1,9},{9,1},{2,10},{10,2},{3,11},{11,3},{4,12},{12,4},... | collective-permute-start | bytes 10616840 | tf_op jit(solution)/shard_map/ppermute | solution.py:231
  245.2 276.1 %all-to-all-start.2 = ((bf16[1,8,320,768]{3,2,0,1:T(8,128)(2,1)}), bf16[1,8,320,768]{3,2,0,1:T(8,128)(2,1)}, u32[]{:S(2)}, u32[]{:S(2)}) async-start(bf16[1,8,320,768]{3,2,0,1:T(8,128)(2,1)} %bitcast.40), calls=%async_computation.2 | async-start | bytes 7864320 | tf_op jit(solution)/shard_map/all_to_all | solution.py:295
  250.5 42.6 %collective-permute-start.13 = (f32[8,640]{1,0:T(8,128)S(1)}, f32[8,640]{1,0:T(8,128)S(1)}, u32[]{:S(2)}, u32[]{:S(2)}) collective-permute-start(f32[8,640]{1,0:T(8,128)S(1)} %get-tuple-element.14), channel_id=1, source_target_pairs={{0,7},{8,15}} | collective-permute-start | bytes 61448 | tf_op jit(solution)/shard_map/ppermute | solution.py:238
  255.0 53.8 %collective-permute-start.11 = (f32[8,640]{1,0:T(8,128)S(1)}, f32[8,640]{1,0:T(8,128)S(1)}, u32[]{:S(2)}, u32[]{:S(2)}) collective-permute-start(f32[8,640]{1,0:T(8,128)S(1)} %get-tuple-element.15), channel_id=1, source_target_pairs={{0,3},{8,11}} | collective-permute-start | bytes 61448 | tf_op jit(solution)/shard_map/ppermute | solution.py:238
  293.2 16.3 %collective-permute-start.12 = (f32[8,640]{1,0:T(8,128)S(1)}, f32[8,640]{1,0:T(8,128)S(1)}, u32[]{:S(2)}, u32[]{:S(2)}) collective-permute-start(f32[8,640]{1,0:T(8,128)S(1)} %get-tuple-element.13), channel_id=1, source_target_pairs={{0,5},{8,13}} | collective-permute-start | bytes 61448 | tf_op jit(solution)/shard_map/ppermute | solution.py:238
  308.8 25.7 %collective-permute-start.10 = (f32[8,1920]{1,0:T(8,128)S(1)}, f32[8,1920]{1,0:T(8,128)S(1)}, u32[]{:S(2)}, u32[]{:S(2)}) collective-permute-start(f32[8,1920]{1,0:T(8,128)S(1)} %slice.52), channel_id=1, source_target_pairs={{1,9},{2,10},{3,11},{4,12},{5,13},{6,14},{7,15},{9,1},{10,2},{11,3... | collective-permute-start | bytes 184328 | tf_op jit(solution)/shard_map/ppermute | solution.py:238
  309.5 2.1 collective-permute-start.7
  311.6 21.6 %collective-permute-start.14 = (f32[8,640]{1,0:T(8,128)S(1)}, f32[8,640]{1,0:T(8,128)S(1)}, u32[]{:S(2)}, u32[]{:S(2)}) collective-permute-start(f32[8,640]{1,0:T(8,128)S(1)} %add_add_fusion), channel_id=1, source_target_pairs={{3,11},{5,13},{7,15},{11,3},{13,5},{15,7}} | collective-permute-start | bytes 61448 | tf_op jit(solution)/shard_map/ppermute | solution.py:238
  333.2 152.1 %collective-permute-start.17 = (f32[8,640]{1,0:T(8,128)S(1)}, f32[8,640]{1,0:T(8,128)S(1)}, u32[]{:S(2)}, u32[]{:S(2)}) collective-permute-start(f32[8,640]{1,0:T(8,128)S(1)} %collective-permute-done.14), channel_id=1, source_target_pairs={{7,0},{15,8}} | collective-permute-start | bytes 61448 | tf_op jit(solution)/shard_map/ppermute | solution.py:238
  334.5 151.5 %collective-permute-start.16 = (f32[8,640]{1,0:T(8,128)S(1)}, f32[8,640]{1,0:T(8,128)S(1)}, u32[]{:S(2)}, u32[]{:S(2)}) collective-permute-start(f32[8,640]{1,0:T(8,128)S(1)} %collective-permute-done.14), channel_id=1, source_target_pairs={{5,0},{13,8}} | collective-permute-start | bytes 61448 | tf_op jit(solution)/shard_map/ppermute | solution.py:238
  485.3 31.9 %collective-permute-start.8 = (f32[8,1152]{1,0:T(8,128)S(1)}, f32[8,1152]{1,0:T(8,128)S(1)}, u32[]{:S(2)}, u32[]{:S(2)}) collective-permute-start(f32[8,1152]{1,0:T(8,128)S(1)} %collective-permute-done.7), channel_id=1, source_target_pairs={{1,9},{3,11},{5,13},{7,15},{9,1},{11,3},{13,5},{15,7}} | collective-permute-start | bytes 110600 | tf_op jit(solution)/shard_map/ppermute | solution.py:238
  485.9 30.5 %collective-permute-start.15 = (f32[8,640]{1,0:T(8,128)S(1)}, f32[8,640]{1,0:T(8,128)S(1)}, u32[]{:S(2)}, u32[]{:S(2)}) collective-permute-start(f32[8,640]{1,0:T(8,128)S(1)} %collective-permute-done.14), channel_id=1, source_target_pairs={{3,0},{11,8}} | collective-permute-start | bytes 61448 | tf_op jit(solution)/shard_map/ppermute | solution.py:238
  516.5 2.0 collective-permute-start.6
  517.1 3.1 collective-permute-start.9
  518.5 25.7 %collective-permute-start.18 = (f32[72,3072]{1,0:T(8,128)S(1)}, f32[72,3072]{1,0:T(8,128)S(1)}, u32[]{:S(2)}, u32[]{:S(2)}) collective-permute-start(f32[72,3072]{1,0:T(8,128)S(1)} %slice.56), channel_id=1, source_target_pairs={{0,8},{8,0},{1,9},{9,1},{2,10},{10,2},{3,11},{11,3},{4,12},{12,4},... | collective-permute-start | bytes 2654216 | tf_op jit(solution)/shard_map/ppermute | solution.py:231
  520.2 27.4 %collective-permute-start.19 = (f32[16,3072]{1,0:T(8,128)S(1)}, f32[16,3072]{1,0:T(8,128)S(1)}, u32[]{:S(2)}, u32[]{:S(2)}) collective-permute-start(f32[16,3072]{1,0:T(8,128)S(1)} %slice.58), channel_id=1, source_target_pairs={{0,8},{8,0},{1,9},{9,1},{2,10},{10,2},{3,11},{11,3},{4,12},{12,4},... | collective-permute-start | bytes 589832 | tf_op jit(solution)/shard_map/ppermute | solution.py:231
  544.2 0.9 copy-start.3
  548.4 12.5 %copy-start.1 = (bf16[2048,768]{1,0:T(8,128)(2,1)S(1)}, bf16[2048,768]{1,0:T(8,128)(2,1)}, u32[]{:S(2)}) copy-start(bf16[2048,768]{1,0:T(8,128)(2,1)} %param.11) | copy-start | bytes 9437188

commit v7 on v5

--- a/solution.py
+++ b/solution.py
@@ -274,9 +274,11 @@
         recv_gate = exchange(part)
         send_up = weight_grad_rhs(1 - z, x_rows, dh_up, fs_n)
         step = send_up.shape[0] // 16
-        cuts = (0, 12 * step, 15 * step, 15 * step + step // 3, 16 * step)
+        cuts = (0, 12 * step + step // 3, 15 * step, 15 * step + step // 3, 16 * step)
         piece = [send_up[lo:hi] for lo, hi in zip(cuts, cuts[1:])]
-        direct, around = detour(piece[2])
+        half = piece[2].shape[1] // 2
+        direct, around = detour(piece[2][:, :half])
+        plain = exchange(piece[2][:, half:])
         recv_up = [exchange(piece[0]), exchange(piece[1]), exchange(piece[3])]
 
         dx_rows = row_grads(z, dh_gate, dh_up, w_gate, other_w_gate, w_up, other_w_up)
@@ -294,7 +296,7 @@
         grad_w_gate = add_rows(grad_w_gate, recv_gate, 0, 4 * step)
         tail = grad_w_up[cuts[3]:]
         grad_w_up = add_piece(grad_w_up, recv_up[0], cuts[0])
-        grad_w_up = add_piece(grad_w_up, direct + around, cuts[2])
+        grad_w_up = add_piece(grad_w_up, jnp.concatenate([direct + around, plain], axis=1), cuts[2])
         grad_w_up = add_piece(grad_w_up, recv_up[1], cuts[1])
         grad_w_up = add_last(grad_w_up, tail, recv_up[-1])
         return grad_x, grad_gates, grad_w_gate[None], grad_w_down[None], grad_w_up[None]

time: 559 us -> 555 us (level)
  waiting for transfers between devices: 234 us -> 227 us
    ppermute x8, waiting for transfers between devices: 188 us -> 182 us  [send(): lax.ppermute(value, ('fsdp', 'ep'), [(a * ep_n + b, c * ep_n + d) for (a,...]
  transfers between devices with their start and end apart: 20 -> 21, of which waited for: 5 -> 5; matrix products, arithmetic and copies ran while one was open for 10% -> 10% of each run, Pallas kernels for 35% -> 35%
where the time goes in v7:
time: 555 us; the launch traced here: 552 us
  waiting for transfers between devices  227 us (41%)
  Pallas kernels  200 us (36%)
  local copies, waits for them, and re-layouts  66 us (12%)
  starting transfers between devices  42.6 us (8%)
  other arithmetic  15.5 us (3%)
    ppermute x8, waiting for transfers between devices, send(): lax.ppermute(value, ('fsdp', 'ep'), [(a * ep_n + b, c * ep_n + d) for (a,...  182 us
    pallas_call x4, Pallas kernels, weight_grad_rhs(): pl.pallas_call(kernel, grid_spec=pltpu.PrefetchScalarGridSpec(num_scalar_...  50.1 us
    pallas_call x1, Pallas kernels, row_grads(): pl.pallas_call(kernel, grid_spec=pltpu.PrefetchScalarGridSpec(num_scalar_...  43.4 us
    all_to_all x1, waiting for transfers between devices, local_backward(): lax.all_to_all(send_dy, 'ep', 1, 1, tiled=True).reshape(rows_loc, width)  42.5 us
    pallas_call x1, Pallas kernels, hidden_grads(): pl.pallas_call(kernel, grid_spec=pltpu.PrefetchScalarGridSpec(num_scalar_...  42.2 us
    pallas_call x2, Pallas kernels, down_grad(): pl.pallas_call(kernel, grid_spec=pltpu.PrefetchScalarGridSpec(num_scalar_...  41.8 us
    ppermute x8, starting transfers between devices, send(): lax.ppermute(value, ('fsdp', 'ep'), [(a * ep_n + b, c * ep_n + d) for (a,...  14.8 us
    gather x1, local copies, waits for them, and re-layouts, local_backward(): jnp.take(gates.reshape(-1), src_choice, mode='fill', fill_value=0)  13.6 us
  transfers between devices with their start and end apart: 21, of which 5 were waited for; matrix products, arithmetic and copies ran while one was open for 10% of the time, Pallas kernels for 35%

profile of v7, /device:TPU:0, one launch (start us, length us, event | category | flops | bytes accessed | tf_op | source)
XLA Modules:
  0.0 552.2 jit_solution(5896671190186124498)
XLA Ops:
  0.6 0.0 copy-start
  0.7 0.9 fusion.4
  1.6 8.1 %scatter_custom_fusion = s32[2560]{0:T(1024)S(1)} fusion(s32[2048]{0:T(1024)S(1)} %bitcast.41, s32[2048]{0:T(1024)S(1)} %iota.3, s32[]{:T(128)} %constant.98.clone.1), kind=kCustom, calls=%fused_computation.21 | custom fusion | bytes 10244 | tf_op jit(solution)/shard_map/scatter | solution.py:263
  9.7 13.6 %gather_fusion.1 = f32[2560]{0:T(1024)S(1)} fusion(f32[2048]{0:T(1024)S(1)} %bitcast.25, s32[3072]{0:T(1024)S(1)} %pad_clamp_fusion), kind=kCustom, calls=%fused_computation.1 | custom fusion | bytes 30720 | tf_op jit(solution)/shard_map/jit(_take)/gather | solution.py:265
  23.3 0.7 select_n.72
  24.0 5.4 all-to-all-start.1
  29.5 8.5 %gather_fusion = bf16[2560,768]{1,0:T(8,128)(2,1)} fusion(bf16[2048,768]{1,0:T(8,128)(2,1)S(1)} %copy-done, s32[3072]{0:T(1024)S(1)} %pad_clamp_fusion), kind=kCustom, calls=%fused_computation | custom fusion | bytes 7874560 | tf_op jit(solution)/shard_map/jit(_take)/gather | solution.py:264
  38.0 0.1 broadcast_in_dim.59
  38.0 3.7 broadcast_select_fusion
  41.8 4.7 all-to-all-start
  46.5 1.6 collective-permute-start
  48.1 0.4 collective-permute-start.1
  48.5 1.6 collective-permute-start.2
  50.2 0.1 mul.21
  50.2 42.5 %all-to-all-done = bf16[1,8,320,768]{3,2,0,1:T(8,128)(2,1)} async-done(((bf16[1,8,320,768]{3,2,0,1:T(8,128)(2,1)}), bf16[1,8,320,768]{3,2,0,1:T(8,128)(2,1)}, u32[]{:S(2)}, u32[]{:S(2)}) %all-to-all-start) | async-done | bytes 3932192 | tf_op jit(solution)/shard_map/all_to_all | solution.py:266
  92.8 6.2 %fusion.1 = (f32[2560]{0:T(1024)S(1)}, bf16[2560,768]{1,0:T(8,128)(2,1)}) fusion(bf16[1,2560,768]{2,1,0:T(8,128)(2,1)} %param.18, bf16[1,8,320,768]{3,2,0,1:T(8,128)(2,1)} %all-to-all-done, f32[2560]{0:T(1024)S(1)} %mul.21), kind=kLoop, calls=%fused_computation.8 | loop fusion | flops 11793920 | bytes 11816960 | tf_op jit(solution)/shard_map/rd,rd->r/dot_general | solution.py:285
  98.9 0.7 reshape.103
  99.6 3.3 all-to-all-start.3
  102.9 42.2 %shard_map.146 = (bf16[2560,3072]{1,0:T(8,128)(2,1)}, bf16[2560,3072]{1,0:T(8,128)(2,1)}) custom-call(s32[1]{0:T(128)} %bitcast.z_ref.s_ref, bf16[2560,768]{1,0:T(8,128)(2,1)} %get-tuple-element.19.g_ref, bf16[1536,768]{1,0:T(8,128)(2,1)} %bitcast.44, bf16[1536,768]{1,0:T(8,128)(2,1)} %collective-permute-done.other_ref, bf16[2560,3072]{1,0:T(8,128)(2,1)} %bitcast.27, ...), custom_call_target="tpu_custom_call" | custom-call | flops 12079595520 | bytes 62914560 | tf_op jit(solution)/shard_map/pallas_call | solution.py:44
  145.2 12.6 %shard_map.149 = f32[384,3072]{1,0:T(8,128)} custom-call(s32[1]{0:T(128)S(6)} %sub.10.s_ref, bf16[2560,768]{1,0:T(8,128)(2,1)} %bitcast.33, bf16[2560,3072]{1,0:T(8,128)(2,1)} %get-tuple-element.7.d1_ref.r_ref), custom_call_target="tpu_custom_call" | custom-call | flops 6039797760 | bytes 20447232 | tf_op jit(solution)/shard_map/pallas_call | solution.py:105
  157.7 1.5 collective-permute-start.3
  159.3 20.9 %shard_map.152 = f32[1536,768]{1,0:T(8,128)} custom-call(s32[1]{0:T(128)S(6)} %sub.10.s_ref, bf16[2560,3072]{1,0:T(8,128)(2,1)} %bitcast.28, bf16[2560,3072]{1,0:T(8,128)(2,1)} %bitcast.31, bf16[2560,768]{1,0:T(8,128)(2,1)} %get-tuple-element.19.g_ref), custom_call_target="tpu_custom_call" | custom-call | flops 6039797760 | bytes 31457280 | tf_op jit(solution)/shard_map/pallas_call | solution.py:84
  180.2 0.5 collective-permute-start.4
  180.7 12.5 %shard_map.155 = f32[384,3072]{1,0:T(8,128)} custom-call(s32[1]{0:T(128)S(6)} %sub.10.s_ref, bf16[2560,768]{1,0:T(8,128)(2,1)} %bitcast.34, bf16[2560,3072]{1,0:T(8,128)(2,1)} %get-tuple-element.8.d3_ref.r_ref), custom_call_target="tpu_custom_call" | custom-call | flops 6039797760 | bytes 20447232 | tf_op jit(solution)/shard_map/pallas_call | solution.py:105
  193.2 4.2 slice.50
  197.4 1.5 collective-permute-start.5
  199.0 0.8 fusion.5
  199.7 4.7 collective-permute-start.9
  204.5 43.4 %shard_map.147 = bf16[2560,768]{1,0:T(8,128)(2,1)} custom-call(s32[1]{0:T(128)} %bitcast.z_ref.s_ref, bf16[2560,3072]{1,0:T(8,128)(2,1)} %get-tuple-element.7.d1_ref.r_ref, bf16[2560,3072]{1,0:T(8,128)(2,1)} %get-tuple-element.8.d3_ref.r_ref, bf16[384,3072]{1,0:T(8,128)(2,1)} %bitcast.47, bf16[384,3072]{1,0:T(8,128)(2,1)} %collective-permute-done.1.g1_ref, ...), custom_call_target="tpu_custom_call" | custom-call | flops 24159191040 | bytes 62914560 | tf_op jit(solution)/shard_map/pallas_call | solution.py:140
  247.9 4.7 all-to-all-start.2
  252.6 12.5 %shard_map.148.own_ref = f32[384,3072]{1,0:T(8,128)} custom-call(s32[1]{0:T(128)} %bitcast.z_ref.s_ref, bf16[2560,768]{1,0:T(8,128)(2,1)} %bitcast.35, bf16[2560,3072]{1,0:T(8,128)(2,1)} %get-tuple-element.7.d1_ref.r_ref), custom_call_target="tpu_custom_call" | custom-call | flops 6039797760 | bytes 20447232 | tf_op jit(solution)/shard_map/pallas_call | solution.py:105
  265.1 3.6 collective-permute-start.7
  268.7 1.3 collective-permute-start.8
  270.0 20.9 %shard_map.151.own_ref = f32[1536,768]{1,0:T(8,128)} custom-call(s32[1]{0:T(128)} %bitcast.z_ref.s_ref, bf16[2560,3072]{1,0:T(8,128)(2,1)} %bitcast.29, bf16[2560,3072]{1,0:T(8,128)(2,1)} %bitcast.32, bf16[2560,768]{1,0:T(8,128)(2,1)} %get-tuple-element.19.g_ref), custom_call_target="tpu_custom_call" | custom-call | flops 6039797760 | bytes 31457280 | tf_op jit(solution)/shard_map/pallas_call | solution.py:84
  290.9 5.0 collective-permute-done.7
  296.0 0.7 collective-permute-start.10
  296.6 12.5 %shard_map.154.own_ref = f32[384,3072]{1,0:T(8,128)} custom-call(s32[1]{0:T(128)} %bitcast.z_ref.s_ref, bf16[2560,768]{1,0:T(8,128)(2,1)} %bitcast.36, bf16[2560,3072]{1,0:T(8,128)(2,1)} %get-tuple-element.8.d3_ref.r_ref), custom_call_target="tpu_custom_call" | custom-call | flops 6039797760 | bytes 20447232 | tf_op jit(solution)/shard_map/pallas_call | solution.py:105
  309.1 1.3 collective-permute-start.13
  310.4 1.3 collective-permute-start.12
  311.7 0.8 fusion.6
  312.6 1.2 slice.56
  313.8 0.9 slice.58
  314.7 0.9 slice.57.tail_ref
  315.7 0.1 reshape.104
  315.8 11.8 %gather_fusion.3 = f32[2048]{0:T(1024)S(1)} fusion(f32[2560]{0:T(1024)S(1)} %reshape.104, s32[2048]{0:T(1024)S(1)} %broadcast_clamp_fusion), kind=kCustom, calls=%fused_computation.3 | custom fusion | bytes 24576 | tf_op jit(solution)/shard_map/jit(_take)/gather | solution.py:290
  327.5 159.7 %collective-permute-done.13 = f32[8,512]{1,0:T(8,128)S(1)} collective-permute-done((f32[8,512]{1,0:T(8,128)S(1)}, f32[8,512]{1,0:T(8,128)S(1)}, u32[]{:S(2)}, u32[]{:S(2)}) %collective-permute-start.13) | collective-permute-done | bytes 16416 | tf_op jit(solution)/shard_map/ppermute | solution.py:237
  487.3 0.7 collective-permute-start.6
  488.0 1.3 collective-permute-start.11
  489.3 0.6 broadcast_select_fusion.3
  489.9 17.2 %collective-permute-done.11 = f32[8,512]{1,0:T(8,128)S(1)} collective-permute-done((f32[8,512]{1,0:T(8,128)S(1)}, f32[8,512]{1,0:T(8,128)S(1)}, u32[]{:S(2)}, u32[]{:S(2)}) %collective-permute-start.11) | collective-permute-done | bytes 16416 | tf_op jit(solution)/shard_map/ppermute | solution.py:237
  507.0 0.4 collective-permute-start.14
  507.5 1.6 collective-permute-start.15
  509.1 2.6 collective-permute-done.14
  511.7 0.5 collective-permute-start.16
  512.1 0.6 pad_maximum_fusion.recv_ref
  512.8 12.7 %gather_fusion.2 = bf16[2048,768]{1,0:T(8,128)(2,1)} fusion(bf16[2560,768]{1,0:T(8,128)(2,1)} %bitcast.13, s32[2048]{0:T(1024)S(1)} %broadcast_clamp_fusion), kind=kCustom, calls=%fused_computation.2 | custom fusion | bytes 6299648 | tf_op jit(solution)/shard_map/jit(_take)/gather | solution.py:288
  525.4 5.4 shard_map.156.own_ref
  530.8 3.3 broadcast_select_fusion.1
  534.1 1.6 shard_map.157.own_ref
  535.7 0.9 copy-done.3
  536.6 2.4 shard_map.158.own_ref
  539.0 0.7 shard_map.159
  539.7 6.3 %shard_map.150 = f32[384,3072]{1,0:T(8,128)} custom-call(f32[384,3072]{1,0:T(8,128)} %shard_map.148.own_ref, f32[384,3072]{1,0:T(8,128)} %collective-permute-done.3.recv_ref), custom_call_target="tpu_custom_call", output_to_operand_aliasing={{}: (0, {})} | custom-call | flops 1179648 | bytes 14155776 | tf_op jit(solution)/shard_map/pallas_call | solution.py:161
  546.0 6.2 %shard_map.153 = f32[1536,768]{1,0:T(8,128)} custom-call(f32[1536,768]{1,0:T(8,128)} %shard_map.151.own_ref, f32[1536,768]{1,0:T(8,128)} %collective-permute-done.4.recv_ref), custom_call_target="tpu_custom_call", output_to_operand_aliasing={{}: (0, {})} | custom-call | flops 1179648 | bytes 14155776 | tf_op jit(solution)/shard_map/pallas_call | solution.py:161
  (33 shorter events, 0.2 us)
Async XLA Ops:
  0.6 28.8 %copy-start = (bf16[2048,768]{1,0:T(8,128)(2,1)S(1)}, bf16[2048,768]{1,0:T(8,128)(2,1)}, u32[]{:S(2)}) copy-start(bf16[2048,768]{1,0:T(8,128)(2,1)} %param.11) | copy-start | bytes 9437188
  0.6 9.0 %copy-start.2 = (f32[2048,1]{0,1:T(1,128)S(1)}, f32[2048,1]{0,1:T(1,128)}, u32[]{:S(2)}) copy-start(f32[2048,1]{0,1:T(1,128)} %param.14) | copy-start | bytes 24580
  24.0 17.8 %all-to-all-start.1 = ((f32[1,8,320]{2,0,1:T(1,128)}), f32[1,8,320]{2,0,1:T(1,128)S(1)}, u32[]{:S(2)}, u32[]{:S(2)}) async-start(f32[1,8,320]{2,0,1:T(1,128)} %select_n.72), calls=%async_computation.1 | async-start | bytes 24576 | tf_op jit(solution)/shard_map/all_to_all | solution.py:267
  41.8 4.7 copy-start.4
  41.8 51.0 %all-to-all-start = ((bf16[1,8,320,768]{3,2,0,1:T(8,128)(2,1)}), bf16[1,8,320,768]{3,2,0,1:T(8,128)(2,1)}, u32[]{:S(2)}, u32[]{:S(2)}) async-start(bf16[1,8,320,768]{3,2,0,1:T(8,128)(2,1)} %broadcast_select_fusion), calls=%async_computation | async-start | bytes 7864320 | tf_op jit(solution)/shard_map/all_to_all | solution.py:266
  46.5 56.5 %collective-permute-start = (bf16[1536,768]{1,0:T(8,128)(2,1)S(1)}, bf16[1536,768]{1,0:T(8,128)(2,1)}, u32[]{:S(2)}, u32[]{:S(2)}) collective-permute-start(bf16[1536,768]{1,0:T(8,128)(2,1)S(1)} %bitcast.45), channel_id=1, source_target_pairs={{0,8},{8,0},{1,9},{9,1},{2,10},{10,2},{3,11},{11,3},{4,12},{12,4},... | collective-permute-start | bytes 7077896 | tf_op jit(solution)/shard_map/ppermute | solution.py:231
  48.1 151.6 %collective-permute-start.1 = (bf16[384,3072]{1,0:T(8,128)(2,1)}, bf16[384,3072]{1,0:T(8,128)(2,1)}, u32[]{:S(2)}, u32[]{:S(2)}) collective-permute-start(bf16[384,3072]{1,0:T(8,128)(2,1)} %bitcast.46), channel_id=1, source_target_pairs={{0,8},{8,0},{1,9},{9,1},{2,10},{10,2},{3,11},{11,3},{4,12},{12,4},... | collective-permute-start | bytes 7077896 | tf_op jit(solution)/shard_map/ppermute | solution.py:231
  48.5 155.9 %collective-permute-start.2 = (bf16[384,3072]{1,0:T(8,128)(2,1)}, bf16[384,3072]{1,0:T(8,128)(2,1)}, u32[]{:S(2)}, u32[]{:S(2)}) collective-permute-start(bf16[384,3072]{1,0:T(8,128)(2,1)} %bitcast.48), channel_id=1, source_target_pairs={{0,8},{8,0},{1,9},{9,1},{2,10},{10,2},{3,11},{11,3},{4,12},{12,4},... | collective-permute-start | bytes 7077896 | tf_op jit(solution)/shard_map/ppermute | solution.py:231
  99.6 148.3 %all-to-all-start.3 = ((f32[1,8,320]{2,0,1:T(1,128)}), f32[1,8,320]{2,0,1:T(1,128)S(1)}, u32[]{:S(2)}, u32[]{:S(2)}) async-start(f32[1,8,320]{2,0,1:T(1,128)} %reshape.103), calls=%async_computation.3 | async-start | bytes 24576 | tf_op jit(solution)/shard_map/all_to_all | solution.py:287
  157.7 382.0 %collective-permute-start.3 = (f32[384,3072]{1,0:T(8,128)}, f32[384,3072]{1,0:T(8,128)}, u32[]{:S(2)}, u32[]{:S(2)}) collective-permute-start(f32[384,3072]{1,0:T(8,128)} %shard_map.149), channel_id=1, source_target_pairs={{0,8},{8,0},{1,9},{9,1},{2,10},{10,2},{3,11},{11,3},{4,12},{12,4},... | collective-permute-start | bytes 14155784 | tf_op jit(solution)/shard_map/ppermute | solution.py:231
  180.2 365.9 %collective-permute-start.4 = (f32[1536,768]{1,0:T(8,128)}, f32[1536,768]{1,0:T(8,128)}, u32[]{:S(2)}, u32[]{:S(2)}) collective-permute-start(f32[1536,768]{1,0:T(8,128)} %shard_map.152), channel_id=1, source_target_pairs={{0,8},{8,0},{1,9},{9,1},{2,10},{10,2},{3,11},{11,3},{4,12},{12,4},... | collective-permute-start | bytes 14155784 | tf_op jit(solution)/shard_map/ppermute | solution.py:231
  197.4 328.0 %collective-permute-start.5 = (f32[296,3072]{1,0:T(8,128)}, f32[296,3072]{1,0:T(8,128)}, u32[]{:S(2)}, u32[]{:S(2)}) collective-permute-start(f32[296,3072]{1,0:T(8,128)} %slice.50), channel_id=1, source_target_pairs={{0,8},{8,0},{1,9},{9,1},{2,10},{10,2},{3,11},{11,3},{4,12},{12,4},... | collective-permute-start | bytes 10911752 | tf_op jit(solution)/shard_map/ppermute | solution.py:231
  199.7 69.0 %collective-permute-start.9 = (f32[8,512]{1,0:T(8,128)S(1)}, f32[8,512]{1,0:T(8,128)S(1)}, u32[]{:S(2)}, u32[]{:S(2)}) collective-permute-start(f32[8,512]{1,0:T(8,128)S(1)} %get-tuple-element.14), channel_id=1, source_target_pairs={{0,6},{1,7},{8,14},{9,15}} | collective-permute-start | bytes 49160 | tf_op jit(solution)/shard_map/ppermute | solution.py:237
  247.9 264.9 %all-to-all-start.2 = ((bf16[1,8,320,768]{3,2,0,1:T(8,128)(2,1)}), bf16[1,8,320,768]{3,2,0,1:T(8,128)(2,1)}, u32[]{:S(2)}, u32[]{:S(2)}) async-start(bf16[1,8,320,768]{3,2,0,1:T(8,128)(2,1)} %bitcast.40), calls=%async_computation.2 | async-start | bytes 7864320 | tf_op jit(solution)/shard_map/all_to_all | solution.py:286
  265.1 30.8 %collective-permute-start.7 = (f32[8,512]{1,0:T(8,128)S(1)}, f32[8,512]{1,0:T(8,128)S(1)}, u32[]{:S(2)}, u32[]{:S(2)}) collective-permute-start(f32[8,512]{1,0:T(8,128)S(1)} %get-tuple-element.15), channel_id=1, source_target_pairs={{0,2},{1,3},{8,10},{9,11}} | collective-permute-start | bytes 49160 | tf_op jit(solution)/shard_map/ppermute | solution.py:237
  268.7 27.2 %collective-permute-start.8 = (f32[8,512]{1,0:T(8,128)S(1)}, f32[8,512]{1,0:T(8,128)S(1)}, u32[]{:S(2)}, u32[]{:S(2)}) collective-permute-start(f32[8,512]{1,0:T(8,128)S(1)} %get-tuple-element.13), channel_id=1, source_target_pairs={{0,4},{1,5},{8,12},{9,13}} | collective-permute-start | bytes 49160 | tf_op jit(solution)/shard_map/ppermute | solution.py:237
  296.0 13.2 %collective-permute-start.10 = (f32[8,512]{1,0:T(8,128)S(1)}, f32[8,512]{1,0:T(8,128)S(1)}, u32[]{:S(2)}, u32[]{:S(2)}) collective-permute-start(f32[8,512]{1,0:T(8,128)S(1)} %add_add_fusion), channel_id=1, source_target_pairs={{2,10},{3,11},{4,12},{5,13},{6,14},{7,15},{10,2},{11,3},{12,4},{13... | collective-permute-start | bytes 49160 | tf_op jit(solution)/shard_map/ppermute | solution.py:237
  309.1 178.1 %collective-permute-start.13 = (f32[8,512]{1,0:T(8,128)S(1)}, f32[8,512]{1,0:T(8,128)S(1)}, u32[]{:S(2)}, u32[]{:S(2)}) collective-permute-start(f32[8,512]{1,0:T(8,128)S(1)} %collective-permute-done.10), channel_id=1, source_target_pairs={{6,0},{7,1},{14,8},{15,9}} | collective-permute-start | bytes 49160 | tf_op jit(solution)/shard_map/ppermute | solution.py:237
  310.4 177.5 %collective-permute-start.12 = (f32[8,512]{1,0:T(8,128)S(1)}, f32[8,512]{1,0:T(8,128)S(1)}, u32[]{:S(2)}, u32[]{:S(2)}) collective-permute-start(f32[8,512]{1,0:T(8,128)S(1)} %collective-permute-done.10), channel_id=1, source_target_pairs={{4,0},{5,1},{12,8},{13,9}} | collective-permute-start | bytes 49160 | tf_op jit(solution)/shard_map/ppermute | solution.py:237
  487.3 20.2 %collective-permute-start.6 = (f32[8,1536]{1,0:T(8,128)S(1)}, f32[8,1536]{1,0:T(8,128)S(1)}, u32[]{:S(2)}, u32[]{:S(2)}) collective-permute-start(f32[8,1536]{1,0:T(8,128)S(1)} %get-tuple-element.16), channel_id=1, source_target_pairs={{2,10},{3,11},{4,12},{5,13},{6,14},{7,15},{10,2},{11,3},{12,4},{13... | collective-permute-start | bytes 147464 | tf_op jit(solution)/shard_map/ppermute | solution.py:237
  488.0 19.1 %collective-permute-start.11 = (f32[8,512]{1,0:T(8,128)S(1)}, f32[8,512]{1,0:T(8,128)S(1)}, u32[]{:S(2)}, u32[]{:S(2)}) collective-permute-start(f32[8,512]{1,0:T(8,128)S(1)} %collective-permute-done.10), channel_id=1, source_target_pairs={{2,0},{3,1},{10,8},{11,9}} | collective-permute-start | bytes 49160 | tf_op jit(solution)/shard_map/ppermute | solution.py:237
  507.0 4.6 collective-permute-start.14
  507.5 28.2 %collective-permute-start.15 = (f32[64,3072]{1,0:T(8,128)S(1)}, f32[64,3072]{1,0:T(8,128)S(1)}, u32[]{:S(2)}, u32[]{:S(2)}) collective-permute-start(f32[64,3072]{1,0:T(8,128)S(1)} %slice.56), channel_id=1, source_target_pairs={{0,8},{8,0},{1,9},{9,1},{2,10},{10,2},{3,11},{11,3},{4,12},{12,4},... | collective-permute-start | bytes 2359304 | tf_op jit(solution)/shard_map/ppermute | solution.py:231
  511.7 27.3 %collective-permute-start.16 = (f32[16,3072]{1,0:T(8,128)S(1)}, f32[16,3072]{1,0:T(8,128)S(1)}, u32[]{:S(2)}, u32[]{:S(2)}) collective-permute-start(f32[16,3072]{1,0:T(8,128)S(1)} %slice.58), channel_id=1, source_target_pairs={{0,8},{8,0},{1,9},{9,1},{2,10},{10,2},{3,11},{11,3},{4,12},{12,4},... | collective-permute-start | bytes 589832 | tf_op jit(solution)/shard_map/ppermute | solution.py:231
  535.7 0.9 copy-start.3
  539.7 12.5 %copy-start.1 = (bf16[2048,768]{1,0:T(8,128)(2,1)S(1)}, bf16[2048,768]{1,0:T(8,128)(2,1)}, u32[]{:S(2)}) copy-start(bf16[2048,768]{1,0:T(8,128)(2,1)} %param.11) | copy-start | bytes 9437188

commit v8 on v7

--- a/solution.py
+++ b/solution.py
@@ -19,7 +19,7 @@
     return pl.CostEstimate(flops=flops, bytes_accessed=bytes_accessed, transcendentals=0)
 
 
-def hidden_grads(z, g_rows, w_own, w_other, h_gate, h_up, row_tile=512, col_tile=512):
+def hidden_grads(z, g_rows, w_own, w_other, h_gate, h_up, row_tile=1280, col_tile=512):
     rows, width = g_rows.shape
     half = w_own.shape[0]
     tiles = half // col_tile
@@ -60,7 +60,7 @@
     )(z, g_rows, w_own, w_other, h_gate, h_up)
 
 
-def down_grad(which, h_gate, h_up, g_rows, halves, row_tile=512, col_tile=512):
+def down_grad(which, h_gate, h_up, g_rows, halves, row_tile=1280, col_tile=512):
     rows, cols = h_gate.shape
     width = g_rows.shape[1]
     tiles = cols // halves // col_tile
@@ -95,12 +95,16 @@
     )(which, h_gate, h_up, g_rows)
 
 
-def weight_grad_rhs(which, x_rows, wide, halves, col_tile=512):
+def weight_grad_rhs(which, x_rows, wide, halves, cuts=(), col_tile=1024):
     rows, cols = wide.shape
     part = x_rows.shape[1] // halves
-
-    def kernel(s_ref, l_ref, r_ref, o_ref):
-        o_ref[...] = lax.dot_general(l_ref[...], r_ref[...], (((0,), (0,)), ((), ())), preferred_element_type=F32)
+    cuts = cuts or (0, part)
+    spans = list(zip(cuts, cuts[1:]))
+
+    def kernel(s_ref, l_ref, r_ref, *o_refs):
+        total = lax.dot_general(l_ref[...], r_ref[...], (((0,), (0,)), ((), ())), preferred_element_type=F32)
+        for o_ref, (lo, hi) in zip(o_refs, spans):
+            o_ref[...] = total[lo:hi]
 
     return pl.pallas_call(
         kernel,
@@ -111,15 +115,15 @@
                 pl.BlockSpec((rows, part), lambda j, s_ref: (0, s_ref[0])),
                 pl.BlockSpec((rows, col_tile), lambda j, s_ref: (0, j)),
             ],
-            out_specs=pl.BlockSpec((part, col_tile), lambda j, s_ref: (0, j)),
+            out_specs=[pl.BlockSpec((hi - lo, col_tile), lambda j, s_ref: (0, j)) for lo, hi in spans],
         ),
-        out_shape=jax.ShapeDtypeStruct((part, cols), F32),
+        out_shape=[jax.ShapeDtypeStruct((hi - lo, cols), F32) for lo, hi in spans],
         compiler_params=params('arbitrary'),
         cost_estimate=cost(2 * rows * part * cols, 2 * rows * cols + 4 * part * cols),
     )(which, x_rows, wide)
 
 
-def row_grads(z, dh_gate, dh_up, gate_own, gate_other, up_own, up_other, row_tile=256):
+def row_grads(z, dh_gate, dh_up, gate_own, gate_other, up_own, up_other, row_tile=640):
     rows, cols = dh_gate.shape
     part = gate_own.shape[0]
 
@@ -270,12 +274,11 @@
         part = down_grad(1 - z, h_gate, h_up, g_rows, fs_n)
         recv_down = exchange(part)
         dh_gate, dh_up = hidden_grads(z, g_rows, w_down, other_w_down, h_gate, h_up)
-        part = weight_grad_rhs(1 - z, x_rows, dh_gate, fs_n)
+        part, = weight_grad_rhs(1 - z, x_rows, dh_gate, fs_n)
         recv_gate = exchange(part)
-        send_up = weight_grad_rhs(1 - z, x_rows, dh_up, fs_n)
-        step = send_up.shape[0] // 16
+        step = width // fs_n // 16
         cuts = (0, 12 * step + step // 3, 15 * step, 15 * step + step // 3, 16 * step)
-        piece = [send_up[lo:hi] for lo, hi in zip(cuts, cuts[1:])]
+        piece = weight_grad_rhs(1 - z, x_rows, dh_up, fs_n, cuts)
         half = piece[2].shape[1] // 2
         direct, around = detour(piece[2][:, :half])
         plain = exchange(piece[2][:, half:])
@@ -290,10 +293,10 @@
         grad_gates = jnp.take(back_gate, send_row, mode='fill', fill_value=0).reshape(tok_n, top_n)
 
         grad_w_down = down_grad(z, h_gate, h_up, g_rows, fs_n)
-        grad_w_gate = weight_grad_rhs(z, x_rows, dh_gate, fs_n)
-        grad_w_up = weight_grad_rhs(z, x_rows, dh_up, fs_n)
-        grad_w_down = add_rows(grad_w_down, recv_down, 0, 384)
-        grad_w_gate = add_rows(grad_w_gate, recv_gate, 0, 4 * step)
+        grad_w_gate, = weight_grad_rhs(z, x_rows, dh_gate, fs_n)
+        grad_w_up, = weight_grad_rhs(z, x_rows, dh_up, fs_n)
+        grad_w_down = add_rows(grad_w_down, recv_down, 0, 768)
+        grad_w_gate = add_rows(grad_w_gate, recv_gate, 0, 8 * step)
         tail = grad_w_up[cuts[3]:]
         grad_w_up = add_piece(grad_w_up, recv_up[0], cuts[0])
         grad_w_up = add_piece(grad_w_up, jnp.concatenate([direct + around, plain], axis=1), cuts[2])

time: 555 us -> 550 us (level)
  waiting for transfers between devices: 227 us -> 254 us
  Pallas kernels: 200 us -> 177 us
  local copies, waits for them, and re-layouts: 66 us -> 58.9 us
    ppermute x9, waiting for transfers between devices: 2.6 us -> 18.7 us  [exchange(): return lax.ppermute(value, 'fsdp', swap)]
    ppermute x8, waiting for transfers between devices: 182 us -> 192 us  [send(): lax.ppermute(value, ('fsdp', 'ep'), [(a * ep_n + b, c * ep_n + d) for (a,...]
    pallas_call x2, Pallas kernels: 41.8 us -> 32.4 us  [down_grad(): pl.pallas_call(kernel, grid_spec=pltpu.PrefetchScalarGridSpec(num_scalar_...]
    pallas_call x1, Pallas kernels: 42.2 us -> 33.8 us  [hidden_grads(): pl.pallas_call(kernel, grid_spec=pltpu.PrefetchScalarGridSpec(num_scalar_...]
    slice x3 -> x0, local copies, waits for them, and re-layouts: 6.36 us -> none  [local_backward(): piece = [send_up[lo:hi] for lo, hi in zip(cuts, cuts[1:])]]
  transfers between devices with their start and end apart: 21 -> 21, of which waited for: 5 -> 6; matrix products, arithmetic and copies ran while one was open for 10% -> 9% of each run, Pallas kernels for 35% -> 31%
where the time goes in v8:
time: 550 us; the launch traced here: 548 us
  waiting for transfers between devices  254 us (46%)
  Pallas kernels  177 us (32%)
  local copies, waits for them, and re-layouts  58.9 us (11%)
  starting transfers between devices  43.1 us (8%)
  other arithmetic  15.5 us (3%)
    ppermute x8, waiting for transfers between devices, send(): lax.ppermute(value, ('fsdp', 'ep'), [(a * ep_n + b, c * ep_n + d) for (a,...  192 us
    pallas_call x4, Pallas kernels, weight_grad_rhs(): pl.pallas_call(kernel, grid_spec=pltpu.PrefetchScalarGridSpec(num_scalar_...  47.2 us
    all_to_all x1, waiting for transfers between devices, local_backward(): lax.all_to_all(send_dy, 'ep', 1, 1, tiled=True).reshape(rows_loc, width)  42.5 us
    pallas_call x1, Pallas kernels, row_grads(): pl.pallas_call(kernel, grid_spec=pltpu.PrefetchScalarGridSpec(num_scalar_...  41.5 us
    pallas_call x1, Pallas kernels, hidden_grads(): pl.pallas_call(kernel, grid_spec=pltpu.PrefetchScalarGridSpec(num_scalar_...  33.8 us
    pallas_call x2, Pallas kernels, down_grad(): pl.pallas_call(kernel, grid_spec=pltpu.PrefetchScalarGridSpec(num_scalar_...  32.4 us
    ppermute x9, waiting for transfers between devices, exchange(): return lax.ppermute(value, 'fsdp', swap)  18.7 us
    ppermute x8, starting transfers between devices, send(): lax.ppermute(value, ('fsdp', 'ep'), [(a * ep_n + b, c * ep_n + d) for (a,...  15.5 us
  transfers between devices with their start and end apart: 21, of which 6 were waited for; matrix products, arithmetic and copies ran while one was open for 9% of the time, Pallas kernels for 31%

profile of v8, /device:TPU:0, one launch (start us, length us, event | category | flops | bytes accessed | tf_op | source)
XLA Modules:
  0.0 548.4 jit_solution(5880709845156871385)
XLA Ops:
  0.6 0.0 copy-start
  0.7 0.9 fusion.4
  1.6 8.1 %scatter_custom_fusion = s32[2560]{0:T(1024)S(1)} fusion(s32[2048]{0:T(1024)S(1)} %bitcast.41, s32[2048]{0:T(1024)S(1)} %iota.3, s32[]{:T(128)} %constant.98.clone.1), kind=kCustom, calls=%fused_computation.21 | custom fusion | bytes 10244 | tf_op jit(solution)/shard_map/scatter | solution.py:267
  9.7 13.6 %gather_fusion.1 = f32[2560]{0:T(1024)S(1)} fusion(f32[2048]{0:T(1024)S(1)} %bitcast.25, s32[3072]{0:T(1024)S(1)} %pad_clamp_fusion), kind=kCustom, calls=%fused_computation.1 | custom fusion | bytes 30720 | tf_op jit(solution)/shard_map/jit(_take)/gather | solution.py:269
  23.3 0.7 select_n.72
  24.0 5.4 all-to-all-start.1
  29.5 8.5 %gather_fusion = bf16[2560,768]{1,0:T(8,128)(2,1)} fusion(bf16[2048,768]{1,0:T(8,128)(2,1)S(1)} %copy-done, s32[3072]{0:T(1024)S(1)} %pad_clamp_fusion), kind=kCustom, calls=%fused_computation | custom fusion | bytes 7874560 | tf_op jit(solution)/shard_map/jit(_take)/gather | solution.py:268
  38.0 0.1 broadcast_in_dim.59
  38.0 3.7 broadcast_select_fusion
  41.8 4.7 all-to-all-start
  46.5 1.6 collective-permute-start
  48.1 0.4 collective-permute-start.1
  48.5 1.6 collective-permute-start.2
  50.2 0.1 mul.21
  50.2 42.5 %all-to-all-done = bf16[1,8,320,768]{3,2,0,1:T(8,128)(2,1)} async-done(((bf16[1,8,320,768]{3,2,0,1:T(8,128)(2,1)}), bf16[1,8,320,768]{3,2,0,1:T(8,128)(2,1)}, u32[]{:S(2)}, u32[]{:S(2)}) %all-to-all-start) | async-done | bytes 3932192 | tf_op jit(solution)/shard_map/all_to_all | solution.py:270
  92.8 6.2 %fusion.1 = (f32[2560]{0:T(1024)S(1)}, bf16[2560,768]{1,0:T(8,128)(2,1)}) fusion(bf16[1,2560,768]{2,1,0:T(8,128)(2,1)} %param.18, bf16[1,8,320,768]{3,2,0,1:T(8,128)(2,1)} %all-to-all-done, f32[2560]{0:T(1024)S(1)} %mul.21), kind=kLoop, calls=%fused_computation.8 | loop fusion | flops 11793920 | bytes 11816960 | tf_op jit(solution)/shard_map/rd,rd->r/dot_general | solution.py:288
  98.9 0.7 reshape.103
  99.6 3.3 all-to-all-start.3
  102.9 0.0 collective-permute-done.other_ref
  102.9 33.8 %shard_map.146 = (bf16[2560,3072]{1,0:T(8,128)(2,1)}, bf16[2560,3072]{1,0:T(8,128)(2,1)}) custom-call(s32[1]{0:T(128)} %bitcast.z_ref.s_ref, bf16[2560,768]{1,0:T(8,128)(2,1)} %get-tuple-element.22.g_ref, bf16[1536,768]{1,0:T(8,128)(2,1)} %bitcast.44, bf16[1536,768]{1,0:T(8,128)(2,1)} %collective-permute-done.other_ref, bf16[2560,3072]{1,0:T(8,128)(2,1)} %bitcast.27, ...), custom_call_target="tpu_custom_call" | custom-call | flops 12079595520 | bytes 62914560 | tf_op jit(solution)/shard_map/pallas_call | solution.py:44
  136.8 11.9 %shard_map.149 = f32[384,3072]{1,0:T(8,128)} custom-call(s32[1]{0:T(128)S(6)} %sub.10.s_ref, bf16[2560,768]{1,0:T(8,128)(2,1)} %bitcast.33, bf16[2560,3072]{1,0:T(8,128)(2,1)} %get-tuple-element.11.d1_ref.r_ref), custom_call_target="tpu_custom_call" | custom-call | flops 6039797760 | bytes 20447232 | tf_op jit(solution)/shard_map/pallas_call | solution.py:109
  148.6 1.5 collective-permute-start.3
  150.1 16.2 %shard_map.152 = f32[1536,768]{1,0:T(8,128)} custom-call(s32[1]{0:T(128)S(6)} %sub.10.s_ref, bf16[2560,3072]{1,0:T(8,128)(2,1)} %bitcast.28, bf16[2560,3072]{1,0:T(8,128)(2,1)} %bitcast.31, bf16[2560,768]{1,0:T(8,128)(2,1)} %get-tuple-element.22.g_ref), custom_call_target="tpu_custom_call" | custom-call | flops 6039797760 | bytes 31457280 | tf_op jit(solution)/shard_map/pallas_call | solution.py:84
  166.3 0.6 collective-permute-start.4
  166.9 11.8 %shard_map.155 = (f32[296,3072]{1,0:T(8,128)}, f32[64,3072]{1,0:T(8,128)}, f32[8,3072]{1,0:T(8,128)}, f32[16,3072]{1,0:T(8,128)}) custom-call(s32[1]{0:T(128)S(6)} %sub.10.s_ref, bf16[2560,768]{1,0:T(8,128)(2,1)} %bitcast.34, bf16[2560,3072]{1,0:T(8,128)(2,1)} %get-tuple-element.12.d3_ref.r_ref), custom_call_target="tpu_custom_call" | custom-call | flops 6039797760 | bytes 20447232 | tf_op jit(solution)/shard_map/pallas_call | solution.py:109
  178.6 1.4 collective-permute-start.5
  180.1 0.8 fusion.5
  180.8 0.0 collective-permute-done.1.g1_ref
  180.8 4.9 collective-permute-start.9
  185.7 16.1 %collective-permute-done.2.u1_ref = bf16[384,3072]{1,0:T(8,128)(2,1)} collective-permute-done((bf16[384,3072]{1,0:T(8,128)(2,1)}, bf16[384,3072]{1,0:T(8,128)(2,1)}, u32[]{:S(2)}, u32[]{:S(2)}) %collective-permute-start.2) | collective-permute-done | bytes 2359328 | tf_op jit(solution)/shard_map/ppermute | solution.py:235
  201.9 41.5 %shard_map.147 = bf16[2560,768]{1,0:T(8,128)(2,1)} custom-call(s32[1]{0:T(128)} %bitcast.z_ref.s_ref, bf16[2560,3072]{1,0:T(8,128)(2,1)} %get-tuple-element.11.d1_ref.r_ref, bf16[2560,3072]{1,0:T(8,128)(2,1)} %get-tuple-element.12.d3_ref.r_ref, bf16[384,3072]{1,0:T(8,128)(2,1)} %bitcast.47, bf16[384,3072]{1,0:T(8,128)(2,1)} %collective-permute-done.1.g1_ref, ...), custom_call_target="tpu_custom_call" | custom-call | flops 24159191040 | bytes 62914560 | tf_op jit(solution)/shard_map/pallas_call | solution.py:144
  243.3 4.5 all-to-all-start.2
  247.8 11.8 %shard_map.148.own_ref = f32[384,3072]{1,0:T(8,128)} custom-call(s32[1]{0:T(128)} %bitcast.z_ref.s_ref, bf16[2560,768]{1,0:T(8,128)(2,1)} %bitcast.35, bf16[2560,3072]{1,0:T(8,128)(2,1)} %get-tuple-element.11.d1_ref.r_ref), custom_call_target="tpu_custom_call" | custom-call | flops 6039797760 | bytes 20447232 | tf_op jit(solution)/shard_map/pallas_call | solution.py:109
  259.6 3.8 collective-permute-start.7
  263.5 1.3 collective-permute-start.8
  264.8 16.2 %shard_map.151.own_ref = f32[1536,768]{1,0:T(8,128)} custom-call(s32[1]{0:T(128)} %bitcast.z_ref.s_ref, bf16[2560,3072]{1,0:T(8,128)(2,1)} %bitcast.29, bf16[2560,3072]{1,0:T(8,128)(2,1)} %bitcast.32, bf16[2560,768]{1,0:T(8,128)(2,1)} %get-tuple-element.22.g_ref), custom_call_target="tpu_custom_call" | custom-call | flops 6039797760 | bytes 31457280 | tf_op jit(solution)/shard_map/pallas_call | solution.py:84
  281.0 10.4 %collective-permute-done.7 = f32[8,512]{1,0:T(8,128)S(1)} collective-permute-done((f32[8,512]{1,0:T(8,128)S(1)}, f32[8,512]{1,0:T(8,128)S(1)}, u32[]{:S(2)}, u32[]{:S(2)}) %collective-permute-start.7) | collective-permute-done | bytes 16416 | tf_op jit(solution)/shard_map/ppermute | solution.py:241
  291.4 0.8 collective-permute-start.10
  292.2 11.8 %shard_map.154.own_ref = f32[384,3072]{1,0:T(8,128)} custom-call(s32[1]{0:T(128)} %bitcast.z_ref.s_ref, bf16[2560,768]{1,0:T(8,128)(2,1)} %bitcast.36, bf16[2560,3072]{1,0:T(8,128)(2,1)} %get-tuple-element.12.d3_ref.r_ref), custom_call_target="tpu_custom_call" | custom-call | flops 6039797760 | bytes 20447232 | tf_op jit(solution)/shard_map/pallas_call | solution.py:109
  304.0 1.3 collective-permute-start.13
  305.3 1.3 collective-permute-start.12
  306.6 0.9 slice.35.tail_ref
  307.6 0.1 reshape.104
  307.7 11.8 %gather_fusion.3 = f32[2048]{0:T(1024)S(1)} fusion(f32[2560]{0:T(1024)S(1)} %reshape.104, s32[2048]{0:T(1024)S(1)} %broadcast_clamp_fusion), kind=kCustom, calls=%fused_computation.3 | custom fusion | bytes 24576 | tf_op jit(solution)/shard_map/jit(_take)/gather | solution.py:293
  319.5 167.8 %collective-permute-done.13 = f32[8,512]{1,0:T(8,128)S(1)} collective-permute-done((f32[8,512]{1,0:T(8,128)S(1)}, f32[8,512]{1,0:T(8,128)S(1)}, u32[]{:S(2)}, u32[]{:S(2)}) %collective-permute-start.13) | collective-permute-done | bytes 16416 | tf_op jit(solution)/shard_map/ppermute | solution.py:241
  487.3 0.7 collective-permute-start.6
  488.0 1.5 collective-permute-start.11
  489.5 0.6 broadcast_select_fusion.3
  490.1 14.0 %collective-permute-done.11 = f32[8,512]{1,0:T(8,128)S(1)} collective-permute-done((f32[8,512]{1,0:T(8,128)S(1)}, f32[8,512]{1,0:T(8,128)S(1)}, u32[]{:S(2)}, u32[]{:S(2)}) %collective-permute-start.11) | collective-permute-done | bytes 16416 | tf_op jit(solution)/shard_map/ppermute | solution.py:241
  504.1 0.4 collective-permute-start.14
  504.6 1.6 collective-permute-start.15
  506.1 2.6 collective-permute-done.14
  508.7 0.4 collective-permute-start.16
  509.2 0.6 pad_maximum_fusion.recv_ref
  509.8 12.7 %gather_fusion.2 = bf16[2048,768]{1,0:T(8,128)(2,1)} fusion(bf16[2560,768]{1,0:T(8,128)(2,1)} %bitcast.13, s32[2048]{0:T(1024)S(1)} %broadcast_clamp_fusion), kind=kCustom, calls=%fused_computation.2 | custom fusion | bytes 6299648 | tf_op jit(solution)/shard_map/jit(_take)/gather | solution.py:291
  522.5 5.4 shard_map.156.own_ref
  527.9 3.3 broadcast_select_fusion.1
  531.1 1.6 shard_map.157.own_ref
  532.8 0.9 copy-done.3
  533.7 2.4 shard_map.158.own_ref
  536.0 0.7 shard_map.159
  536.8 0.0 copy-start.1
  536.8 5.9 %shard_map.150 = f32[384,3072]{1,0:T(8,128)} custom-call(f32[384,3072]{1,0:T(8,128)} %shard_map.148.own_ref, f32[384,3072]{1,0:T(8,128)} %collective-permute-done.3.recv_ref), custom_call_target="tpu_custom_call", output_to_operand_aliasing={{}: (0, {})} | custom-call | flops 1179648 | bytes 14155776 | tf_op jit(solution)/shard_map/pallas_call | solution.py:165
  542.7 5.8 %shard_map.153 = f32[1536,768]{1,0:T(8,128)} custom-call(f32[1536,768]{1,0:T(8,128)} %shard_map.151.own_ref, f32[1536,768]{1,0:T(8,128)} %collective-permute-done.4.recv_ref), custom_call_target="tpu_custom_call", output_to_operand_aliasing={{}: (0, {})} | custom-call | flops 1179648 | bytes 14155776 | tf_op jit(solution)/shard_map/pallas_call | solution.py:165
  (36 shorter events, 0.2 us)
Async XLA Ops:
  0.6 28.8 %copy-start = (bf16[2048,768]{1,0:T(8,128)(2,1)S(1)}, bf16[2048,768]{1,0:T(8,128)(2,1)}, u32[]{:S(2)}) copy-start(bf16[2048,768]{1,0:T(8,128)(2,1)} %param.11) | copy-start | bytes 9437188
  0.6 9.0 %copy-start.2 = (f32[2048,1]{0,1:T(1,128)S(1)}, f32[2048,1]{0,1:T(1,128)}, u32[]{:S(2)}) copy-start(f32[2048,1]{0,1:T(1,128)} %param.14) | copy-start | bytes 24580
  24.0 17.8 %all-to-all-start.1 = ((f32[1,8,320]{2,0,1:T(1,128)}), f32[1,8,320]{2,0,1:T(1,128)S(1)}, u32[]{:S(2)}, u32[]{:S(2)}) async-start(f32[1,8,320]{2,0,1:T(1,128)} %select_n.72), calls=%async_computation.1 | async-start | bytes 24576 | tf_op jit(solution)/shard_map/all_to_all | solution.py:271
  41.8 4.7 copy-start.5
  41.8 51.0 %all-to-all-start = ((bf16[1,8,320,768]{3,2,0,1:T(8,128)(2,1)}), bf16[1,8,320,768]{3,2,0,1:T(8,128)(2,1)}, u32[]{:S(2)}, u32[]{:S(2)}) async-start(bf16[1,8,320,768]{3,2,0,1:T(8,128)(2,1)} %broadcast_select_fusion), calls=%async_computation | async-start | bytes 7864320 | tf_op jit(solution)/shard_map/all_to_all | solution.py:270
  46.5 56.5 %collective-permute-start = (bf16[1536,768]{1,0:T(8,128)(2,1)S(1)}, bf16[1536,768]{1,0:T(8,128)(2,1)}, u32[]{:S(2)}, u32[]{:S(2)}) collective-permute-start(bf16[1536,768]{1,0:T(8,128)(2,1)S(1)} %bitcast.45), channel_id=1, source_target_pairs={{0,8},{8,0},{1,9},{9,1},{2,10},{10,2},{3,11},{11,3},{4,12},{12,4},... | collective-permute-start | bytes 7077896 | tf_op jit(solution)/shard_map/ppermute | solution.py:235
  48.1 132.7 %collective-permute-start.1 = (bf16[384,3072]{1,0:T(8,128)(2,1)}, bf16[384,3072]{1,0:T(8,128)(2,1)}, u32[]{:S(2)}, u32[]{:S(2)}) collective-permute-start(bf16[384,3072]{1,0:T(8,128)(2,1)} %bitcast.46), channel_id=1, source_target_pairs={{0,8},{8,0},{1,9},{9,1},{2,10},{10,2},{3,11},{11,3},{4,12},{12,4},... | collective-permute-start | bytes 7077896 | tf_op jit(solution)/shard_map/ppermute | solution.py:235
  48.5 153.3 %collective-permute-start.2 = (bf16[384,3072]{1,0:T(8,128)(2,1)}, bf16[384,3072]{1,0:T(8,128)(2,1)}, u32[]{:S(2)}, u32[]{:S(2)}) collective-permute-start(bf16[384,3072]{1,0:T(8,128)(2,1)} %bitcast.48), channel_id=1, source_target_pairs={{0,8},{8,0},{1,9},{9,1},{2,10},{10,2},{3,11},{11,3},{4,12},{12,4},... | collective-permute-start | bytes 7077896 | tf_op jit(solution)/shard_map/ppermute | solution.py:235
  99.6 143.7 %all-to-all-start.3 = ((f32[1,8,320]{2,0,1:T(1,128)}), f32[1,8,320]{2,0,1:T(1,128)S(1)}, u32[]{:S(2)}, u32[]{:S(2)}) async-start(f32[1,8,320]{2,0,1:T(1,128)} %reshape.103), calls=%async_computation.3 | async-start | bytes 24576 | tf_op jit(solution)/shard_map/all_to_all | solution.py:290
  148.6 388.1 %collective-permute-start.3 = (f32[384,3072]{1,0:T(8,128)}, f32[384,3072]{1,0:T(8,128)}, u32[]{:S(2)}, u32[]{:S(2)}) collective-permute-start(f32[384,3072]{1,0:T(8,128)} %shard_map.149), channel_id=1, source_target_pairs={{0,8},{8,0},{1,9},{9,1},{2,10},{10,2},{3,11},{11,3},{4,12},{12,4},... | collective-permute-start | bytes 14155784 | tf_op jit(solution)/shard_map/ppermute | solution.py:235
  166.3 376.4 %collective-permute-start.4 = (f32[1536,768]{1,0:T(8,128)}, f32[1536,768]{1,0:T(8,128)}, u32[]{:S(2)}, u32[]{:S(2)}) collective-permute-start(f32[1536,768]{1,0:T(8,128)} %shard_map.152), channel_id=1, source_target_pairs={{0,8},{8,0},{1,9},{9,1},{2,10},{10,2},{3,11},{11,3},{4,12},{12,4},... | collective-permute-start | bytes 14155784 | tf_op jit(solution)/shard_map/ppermute | solution.py:235
  178.6 343.9 %collective-permute-start.5 = (f32[296,3072]{1,0:T(8,128)}, f32[296,3072]{1,0:T(8,128)}, u32[]{:S(2)}, u32[]{:S(2)}) collective-permute-start(f32[296,3072]{1,0:T(8,128)} %get-tuple-element.13), channel_id=1, source_target_pairs={{0,8},{8,0},{1,9},{9,1},{2,10},{10,2},{3,11},{11,3},{4,12},{12,4},... | collective-permute-start | bytes 10911752 | tf_op jit(solution)/shard_map/ppermute | solution.py:235
  180.8 82.6 %collective-permute-start.9 = (f32[8,512]{1,0:T(8,128)S(1)}, f32[8,512]{1,0:T(8,128)S(1)}, u32[]{:S(2)}, u32[]{:S(2)}) collective-permute-start(f32[8,512]{1,0:T(8,128)S(1)} %get-tuple-element.24), channel_id=1, source_target_pairs={{0,6},{1,7},{8,14},{9,15}} | collective-permute-start | bytes 49160 | tf_op jit(solution)/shard_map/ppermute | solution.py:241
  243.3 266.5 %all-to-all-start.2 = ((bf16[1,8,320,768]{3,2,0,1:T(8,128)(2,1)}), bf16[1,8,320,768]{3,2,0,1:T(8,128)(2,1)}, u32[]{:S(2)}, u32[]{:S(2)}) async-start(bf16[1,8,320,768]{3,2,0,1:T(8,128)(2,1)} %bitcast.40), calls=%async_computation.2 | async-start | bytes 7864320 | tf_op jit(solution)/shard_map/all_to_all | solution.py:289
  259.6 31.7 %collective-permute-start.7 = (f32[8,512]{1,0:T(8,128)S(1)}, f32[8,512]{1,0:T(8,128)S(1)}, u32[]{:S(2)}, u32[]{:S(2)}) collective-permute-start(f32[8,512]{1,0:T(8,128)S(1)} %get-tuple-element.25), channel_id=1, source_target_pairs={{0,2},{1,3},{8,10},{9,11}} | collective-permute-start | bytes 49160 | tf_op jit(solution)/shard_map/ppermute | solution.py:241
  263.5 27.9 %collective-permute-start.8 = (f32[8,512]{1,0:T(8,128)S(1)}, f32[8,512]{1,0:T(8,128)S(1)}, u32[]{:S(2)}, u32[]{:S(2)}) collective-permute-start(f32[8,512]{1,0:T(8,128)S(1)} %get-tuple-element.23), channel_id=1, source_target_pairs={{0,4},{1,5},{8,12},{9,13}} | collective-permute-start | bytes 49160 | tf_op jit(solution)/shard_map/ppermute | solution.py:241
  291.4 15.2 %copy-start.4 = (f32[8,3072]{1,0:T(8,128)S(1)}, f32[8,3072]{1,0:T(8,128)}, u32[]{:S(2)}) copy-start(f32[8,3072]{1,0:T(8,128)} %get-tuple-element.14) | copy-start | bytes 294916
  291.4 12.6 %collective-permute-start.10 = (f32[8,512]{1,0:T(8,128)S(1)}, f32[8,512]{1,0:T(8,128)S(1)}, u32[]{:S(2)}, u32[]{:S(2)}) collective-permute-start(f32[8,512]{1,0:T(8,128)S(1)} %add_add_fusion), channel_id=1, source_target_pairs={{2,10},{3,11},{4,12},{5,13},{6,14},{7,15},{10,2},{11,3},{12,4},{13... | collective-permute-start | bytes 49160 | tf_op jit(solution)/shard_map/ppermute | solution.py:241
  304.0 183.3 %collective-permute-start.13 = (f32[8,512]{1,0:T(8,128)S(1)}, f32[8,512]{1,0:T(8,128)S(1)}, u32[]{:S(2)}, u32[]{:S(2)}) collective-permute-start(f32[8,512]{1,0:T(8,128)S(1)} %collective-permute-done.10), channel_id=1, source_target_pairs={{6,0},{7,1},{14,8},{15,9}} | collective-permute-start | bytes 49160 | tf_op jit(solution)/shard_map/ppermute | solution.py:241
  305.3 182.6 %collective-permute-start.12 = (f32[8,512]{1,0:T(8,128)S(1)}, f32[8,512]{1,0:T(8,128)S(1)}, u32[]{:S(2)}, u32[]{:S(2)}) collective-permute-start(f32[8,512]{1,0:T(8,128)S(1)} %collective-permute-done.10), channel_id=1, source_target_pairs={{4,0},{5,1},{12,8},{13,9}} | collective-permute-start | bytes 49160 | tf_op jit(solution)/shard_map/ppermute | solution.py:241
  307.7 196.9 %copy-start.6 = (f32[64,3072]{1,0:T(8,128)S(1)}, f32[64,3072]{1,0:T(8,128)}, u32[]{:S(2)}) copy-start(f32[64,3072]{1,0:T(8,128)} %get-tuple-element.15) | copy-start | bytes 2359300
  307.7 201.0 %copy-start.7 = (f32[16,3072]{1,0:T(8,128)S(1)}, f32[16,3072]{1,0:T(8,128)}, u32[]{:S(2)}) copy-start(f32[16,3072]{1,0:T(8,128)} %get-tuple-element.16) | copy-start | bytes 589828
  487.3 17.3 %collective-permute-start.6 = (f32[8,1536]{1,0:T(8,128)S(1)}, f32[8,1536]{1,0:T(8,128)S(1)}, u32[]{:S(2)}, u32[]{:S(2)}) collective-permute-start(f32[8,1536]{1,0:T(8,128)S(1)} %get-tuple-element.26), channel_id=1, source_target_pairs={{2,10},{3,11},{4,12},{5,13},{6,14},{7,15},{10,2},{11,3},{12,4},{13... | collective-permute-start | bytes 147464 | tf_op jit(solution)/shard_map/ppermute | solution.py:241
  488.0 16.1 %collective-permute-start.11 = (f32[8,512]{1,0:T(8,128)S(1)}, f32[8,512]{1,0:T(8,128)S(1)}, u32[]{:S(2)}, u32[]{:S(2)}) collective-permute-start(f32[8,512]{1,0:T(8,128)S(1)} %collective-permute-done.10), channel_id=1, source_target_pairs={{2,0},{3,1},{10,8},{11,9}} | collective-permute-start | bytes 49160 | tf_op jit(solution)/shard_map/ppermute | solution.py:241
  504.1 4.6 collective-permute-start.14
  504.6 28.2 %collective-permute-start.15 = (f32[64,3072]{1,0:T(8,128)S(1)}, f32[64,3072]{1,0:T(8,128)S(1)}, u32[]{:S(2)}, u32[]{:S(2)}) collective-permute-start(f32[64,3072]{1,0:T(8,128)S(1)} %copy-done.6), channel_id=1, source_target_pairs={{0,8},{8,0},{1,9},{9,1},{2,10},{10,2},{3,11},{11,3},{4,12},{12,4},... | collective-permute-start | bytes 2359304 | tf_op jit(solution)/shard_map/ppermute | solution.py:235
  508.7 27.3 %collective-permute-start.16 = (f32[16,3072]{1,0:T(8,128)S(1)}, f32[16,3072]{1,0:T(8,128)S(1)}, u32[]{:S(2)}, u32[]{:S(2)}) collective-permute-start(f32[16,3072]{1,0:T(8,128)S(1)} %copy-done.7), channel_id=1, source_target_pairs={{0,8},{8,0},{1,9},{9,1},{2,10},{10,2},{3,11},{11,3},{4,12},{12,4},... | collective-permute-start | bytes 589832 | tf_op jit(solution)/shard_map/ppermute | solution.py:235
  532.8 0.9 copy-start.3
  536.8 11.7 %copy-start.1 = (bf16[2048,768]{1,0:T(8,128)(2,1)S(1)}, bf16[2048,768]{1,0:T(8,128)(2,1)}, u32[]{:S(2)}) copy-start(bf16[2048,768]{1,0:T(8,128)(2,1)} %param.11) | copy-start | bytes 9437188

commit v9 on v8

--- a/solution.py
+++ b/solution.py
@@ -60,12 +60,15 @@
     )(z, g_rows, w_own, w_other, h_gate, h_up)
 
 
-def down_grad(which, h_gate, h_up, g_rows, halves, row_tile=1280, col_tile=512):
+def down_grad(which, h_gate, h_up, g_rows, halves, recv=None, row_tile=1280, col_tile=512):
     rows, cols = h_gate.shape
     width = g_rows.shape[1]
     tiles = cols // halves // col_tile
-
-    def kernel(s_ref, h1_ref, h3_ref, g_ref, o_ref):
+    steps = rows // row_tile
+    extra = [] if recv is None else [recv]
+
+    def kernel(s_ref, h1_ref, h3_ref, g_ref, *refs):
+        o_ref = refs[-1]
         i = pl.program_id(1)
         h1 = h1_ref[...].astype(F32)
         act = (h1 * jax.nn.sigmoid(h1) * h3_ref[...].astype(F32)).astype(BF16)
@@ -80,31 +83,41 @@
         def _():
             o_ref[...] += term
 
+        if extra:
+            @pl.when(i == steps - 1)
+            def _():
+                o_ref[...] += refs[0][...]
+
+    out_tile = pl.BlockSpec((col_tile, width), lambda j, i, s_ref: (j, 0))
     tile = pl.BlockSpec((row_tile, col_tile), lambda j, i, s_ref: (i, s_ref[0] * tiles + j))
     return pl.pallas_call(
         kernel,
         grid_spec=pltpu.PrefetchScalarGridSpec(
             num_scalar_prefetch=1,
-            grid=(tiles, rows // row_tile),
-            in_specs=[tile, tile, pl.BlockSpec((rows, width), lambda j, i, s_ref: (0, 0))],
-            out_specs=pl.BlockSpec((col_tile, width), lambda j, i, s_ref: (j, 0)),
+            grid=(tiles, steps),
+            in_specs=[tile, tile, pl.BlockSpec((rows, width), lambda j, i, s_ref: (0, 0))] + [out_tile] * len(extra),
+            out_specs=out_tile,
         ),
         out_shape=jax.ShapeDtypeStruct((tiles * col_tile, width), F32),
         compiler_params=params('arbitrary', 'arbitrary'),
         cost_estimate=cost(2 * rows * width * tiles * col_tile, 4 * rows * cols),
-    )(which, h_gate, h_up, g_rows)
-
-
-def weight_grad_rhs(which, x_rows, wide, halves, cuts=(), col_tile=1024):
+    )(which, h_gate, h_up, g_rows, *extra)
+
+
+def weight_grad_rhs(which, x_rows, wide, halves, cuts=(), recv=None, col_tile=1024):
     rows, cols = wide.shape
     part = x_rows.shape[1] // halves
     cuts = cuts or (0, part)
     spans = list(zip(cuts, cuts[1:]))
-
-    def kernel(s_ref, l_ref, r_ref, *o_refs):
+    extra = [] if recv is None else [recv]
+
+    def kernel(s_ref, l_ref, r_ref, *refs):
+        o_refs = refs[len(extra):]
         total = lax.dot_general(l_ref[...], r_ref[...], (((0,), (0,)), ((), ())), preferred_element_type=F32)
         for o_ref, (lo, hi) in zip(o_refs, spans):
             o_ref[...] = total[lo:hi]
+        if extra:
+            o_refs[0][:recv.shape[0], :] += refs[0][...]
 
     return pl.pallas_call(
         kernel,
@@ -114,13 +127,13 @@
             in_specs=[
                 pl.BlockSpec((rows, part), lambda j, s_ref: (0, s_ref[0])),
                 pl.BlockSpec((rows, col_tile), lambda j, s_ref: (0, j)),
-            ],
+            ] + [pl.BlockSpec((v.shape[0], col_tile), lambda j, s_ref: (0, j)) for v in extra],
             out_specs=[pl.BlockSpec((hi - lo, col_tile), lambda j, s_ref: (0, j)) for lo, hi in spans],
         ),
         out_shape=[jax.ShapeDtypeStruct((hi - lo, cols), F32) for lo, hi in spans],
         compiler_params=params('arbitrary'),
         cost_estimate=cost(2 * rows * part * cols, 2 * rows * cols + 4 * part * cols),
-    )(which, x_rows, wide)
+    )(which, x_rows, wide, *extra)
 
 
 def row_grads(z, dh_gate, dh_up, gate_own, gate_other, up_own, up_other, row_tile=640):
@@ -153,25 +166,6 @@
         compiler_params=params('arbitrary', 'arbitrary'),
         cost_estimate=cost(8 * rows * cols * part, 8 * rows * cols),
     )(z, dh_gate, dh_up, gate_own, gate_other, up_own, up_other)
-
-
-def add_rows(own, recv, first, tile):
-    rows, width = recv.shape
-    base = first // tile
-
-    def kernel(own_ref, recv_ref, o_ref):
-        o_ref[...] = own_ref[...] + recv_ref[...]
-
-    return pl.pallas_call(
-        kernel,
-        grid=(rows // tile,),
-        in_specs=[pl.BlockSpec((tile, width), lambda i: (base + i, 0)), pl.BlockSpec((tile, width), lambda i: (i, 0))],
-        out_specs=pl.BlockSpec((tile, width), lambda i: (base + i, 0)),
-        out_shape=jax.ShapeDtypeStruct(own.shape, own.dtype),
-        input_output_aliases={0: 0},
-        compiler_params=params('arbitrary'),
-        cost_estimate=cost(rows * width, 12 * rows * width),
-    )(own, recv)
 
 
 def add_piece(own, recv, first):
@@ -265,7 +259,7 @@
 
         send_row = jnp.where(slot_pos >= 0, ((expert_idx % e_loc) * ep_n + expert_idx // e_loc) * slot_cap + slot_pos, slots_n).reshape(-1)
         src_choice = jnp.full((slots_n,), choices, jnp.int32).at[send_row].set(jnp.arange(choices, dtype=jnp.int32), mode='drop')
-        send_dy = jnp.take(grad_out, src_choice // top_n, axis=0, mode='fill', fill_value=0).reshape(e_loc, ep_n, slot_cap, width)
+        send_dy = jnp.take(grad_out, src_choice // top_n, axis=0, mode='clip').reshape(e_loc, ep_n, slot_cap, width)
         send_gate = jnp.take(gates.reshape(-1), src_choice, mode='fill', fill_value=0).reshape(e_loc, ep_n, slot_cap)
         dy_rows = lax.all_to_all(send_dy, 'ep', 1, 1, tiled=True).reshape(rows_loc, width)
         gate_rows = lax.all_to_all(send_gate, 'ep', 1, 1, tiled=True).reshape(rows_loc)
@@ -277,7 +271,7 @@
         part, = weight_grad_rhs(1 - z, x_rows, dh_gate, fs_n)
         recv_gate = exchange(part)
         step = width // fs_n // 16
-        cuts = (0, 12 * step + step // 3, 15 * step, 15 * step + step // 3, 16 * step)
+        cuts = (0, 11 * step + step // 3, 15 * step, 15 * step + step // 3, 16 * step)
         piece = weight_grad_rhs(1 - z, x_rows, dh_up, fs_n, cuts)
         half = piece[2].shape[1] // 2
         direct, around = detour(piece[2][:, :half])
@@ -292,13 +286,10 @@
         grad_x = jnp.sum(picked.astype(F32), axis=1).astype(BF16)
         grad_gates = jnp.take(back_gate, send_row, mode='fill', fill_value=0).reshape(tok_n, top_n)
 
-        grad_w_down = down_grad(z, h_gate, h_up, g_rows, fs_n)
-        grad_w_gate, = weight_grad_rhs(z, x_rows, dh_gate, fs_n)
-        grad_w_up, = weight_grad_rhs(z, x_rows, dh_up, fs_n)
-        grad_w_down = add_rows(grad_w_down, recv_down, 0, 768)
-        grad_w_gate = add_rows(grad_w_gate, recv_gate, 0, 8 * step)
+        grad_w_down = down_grad(z, h_gate, h_up, g_rows, fs_n, recv_down)
+        grad_w_gate, = weight_grad_rhs(z, x_rows, dh_gate, fs_n, recv=recv_gate)
+        grad_w_up, = weight_grad_rhs(z, x_rows, dh_up, fs_n, recv=recv_up[0])
         tail = grad_w_up[cuts[3]:]
-        grad_w_up = add_piece(grad_w_up, recv_up[0], cuts[0])
         grad_w_up = add_piece(grad_w_up, jnp.concatenate([direct + around, plain], axis=1), cuts[2])
         grad_w_up = add_piece(grad_w_up, recv_up[1], cuts[1])
         grad_w_up = add_last(grad_w_up, tail, recv_up[-1])

time: 550 us -> 569 us (1.035)
  waiting for transfers between devices: 254 us -> 294 us
  Pallas kernels: 177 us -> 164 us
    ppermute x8, waiting for transfers between devices: 192 us -> 222 us  [send(): lax.ppermute(value, ('fsdp', 'ep'), [(a * ep_n + b, c * ep_n + d) for (a,...]
    pallas_call x2 -> x0, Pallas kernels: 11.6 us -> none  [add_rows(): pl.pallas_call(kernel, grid=(rows // tile,), in_specs=[pl.BlockSpec((tile...]
    ppermute x9, waiting for transfers between devices: 18.7 us -> 29.5 us  [exchange(): return lax.ppermute(value, 'fsdp', swap)]
  transfers between devices with their start and end apart: 21 -> 21, of which waited for: 6 -> 7; matrix products, arithmetic and copies ran while one was open for 9% -> 7% of each run, Pallas kernels for 31% -> 26%
where the time goes in v9:
time: 569 us; the launch traced here: 568 us
  waiting for transfers between devices  294 us (52%)
  Pallas kernels  164 us (29%)
  local copies, waits for them, and re-layouts  56.5 us (10%)
  starting transfers between devices  41.8 us (7%)
  other arithmetic  10.3 us (2%)
    ppermute x8, waiting for transfers between devices, send(): lax.ppermute(value, ('fsdp', 'ep'), [(a * ep_n + b, c * ep_n + d) for (a,...  222 us
    pallas_call x4, Pallas kernels, weight_grad_rhs(): pl.pallas_call(kernel, grid_spec=pltpu.PrefetchScalarGridSpec(num_scalar_...  49.8 us
    all_to_all x1, waiting for transfers between devices, local_backward(): lax.all_to_all(send_dy, 'ep', 1, 1, tiled=True).reshape(rows_loc, width)  42.5 us
    pallas_call x1, Pallas kernels, row_grads(): pl.pallas_call(kernel, grid_spec=pltpu.PrefetchScalarGridSpec(num_scalar_...  41.3 us
    pallas_call x2, Pallas kernels, down_grad(): pl.pallas_call(kernel, grid_spec=pltpu.PrefetchScalarGridSpec(num_scalar_...  33.9 us
    pallas_call x1, Pallas kernels, hidden_grads(): pl.pallas_call(kernel, grid_spec=pltpu.PrefetchScalarGridSpec(num_scalar_...  33.8 us
    ppermute x9, waiting for transfers between devices, exchange(): return lax.ppermute(value, 'fsdp', swap)  29.5 us
    gather x1, local copies, waits for them, and re-layouts, local_backward(): jnp.take(gates.reshape(-1), src_choice, mode='fill', fill_value=0)  13.6 us
  transfers between devices with their start and end apart: 21, of which 7 were waited for; matrix products, arithmetic and copies ran while one was open for 7% of the time, Pallas kernels for 26%

profile of v9, /device:TPU:0, one launch (start us, length us, event | category | flops | bytes accessed | tf_op | source)
XLA Modules:
  0.0 567.7 jit_solution(2812465493481715124)
XLA Ops:
  0.6 0.0 copy-start
  0.7 0.9 fusion.4
  1.6 8.1 %scatter_custom_fusion = s32[2560]{0:T(1024)S(1)} fusion(s32[2048]{0:T(1024)S(1)} %bitcast.41, s32[2048]{0:T(1024)S(1)} %iota.3, s32[]{:T(128)} %constant.86.clone.1), kind=kCustom, calls=%fused_computation.20 | custom fusion | bytes 10244 | tf_op jit(solution)/shard_map/scatter | solution.py:261
  9.7 13.6 %gather_fusion.1 = f32[2560]{0:T(1024)S(1)} fusion(f32[2048]{0:T(1024)S(1)} %bitcast.25, s32[3072]{0:T(1024)S(1)} %pad_clamp_fusion), kind=kCustom, calls=%fused_computation.1 | custom fusion | bytes 30720 | tf_op jit(solution)/shard_map/jit(_take)/gather | solution.py:263
  23.3 0.7 select_n.58
  24.0 5.4 all-to-all-start.1
  29.5 8.5 %gather_fusion = bf16[2560,768]{1,0:T(8,128)(2,1)} fusion(bf16[2048,768]{1,0:T(8,128)(2,1)S(1)} %copy-done, s32[3072]{0:T(1024)S(1)} %pad_clamp_fusion.1), kind=kCustom, calls=%fused_computation | custom fusion | bytes 7874560 | tf_op jit(solution)/shard_map/jit(_take)/gather | solution.py:262
  38.0 0.0 all-to-all-done.1
  38.0 4.7 all-to-all-start
  42.7 1.6 collective-permute-start
  44.3 0.4 collective-permute-start.1
  44.7 1.6 collective-permute-start.2
  46.3 0.1 mul.21
  46.4 42.5 %all-to-all-done = bf16[1,8,320,768]{3,2,0,1:T(8,128)(2,1)} async-done(((bf16[1,8,320,768]{3,2,0,1:T(8,128)(2,1)}), bf16[1,8,320,768]{3,2,0,1:T(8,128)(2,1)}, u32[]{:S(2)}, u32[]{:S(2)}) %all-to-all-start) | async-done | bytes 3932192 | tf_op jit(solution)/shard_map/all_to_all | solution.py:264
  88.9 6.1 %fusion.1 = (f32[2560]{0:T(1024)S(1)}, bf16[2560,768]{1,0:T(8,128)(2,1)}) fusion(bf16[1,2560,768]{2,1,0:T(8,128)(2,1)} %param.18, bf16[1,8,320,768]{3,2,0,1:T(8,128)(2,1)} %all-to-all-done, f32[2560]{0:T(1024)S(1)} %mul.21), kind=kLoop, calls=%fused_computation.8 | loop fusion | flops 11793920 | bytes 11816960 | tf_op jit(solution)/shard_map/rd,rd->r/dot_general | solution.py:282
  95.1 0.7 reshape.84
  95.8 3.5 all-to-all-start.3
  99.3 0.0 collective-permute-done.other_ref
  99.3 33.8 %shard_map.146 = (bf16[2560,3072]{1,0:T(8,128)(2,1)}, bf16[2560,3072]{1,0:T(8,128)(2,1)}) custom-call(s32[1]{0:T(128)} %bitcast.z_ref.s_ref, bf16[2560,768]{1,0:T(8,128)(2,1)} %get-tuple-element.20.g_ref, bf16[1536,768]{1,0:T(8,128)(2,1)} %bitcast.44, bf16[1536,768]{1,0:T(8,128)(2,1)} %collective-permute-done.other_ref, bf16[2560,3072]{1,0:T(8,128)(2,1)} %bitcast.27, ...), custom_call_target="tpu_custom_call" | custom-call | flops 12079595520 | bytes 62914560 | tf_op jit(solution)/shard_map/pallas_call | solution.py:44
  133.1 11.8 %shard_map.148 = f32[384,3072]{1,0:T(8,128)} custom-call(s32[1]{0:T(128)S(6)} %sub.10.s_ref, bf16[2560,768]{1,0:T(8,128)(2,1)} %bitcast.33, bf16[2560,3072]{1,0:T(8,128)(2,1)} %get-tuple-element.11.d1_ref.r_ref), custom_call_target="tpu_custom_call" | custom-call | flops 6039797760 | bytes 20447232 | tf_op jit(solution)/shard_map/pallas_call | solution.py:122
  144.9 1.5 collective-permute-start.3
  146.4 16.2 %shard_map.150 = f32[1536,768]{1,0:T(8,128)} custom-call(s32[1]{0:T(128)S(6)} %sub.10.s_ref, bf16[2560,3072]{1,0:T(8,128)(2,1)} %bitcast.28, bf16[2560,3072]{1,0:T(8,128)(2,1)} %bitcast.31, bf16[2560,768]{1,0:T(8,128)(2,1)} %get-tuple-element.20.g_ref), custom_call_target="tpu_custom_call" | custom-call | flops 6039797760 | bytes 31457280 | tf_op jit(solution)/shard_map/pallas_call | solution.py:93
  162.6 0.5 collective-permute-start.4
  163.1 11.7 %shard_map.152 = (f32[272,3072]{1,0:T(8,128)}, f32[88,3072]{1,0:T(8,128)}, f32[8,3072]{1,0:T(8,128)}, f32[16,3072]{1,0:T(8,128)}) custom-call(s32[1]{0:T(128)S(6)} %sub.10.s_ref, bf16[2560,768]{1,0:T(8,128)(2,1)} %bitcast.34, bf16[2560,3072]{1,0:T(8,128)(2,1)} %get-tuple-element.12.d3_ref.r_ref), custom_call_target="tpu_custom_call" | custom-call | flops 6039797760 | bytes 20447232 | tf_op jit(solution)/shard_map/pallas_call | solution.py:122
  174.8 1.5 collective-permute-start.5
  176.3 0.0 collective-permute-done.1.g1_ref
  176.3 21.7 %collective-permute-done.2.u1_ref = bf16[384,3072]{1,0:T(8,128)(2,1)} collective-permute-done((bf16[384,3072]{1,0:T(8,128)(2,1)}, bf16[384,3072]{1,0:T(8,128)(2,1)}, u32[]{:S(2)}, u32[]{:S(2)}) %collective-permute-start.2) | collective-permute-done | bytes 2359328 | tf_op jit(solution)/shard_map/ppermute | solution.py:229
  198.0 41.3 %shard_map.147 = bf16[2560,768]{1,0:T(8,128)(2,1)} custom-call(s32[1]{0:T(128)} %bitcast.z_ref.s_ref, bf16[2560,3072]{1,0:T(8,128)(2,1)} %get-tuple-element.11.d1_ref.r_ref, bf16[2560,3072]{1,0:T(8,128)(2,1)} %get-tuple-element.12.d3_ref.r_ref, bf16[384,3072]{1,0:T(8,128)(2,1)} %bitcast.47, bf16[384,3072]{1,0:T(8,128)(2,1)} %collective-permute-done.1.g1_ref, ...), custom_call_target="tpu_custom_call" | custom-call | flops 24159191040 | bytes 62914560 | tf_op jit(solution)/shard_map/pallas_call | solution.py:157
  239.3 4.9 all-to-all-start.2
  244.2 4.7 collective-permute-start.9
  249.0 1.3 collective-permute-start.7
  250.3 37.4 %collective-permute-done.9 = f32[8,512]{1,0:T(8,128)S(1)} collective-permute-done((f32[8,512]{1,0:T(8,128)S(1)}, f32[8,512]{1,0:T(8,128)S(1)}, u32[]{:S(2)}, u32[]{:S(2)}) %collective-permute-start.9) | collective-permute-done | bytes 16416 | tf_op jit(solution)/shard_map/ppermute | solution.py:235
  287.7 1.3 collective-permute-start.8
  289.0 1.4 collective-permute-done.8
  290.4 0.7 collective-permute-start.10
  291.1 1.3 collective-permute-start.13
  292.4 1.3 collective-permute-start.12
  293.7 183.4 %collective-permute-done.13 = f32[8,512]{1,0:T(8,128)S(1)} collective-permute-done((f32[8,512]{1,0:T(8,128)S(1)}, f32[8,512]{1,0:T(8,128)S(1)}, u32[]{:S(2)}, u32[]{:S(2)}) %collective-permute-start.13) | collective-permute-done | bytes 16416 | tf_op jit(solution)/shard_map/ppermute | solution.py:235
  477.1 0.7 collective-permute-start.6
  477.8 0.0 collective-permute-done.12
  477.8 1.3 collective-permute-start.11
  479.2 0.1 reshape.85
  479.2 11.8 %gather_fusion.3 = f32[2048]{0:T(1024)S(1)} fusion(f32[2560]{0:T(1024)S(1)} %reshape.85, s32[2048]{0:T(1024)S(1)} %broadcast_clamp_fusion), kind=kCustom, calls=%fused_computation.3 | custom fusion | bytes 24576 | tf_op jit(solution)/shard_map/jit(_take)/gather | solution.py:287
  491.0 0.0 collective-permute-done.11
  491.0 1.6 collective-permute-start.14
  492.7 0.0 collective-permute-done.6
  492.7 0.5 collective-permute-start.15
  493.1 2.6 collective-permute-done.14
  495.7 1.6 collective-permute-start.16
  497.3 0.6 pad_maximum_fusion.recv_ref
  497.9 0.0 collective-permute-done.5.refs_0_
  497.9 13.0 %shard_map.153.own_ref = f32[384,3072]{1,0:T(8,128)} custom-call(s32[1]{0:T(128)} %bitcast.z_ref.s_ref, bf16[2560,768]{1,0:T(8,128)(2,1)} %bitcast.35, bf16[2560,3072]{1,0:T(8,128)(2,1)} %get-tuple-element.12.d3_ref.r_ref, f32[272,3072]{1,0:T(8,128)} %collective-permute-done.5.refs_0_), custom_call_target="tpu_custom_call" | custom-call | flops 6039797760 | bytes 20447232 | tf_op jit(solution)/shard_map/pallas_call | solution.py:122
  510.9 0.9 slice.35.tail_ref
  511.9 0.6 broadcast_select_fusion.1
  512.5 1.6 shard_map.154.own_ref
  514.1 5.2 collective-permute-done.15.recv_ref
  519.3 1.0 copy-done.3
  520.2 2.7 shard_map.155.own_ref
  522.9 0.7 shard_map.156
  523.7 11.1 %gather_fusion.2 = bf16[2048,768]{1,0:T(8,128)(2,1)S(1)} fusion(bf16[2560,768]{1,0:T(8,128)(2,1)} %bitcast.13, s32[2048]{0:T(1024)S(1)} %broadcast_clamp_fusion), kind=kCustom, calls=%fused_computation.2 | custom fusion | bytes 6299648 | tf_op jit(solution)/shard_map/jit(_take)/gather | solution.py:285
  534.8 1.9 broadcast_select_fusion
  536.7 13.3 %shard_map.149 = f32[384,3072]{1,0:T(8,128)} custom-call(s32[1]{0:T(128)} %bitcast.z_ref.s_ref, bf16[2560,768]{1,0:T(8,128)(2,1)} %bitcast.36, bf16[2560,3072]{1,0:T(8,128)(2,1)} %get-tuple-element.11.d1_ref.r_ref, f32[384,3072]{1,0:T(8,128)} %collective-permute-done.3.refs_0_), custom_call_target="tpu_custom_call" | custom-call | flops 6039797760 | bytes 20447232 | tf_op jit(solution)/shard_map/pallas_call | solution.py:122
  550.0 0.0 collective-permute-done.4.refs_0_
  550.0 17.7 %shard_map.151 = f32[1536,768]{1,0:T(8,128)} custom-call(s32[1]{0:T(128)} %bitcast.z_ref.s_ref, bf16[2560,3072]{1,0:T(8,128)(2,1)} %bitcast.29, bf16[2560,3072]{1,0:T(8,128)(2,1)} %bitcast.32, bf16[2560,768]{1,0:T(8,128)(2,1)} %get-tuple-element.20.g_ref, f32[1536,768]{1,0:T(8,128)} %collective-permute-done.4.refs_0_), custom_call_target="tpu_custom_call" | custom-call | flops 6039797760 | bytes 31457280 | tf_op jit(solution)/shard_map/pallas_call | solution.py:93
  (32 shorter events, 0.2 us)
Async XLA Ops:
  0.6 28.8 %copy-start = (bf16[2048,768]{1,0:T(8,128)(2,1)S(1)}, bf16[2048,768]{1,0:T(8,128)(2,1)}, u32[]{:S(2)}) copy-start(bf16[2048,768]{1,0:T(8,128)(2,1)} %param.11) | copy-start | bytes 9437188
  0.6 9.0 %copy-start.2 = (f32[2048,1]{0,1:T(1,128)S(1)}, f32[2048,1]{0,1:T(1,128)}, u32[]{:S(2)}) copy-start(f32[2048,1]{0,1:T(1,128)} %param.14) | copy-start | bytes 24580
  24.0 14.0 %all-to-all-start.1 = ((f32[1,8,320]{2,0,1:T(1,128)}), f32[1,8,320]{2,0,1:T(1,128)S(1)}, u32[]{:S(2)}, u32[]{:S(2)}) async-start(f32[1,8,320]{2,0,1:T(1,128)} %select_n.58), calls=%async_computation.1 | async-start | bytes 24576 | tf_op jit(solution)/shard_map/all_to_all | solution.py:265
  38.0 4.7 copy-start.5
  38.0 51.0 %all-to-all-start = ((bf16[1,8,320,768]{3,2,0,1:T(8,128)(2,1)}), bf16[1,8,320,768]{3,2,0,1:T(8,128)(2,1)}, u32[]{:S(2)}, u32[]{:S(2)}) async-start(bf16[1,8,320,768]{3,2,0,1:T(8,128)(2,1)} %bitcast.37), calls=%async_computation | async-start | bytes 7864320 | tf_op jit(solution)/shard_map/all_to_all | solution.py:264
  42.7 56.6 %collective-permute-start = (bf16[1536,768]{1,0:T(8,128)(2,1)S(1)}, bf16[1536,768]{1,0:T(8,128)(2,1)}, u32[]{:S(2)}, u32[]{:S(2)}) collective-permute-start(bf16[1536,768]{1,0:T(8,128)(2,1)S(1)} %bitcast.45), channel_id=1, source_target_pairs={{0,8},{8,0},{1,9},{9,1},{2,10},{10,2},{3,11},{11,3},{4,12},{12,4},... | collective-permute-start | bytes 7077896 | tf_op jit(solution)/shard_map/ppermute | solution.py:229
  44.3 132.1 %collective-permute-start.1 = (bf16[384,3072]{1,0:T(8,128)(2,1)}, bf16[384,3072]{1,0:T(8,128)(2,1)}, u32[]{:S(2)}, u32[]{:S(2)}) collective-permute-start(bf16[384,3072]{1,0:T(8,128)(2,1)} %bitcast.46), channel_id=1, source_target_pairs={{0,8},{8,0},{1,9},{9,1},{2,10},{10,2},{3,11},{11,3},{4,12},{12,4},... | collective-permute-start | bytes 7077896 | tf_op jit(solution)/shard_map/ppermute | solution.py:229
  44.7 153.3 %collective-permute-start.2 = (bf16[384,3072]{1,0:T(8,128)(2,1)}, bf16[384,3072]{1,0:T(8,128)(2,1)}, u32[]{:S(2)}, u32[]{:S(2)}) collective-permute-start(bf16[384,3072]{1,0:T(8,128)(2,1)} %bitcast.48), channel_id=1, source_target_pairs={{0,8},{8,0},{1,9},{9,1},{2,10},{10,2},{3,11},{11,3},{4,12},{12,4},... | collective-permute-start | bytes 7077896 | tf_op jit(solution)/shard_map/ppermute | solution.py:229
  95.8 143.5 %all-to-all-start.3 = ((f32[1,8,320]{2,0,1:T(1,128)}), f32[1,8,320]{2,0,1:T(1,128)S(1)}, u32[]{:S(2)}, u32[]{:S(2)}) async-start(f32[1,8,320]{2,0,1:T(1,128)} %reshape.84), calls=%async_computation.3 | async-start | bytes 24576 | tf_op jit(solution)/shard_map/all_to_all | solution.py:284
  144.9 391.7 %collective-permute-start.3 = (f32[384,3072]{1,0:T(8,128)}, f32[384,3072]{1,0:T(8,128)}, u32[]{:S(2)}, u32[]{:S(2)}) collective-permute-start(f32[384,3072]{1,0:T(8,128)} %shard_map.148), channel_id=1, source_target_pairs={{0,8},{8,0},{1,9},{9,1},{2,10},{10,2},{3,11},{11,3},{4,12},{12,4},... | collective-permute-start | bytes 14155784 | tf_op jit(solution)/shard_map/ppermute | solution.py:229
  162.6 387.4 %collective-permute-start.4 = (f32[1536,768]{1,0:T(8,128)}, f32[1536,768]{1,0:T(8,128)}, u32[]{:S(2)}, u32[]{:S(2)}) collective-permute-start(f32[1536,768]{1,0:T(8,128)} %shard_map.150), channel_id=1, source_target_pairs={{0,8},{8,0},{1,9},{9,1},{2,10},{10,2},{3,11},{11,3},{4,12},{12,4},... | collective-permute-start | bytes 14155784 | tf_op jit(solution)/shard_map/ppermute | solution.py:229
  174.8 323.1 %collective-permute-start.5 = (f32[272,3072]{1,0:T(8,128)}, f32[272,3072]{1,0:T(8,128)}, u32[]{:S(2)}, u32[]{:S(2)}) collective-permute-start(f32[272,3072]{1,0:T(8,128)} %get-tuple-element.13), channel_id=1, source_target_pairs={{0,8},{8,0},{1,9},{9,1},{2,10},{10,2},{3,11},{11,3},{4,12},{12,4},... | collective-permute-start | bytes 10027016 | tf_op jit(solution)/shard_map/ppermute | solution.py:229
  239.3 4.9 copy-start.4
  239.3 284.4 %all-to-all-start.2 = ((bf16[1,8,320,768]{3,2,0,1:T(8,128)(2,1)}), bf16[1,8,320,768]{3,2,0,1:T(8,128)(2,1)}, u32[]{:S(2)}, u32[]{:S(2)}) async-start(bf16[1,8,320,768]{3,2,0,1:T(8,128)(2,1)} %bitcast.40), calls=%async_computation.2 | async-start | bytes 7864320 | tf_op jit(solution)/shard_map/all_to_all | solution.py:283
  244.2 43.5 %collective-permute-start.9 = (f32[8,512]{1,0:T(8,128)S(1)}, f32[8,512]{1,0:T(8,128)S(1)}, u32[]{:S(2)}, u32[]{:S(2)}) collective-permute-start(f32[8,512]{1,0:T(8,128)S(1)} %get-tuple-element.22), channel_id=1, source_target_pairs={{0,6},{1,7},{8,14},{9,15}} | collective-permute-start | bytes 49160 | tf_op jit(solution)/shard_map/ppermute | solution.py:235
  249.0 40.0 %collective-permute-start.7 = (f32[8,512]{1,0:T(8,128)S(1)}, f32[8,512]{1,0:T(8,128)S(1)}, u32[]{:S(2)}, u32[]{:S(2)}) collective-permute-start(f32[8,512]{1,0:T(8,128)S(1)} %get-tuple-element.23), channel_id=1, source_target_pairs={{0,2},{1,3},{8,10},{9,11}} | collective-permute-start | bytes 49160 | tf_op jit(solution)/shard_map/ppermute | solution.py:235
  287.7 2.7 collective-permute-start.8
  290.4 0.7 collective-permute-start.10
  291.1 186.1 %collective-permute-start.13 = (f32[8,512]{1,0:T(8,128)S(1)}, f32[8,512]{1,0:T(8,128)S(1)}, u32[]{:S(2)}, u32[]{:S(2)}) collective-permute-start(f32[8,512]{1,0:T(8,128)S(1)} %collective-permute-done.10), channel_id=1, source_target_pairs={{6,0},{7,1},{14,8},{15,9}} | collective-permute-start | bytes 49160 | tf_op jit(solution)/shard_map/ppermute | solution.py:235
  292.4 185.4 %collective-permute-start.12 = (f32[8,512]{1,0:T(8,128)S(1)}, f32[8,512]{1,0:T(8,128)S(1)}, u32[]{:S(2)}, u32[]{:S(2)}) collective-permute-start(f32[8,512]{1,0:T(8,128)S(1)} %collective-permute-done.10), channel_id=1, source_target_pairs={{4,0},{5,1},{12,8},{13,9}} | collective-permute-start | bytes 49160 | tf_op jit(solution)/shard_map/ppermute | solution.py:235
  477.1 15.5 %collective-permute-start.6 = (f32[8,1536]{1,0:T(8,128)S(1)}, f32[8,1536]{1,0:T(8,128)S(1)}, u32[]{:S(2)}, u32[]{:S(2)}) collective-permute-start(f32[8,1536]{1,0:T(8,128)S(1)} %get-tuple-element.24), channel_id=1, source_target_pairs={{2,10},{3,11},{4,12},{5,13},{6,14},{7,15},{10,2},{11,3},{12,4},{13... | collective-permute-start | bytes 147464 | tf_op jit(solution)/shard_map/ppermute | solution.py:235
  477.8 13.2 %collective-permute-start.11 = (f32[8,512]{1,0:T(8,128)S(1)}, f32[8,512]{1,0:T(8,128)S(1)}, u32[]{:S(2)}, u32[]{:S(2)}) collective-permute-start(f32[8,512]{1,0:T(8,128)S(1)} %collective-permute-done.10), channel_id=1, source_target_pairs={{2,0},{3,1},{10,8},{11,9}} | collective-permute-start | bytes 49160 | tf_op jit(solution)/shard_map/ppermute | solution.py:235
  479.2 13.4 %copy-start.6 = (f32[88,3072]{1,0:T(8,128)S(1)}, f32[88,3072]{1,0:T(8,128)}, u32[]{:S(2)}) copy-start(f32[88,3072]{1,0:T(8,128)} %get-tuple-element.15) | copy-start | bytes 3244036
  479.2 16.4 %copy-start.7 = (f32[16,3072]{1,0:T(8,128)S(1)}, f32[16,3072]{1,0:T(8,128)}, u32[]{:S(2)}) copy-start(f32[16,3072]{1,0:T(8,128)} %get-tuple-element.16) | copy-start | bytes 589828
  491.0 4.7 collective-permute-start.14
  492.7 26.6 %collective-permute-start.15 = (f32[88,3072]{1,0:T(8,128)S(1)}, f32[88,3072]{1,0:T(8,128)S(1)}, u32[]{:S(2)}, u32[]{:S(2)}) collective-permute-start(f32[88,3072]{1,0:T(8,128)S(1)} %copy-done.6), channel_id=1, source_target_pairs={{0,8},{8,0},{1,9},{9,1},{2,10},{10,2},{3,11},{11,3},{4,12},{12,4},... | collective-permute-start | bytes 3244040 | tf_op jit(solution)/shard_map/ppermute | solution.py:229
  495.7 27.2 %collective-permute-start.16 = (f32[16,3072]{1,0:T(8,128)S(1)}, f32[16,3072]{1,0:T(8,128)S(1)}, u32[]{:S(2)}, u32[]{:S(2)}) collective-permute-start(f32[16,3072]{1,0:T(8,128)S(1)} %copy-done.7), channel_id=1, source_target_pairs={{0,8},{8,0},{1,9},{9,1},{2,10},{10,2},{3,11},{11,3},{4,12},{12,4},... | collective-permute-start | bytes 589832 | tf_op jit(solution)/shard_map/ppermute | solution.py:229
  519.3 1.0 copy-start.3
  550.0 17.7 %copy-start.1 = (bf16[2048,768]{1,0:T(8,128)(2,1)S(1)}, bf16[2048,768]{1,0:T(8,128)(2,1)}, u32[]{:S(2)}) copy-start(bf16[2048,768]{1,0:T(8,128)(2,1)} %param.11) | copy-start | bytes 9437188

commit v10 on v9

--- a/solution.py
+++ b/solution.py
@@ -19,7 +19,7 @@
     return pl.CostEstimate(flops=flops, bytes_accessed=bytes_accessed, transcendentals=0)
 
 
-def hidden_grads(z, g_rows, w_own, w_other, h_gate, h_up, row_tile=1280, col_tile=512):
+def hidden_grads(z, g_rows, w_own, w_other, h_gate, h_up, row_tile=1280, col_tile=768):
     rows, width = g_rows.shape
     half = w_own.shape[0]
     tiles = half // col_tile
@@ -136,7 +136,7 @@
     )(which, x_rows, wide, *extra)
 
 
-def row_grads(z, dh_gate, dh_up, gate_own, gate_other, up_own, up_other, row_tile=640):
+def row_grads(z, dh_gate, dh_up, gate_own, gate_other, up_own, up_other, row_tile=1280):
     rows, cols = dh_gate.shape
     part = gate_own.shape[0]
 
@@ -153,7 +153,7 @@
         pl.when(h == 1)(lambda: emit(g1_ref, u1_ref))
 
     tile = pl.BlockSpec((row_tile, cols), lambda h, i, z_ref: (i, 0))
-    full = pl.BlockSpec((part, cols), lambda h, i, z_ref: (0, 0))
+    full = pl.BlockSpec((part, cols), lambda h, i, z_ref: (0, 0), pipeline_mode=pl.Buffered(1))
     return pl.pallas_call(
         kernel,
         grid_spec=pltpu.PrefetchScalarGridSpec(
@@ -271,7 +271,7 @@
         part, = weight_grad_rhs(1 - z, x_rows, dh_gate, fs_n)
         recv_gate = exchange(part)
         step = width // fs_n // 16
-        cuts = (0, 11 * step + step // 3, 15 * step, 15 * step + step // 3, 16 * step)
+        cuts = (0, 11 * step + 2 * step // 3, 15 * step, 15 * step + step // 3, 16 * step)
         piece = weight_grad_rhs(1 - z, x_rows, dh_up, fs_n, cuts)
         half = piece[2].shape[1] // 2
         direct, around = detour(piece[2][:, :half])

time: 569 us -> 569 us (level)
  no operation moved by 1% of the time
where the time goes in v10:
time: 569 us; the launch traced here: 568 us
  waiting for transfers between devices  295 us (52%)
  Pallas kernels  163 us (29%)
  local copies, waits for them, and re-layouts  56.5 us (10%)
  starting transfers between devices  41.4 us (7%)
  other arithmetic  10.3 us (2%)
    ppermute x8, waiting for transfers between devices, send(): lax.ppermute(value, ('fsdp', 'ep'), [(a * ep_n + b, c * ep_n + d) for (a,...  223 us
    pallas_call x4, Pallas kernels, weight_grad_rhs(): pl.pallas_call(kernel, grid_spec=pltpu.PrefetchScalarGridSpec(num_scalar_...  49.9 us
    pallas_call x1, Pallas kernels, row_grads(): pl.pallas_call(kernel, grid_spec=pltpu.PrefetchScalarGridSpec(num_scalar_...  42.6 us
    all_to_all x1, waiting for transfers between devices, local_backward(): lax.all_to_all(send_dy, 'ep', 1, 1, tiled=True).reshape(rows_loc, width)  42.5 us
    pallas_call x2, Pallas kernels, down_grad(): pl.pallas_call(kernel, grid_spec=pltpu.PrefetchScalarGridSpec(num_scalar_...  33.9 us
    pallas_call x1, Pallas kernels, hidden_grads(): pl.pallas_call(kernel, grid_spec=pltpu.PrefetchScalarGridSpec(num_scalar_...  31.9 us
    ppermute x9, waiting for transfers between devices, exchange(): return lax.ppermute(value, 'fsdp', swap)  29.4 us
    gather x1, local copies, waits for them, and re-layouts, local_backward(): jnp.take(gates.reshape(-1), src_choice, mode='fill', fill_value=0)  13.6 us
  transfers between devices with their start and end apart: 21, of which 7 were waited for; matrix products, arithmetic and copies ran while one was open for 7% of the time, Pallas kernels for 26%

profile of v10, /device:TPU:0, one launch (start us, length us, event | category | flops | bytes accessed | tf_op | source)
XLA Modules:
  0.0 567.5 jit_solution(9704578183850701749)
XLA Ops:
  0.6 0.0 copy-start
  0.7 0.9 fusion.4
  1.6 8.1 %scatter_custom_fusion = s32[2560]{0:T(1024)S(1)} fusion(s32[2048]{0:T(1024)S(1)} %bitcast.41, s32[2048]{0:T(1024)S(1)} %iota.3, s32[]{:T(128)} %constant.86.clone.1), kind=kCustom, calls=%fused_computation.20 | custom fusion | bytes 10244 | tf_op jit(solution)/shard_map/scatter | solution.py:261
  9.7 13.6 %gather_fusion.1 = f32[2560]{0:T(1024)S(1)} fusion(f32[2048]{0:T(1024)S(1)} %bitcast.25, s32[3072]{0:T(1024)S(1)} %pad_clamp_fusion), kind=kCustom, calls=%fused_computation.1 | custom fusion | bytes 30720 | tf_op jit(solution)/shard_map/jit(_take)/gather | solution.py:263
  23.3 0.7 select_n.58
  24.0 5.4 all-to-all-start.1
  29.5 8.5 %gather_fusion = bf16[2560,768]{1,0:T(8,128)(2,1)} fusion(bf16[2048,768]{1,0:T(8,128)(2,1)S(1)} %copy-done, s32[3072]{0:T(1024)S(1)} %pad_clamp_fusion.1), kind=kCustom, calls=%fused_computation | custom fusion | bytes 7874560 | tf_op jit(solution)/shard_map/jit(_take)/gather | solution.py:262
  38.0 0.0 all-to-all-done.1
  38.0 4.7 all-to-all-start
  42.7 1.6 collective-permute-start
  44.3 0.4 collective-permute-start.1
  44.7 1.6 collective-permute-start.2
  46.3 0.1 mul.21
  46.4 42.5 %all-to-all-done = bf16[1,8,320,768]{3,2,0,1:T(8,128)(2,1)} async-done(((bf16[1,8,320,768]{3,2,0,1:T(8,128)(2,1)}), bf16[1,8,320,768]{3,2,0,1:T(8,128)(2,1)}, u32[]{:S(2)}, u32[]{:S(2)}) %all-to-all-start) | async-done | bytes 3932192 | tf_op jit(solution)/shard_map/all_to_all | solution.py:264
  88.9 6.1 %fusion.1 = (f32[2560]{0:T(1024)S(1)}, bf16[2560,768]{1,0:T(8,128)(2,1)}) fusion(bf16[1,2560,768]{2,1,0:T(8,128)(2,1)} %param.18, bf16[1,8,320,768]{3,2,0,1:T(8,128)(2,1)} %all-to-all-done, f32[2560]{0:T(1024)S(1)} %mul.21), kind=kLoop, calls=%fused_computation.8 | loop fusion | flops 11793920 | bytes 11816960 | tf_op jit(solution)/shard_map/rd,rd->r/dot_general | solution.py:282
  95.1 0.7 reshape.84
  95.8 3.5 all-to-all-start.3
  99.3 0.0 collective-permute-done.other_ref
  99.3 31.9 %shard_map.146 = (bf16[2560,3072]{1,0:T(8,128)(2,1)}, bf16[2560,3072]{1,0:T(8,128)(2,1)}) custom-call(s32[1]{0:T(128)} %bitcast.z_ref.s_ref, bf16[2560,768]{1,0:T(8,128)(2,1)} %get-tuple-element.20.g_ref, bf16[1536,768]{1,0:T(8,128)(2,1)} %bitcast.44, bf16[1536,768]{1,0:T(8,128)(2,1)} %collective-permute-done.other_ref, bf16[2560,3072]{1,0:T(8,128)(2,1)} %bitcast.27, ...), custom_call_target="tpu_custom_call" | custom-call | flops 12079595520 | bytes 62914560 | tf_op jit(solution)/shard_map/pallas_call | solution.py:44
  131.2 11.8 %shard_map.148 = f32[384,3072]{1,0:T(8,128)} custom-call(s32[1]{0:T(128)S(6)} %sub.10.s_ref, bf16[2560,768]{1,0:T(8,128)(2,1)} %bitcast.33, bf16[2560,3072]{1,0:T(8,128)(2,1)} %get-tuple-element.11.d1_ref.r_ref), custom_call_target="tpu_custom_call" | custom-call | flops 6039797760 | bytes 20447232 | tf_op jit(solution)/shard_map/pallas_call | solution.py:122
  143.0 1.3 collective-permute-start.3
  144.3 16.2 %shard_map.150 = f32[1536,768]{1,0:T(8,128)} custom-call(s32[1]{0:T(128)S(6)} %sub.10.s_ref, bf16[2560,3072]{1,0:T(8,128)(2,1)} %bitcast.28, bf16[2560,3072]{1,0:T(8,128)(2,1)} %bitcast.31, bf16[2560,768]{1,0:T(8,128)(2,1)} %get-tuple-element.20.g_ref), custom_call_target="tpu_custom_call" | custom-call | flops 6039797760 | bytes 31457280 | tf_op jit(solution)/shard_map/pallas_call | solution.py:93
  160.5 0.7 collective-permute-start.4
  161.2 11.7 %shard_map.152 = (f32[280,3072]{1,0:T(8,128)}, f32[80,3072]{1,0:T(8,128)}, f32[8,3072]{1,0:T(8,128)}, f32[16,3072]{1,0:T(8,128)}) custom-call(s32[1]{0:T(128)S(6)} %sub.10.s_ref, bf16[2560,768]{1,0:T(8,128)(2,1)} %bitcast.34, bf16[2560,3072]{1,0:T(8,128)(2,1)} %get-tuple-element.12.d3_ref.r_ref), custom_call_target="tpu_custom_call" | custom-call | flops 6039797760 | bytes 20447232 | tf_op jit(solution)/shard_map/pallas_call | solution.py:122
  172.9 1.3 collective-permute-start.5
  174.2 0.0 collective-permute-done.1.g1_ref
  174.2 23.8 %collective-permute-done.2.u1_ref = bf16[384,3072]{1,0:T(8,128)(2,1)} collective-permute-done((bf16[384,3072]{1,0:T(8,128)(2,1)}, bf16[384,3072]{1,0:T(8,128)(2,1)}, u32[]{:S(2)}, u32[]{:S(2)}) %collective-permute-start.2) | collective-permute-done | bytes 2359328 | tf_op jit(solution)/shard_map/ppermute | solution.py:229
  198.0 42.6 %shard_map.147 = bf16[2560,768]{1,0:T(8,128)(2,1)} custom-call(s32[1]{0:T(128)} %bitcast.z_ref.s_ref, bf16[2560,3072]{1,0:T(8,128)(2,1)} %get-tuple-element.11.d1_ref.r_ref, bf16[2560,3072]{1,0:T(8,128)(2,1)} %get-tuple-element.12.d3_ref.r_ref, bf16[384,3072]{1,0:T(8,128)(2,1)} %bitcast.47, bf16[384,3072]{1,0:T(8,128)(2,1)} %collective-permute-done.1.g1_ref, ...), custom_call_target="tpu_custom_call" | custom-call | flops 24159191040 | bytes 62914560 | tf_op jit(solution)/shard_map/pallas_call | solution.py:157
  240.6 0.0 all-to-all-done.3
  240.7 4.7 all-to-all-start.2
  245.3 4.7 collective-permute-start.9
  250.1 1.3 collective-permute-start.7
  251.4 37.7 %collective-permute-done.9 = f32[8,512]{1,0:T(8,128)S(1)} collective-permute-done((f32[8,512]{1,0:T(8,128)S(1)}, f32[8,512]{1,0:T(8,128)S(1)}, u32[]{:S(2)}, u32[]{:S(2)}) %collective-permute-start.9) | collective-permute-done | bytes 16416 | tf_op jit(solution)/shard_map/ppermute | solution.py:235
  289.1 1.3 collective-permute-start.8
  290.4 1.4 collective-permute-done.8
  291.8 0.7 collective-permute-start.10
  292.5 1.3 collective-permute-start.13
  293.8 1.3 collective-permute-start.12
  295.1 184.2 %collective-permute-done.13 = f32[8,512]{1,0:T(8,128)S(1)} collective-permute-done((f32[8,512]{1,0:T(8,128)S(1)}, f32[8,512]{1,0:T(8,128)S(1)}, u32[]{:S(2)}, u32[]{:S(2)}) %collective-permute-start.13) | collective-permute-done | bytes 16416 | tf_op jit(solution)/shard_map/ppermute | solution.py:235
  479.3 0.7 collective-permute-start.6
  479.9 0.0 collective-permute-done.12
  479.9 1.3 collective-permute-start.11
  481.3 0.1 reshape.85
  481.4 11.8 %gather_fusion.3 = f32[2048]{0:T(1024)S(1)} fusion(f32[2560]{0:T(1024)S(1)} %reshape.85, s32[2048]{0:T(1024)S(1)} %broadcast_clamp_fusion), kind=kCustom, calls=%fused_computation.3 | custom fusion | bytes 24576 | tf_op jit(solution)/shard_map/jit(_take)/gather | solution.py:287
  493.1 0.0 collective-permute-done.11
  493.2 1.6 collective-permute-start.14
  494.8 0.0 collective-permute-done.6
  494.8 0.5 collective-permute-start.15
  495.2 2.6 collective-permute-done.14
  497.8 1.6 collective-permute-start.16
  499.4 0.6 pad_maximum_fusion.recv_ref
  500.0 13.0 %shard_map.153.own_ref = f32[384,3072]{1,0:T(8,128)} custom-call(s32[1]{0:T(128)} %bitcast.z_ref.s_ref, bf16[2560,768]{1,0:T(8,128)(2,1)} %bitcast.35, bf16[2560,3072]{1,0:T(8,128)(2,1)} %get-tuple-element.12.d3_ref.r_ref, f32[280,3072]{1,0:T(8,128)} %collective-permute-done.5.refs_0_), custom_call_target="tpu_custom_call" | custom-call | flops 6039797760 | bytes 20447232 | tf_op jit(solution)/shard_map/pallas_call | solution.py:122
  513.1 0.9 slice.35.tail_ref
  514.0 0.6 broadcast_select_fusion.1
  514.6 1.6 shard_map.154.own_ref
  516.2 3.0 collective-permute-done.15.recv_ref
  519.3 0.9 copy-done.3
  520.2 2.6 shard_map.155.own_ref
  522.8 0.7 shard_map.156
  523.5 11.1 %gather_fusion.2 = bf16[2048,768]{1,0:T(8,128)(2,1)S(1)} fusion(bf16[2560,768]{1,0:T(8,128)(2,1)} %bitcast.13, s32[2048]{0:T(1024)S(1)} %broadcast_clamp_fusion), kind=kCustom, calls=%fused_computation.2 | custom fusion | bytes 6299648 | tf_op jit(solution)/shard_map/jit(_take)/gather | solution.py:285
  534.6 1.9 broadcast_select_fusion
  536.5 13.3 %shard_map.149 = f32[384,3072]{1,0:T(8,128)} custom-call(s32[1]{0:T(128)} %bitcast.z_ref.s_ref, bf16[2560,768]{1,0:T(8,128)(2,1)} %bitcast.36, bf16[2560,3072]{1,0:T(8,128)(2,1)} %get-tuple-element.11.d1_ref.r_ref, f32[384,3072]{1,0:T(8,128)} %collective-permute-done.3.refs_0_), custom_call_target="tpu_custom_call" | custom-call | flops 6039797760 | bytes 20447232 | tf_op jit(solution)/shard_map/pallas_call | solution.py:122
  549.8 0.0 collective-permute-done.4.refs_0_
  549.8 17.7 %shard_map.151 = f32[1536,768]{1,0:T(8,128)} custom-call(s32[1]{0:T(128)} %bitcast.z_ref.s_ref, bf16[2560,3072]{1,0:T(8,128)(2,1)} %bitcast.29, bf16[2560,3072]{1,0:T(8,128)(2,1)} %bitcast.32, bf16[2560,768]{1,0:T(8,128)(2,1)} %get-tuple-element.20.g_ref, f32[1536,768]{1,0:T(8,128)} %collective-permute-done.4.refs_0_), custom_call_target="tpu_custom_call" | custom-call | flops 6039797760 | bytes 31457280 | tf_op jit(solution)/shard_map/pallas_call | solution.py:93
  (32 shorter events, 0.2 us)
Async XLA Ops:
  0.6 28.8 %copy-start = (bf16[2048,768]{1,0:T(8,128)(2,1)S(1)}, bf16[2048,768]{1,0:T(8,128)(2,1)}, u32[]{:S(2)}) copy-start(bf16[2048,768]{1,0:T(8,128)(2,1)} %param.11) | copy-start | bytes 9437188
  0.6 9.0 %copy-start.2 = (f32[2048,1]{0,1:T(1,128)S(1)}, f32[2048,1]{0,1:T(1,128)}, u32[]{:S(2)}) copy-start(f32[2048,1]{0,1:T(1,128)} %param.14) | copy-start | bytes 24580
  24.0 14.0 %all-to-all-start.1 = ((f32[1,8,320]{2,0,1:T(1,128)}), f32[1,8,320]{2,0,1:T(1,128)S(1)}, u32[]{:S(2)}, u32[]{:S(2)}) async-start(f32[1,8,320]{2,0,1:T(1,128)} %select_n.58), calls=%async_computation.1 | async-start | bytes 24576 | tf_op jit(solution)/shard_map/all_to_all | solution.py:265
  38.0 4.7 copy-start.5
  38.0 51.0 %all-to-all-start = ((bf16[1,8,320,768]{3,2,0,1:T(8,128)(2,1)}), bf16[1,8,320,768]{3,2,0,1:T(8,128)(2,1)}, u32[]{:S(2)}, u32[]{:S(2)}) async-start(bf16[1,8,320,768]{3,2,0,1:T(8,128)(2,1)} %bitcast.37), calls=%async_computation | async-start | bytes 7864320 | tf_op jit(solution)/shard_map/all_to_all | solution.py:264
  42.7 56.6 %collective-permute-start = (bf16[1536,768]{1,0:T(8,128)(2,1)S(1)}, bf16[1536,768]{1,0:T(8,128)(2,1)}, u32[]{:S(2)}, u32[]{:S(2)}) collective-permute-start(bf16[1536,768]{1,0:T(8,128)(2,1)S(1)} %bitcast.45), channel_id=1, source_target_pairs={{0,8},{8,0},{1,9},{9,1},{2,10},{10,2},{3,11},{11,3},{4,12},{12,4},... | collective-permute-start | bytes 7077896 | tf_op jit(solution)/shard_map/ppermute | solution.py:229
  44.3 129.9 %collective-permute-start.1 = (bf16[384,3072]{1,0:T(8,128)(2,1)}, bf16[384,3072]{1,0:T(8,128)(2,1)}, u32[]{:S(2)}, u32[]{:S(2)}) collective-permute-start(bf16[384,3072]{1,0:T(8,128)(2,1)} %bitcast.46), channel_id=1, source_target_pairs={{0,8},{8,0},{1,9},{9,1},{2,10},{10,2},{3,11},{11,3},{4,12},{12,4},... | collective-permute-start | bytes 7077896 | tf_op jit(solution)/shard_map/ppermute | solution.py:229
  44.7 153.3 %collective-permute-start.2 = (bf16[384,3072]{1,0:T(8,128)(2,1)}, bf16[384,3072]{1,0:T(8,128)(2,1)}, u32[]{:S(2)}, u32[]{:S(2)}) collective-permute-start(bf16[384,3072]{1,0:T(8,128)(2,1)} %bitcast.48), channel_id=1, source_target_pairs={{0,8},{8,0},{1,9},{9,1},{2,10},{10,2},{3,11},{11,3},{4,12},{12,4},... | collective-permute-start | bytes 7077896 | tf_op jit(solution)/shard_map/ppermute | solution.py:229
  95.8 144.9 %all-to-all-start.3 = ((f32[1,8,320]{2,0,1:T(1,128)}), f32[1,8,320]{2,0,1:T(1,128)S(1)}, u32[]{:S(2)}, u32[]{:S(2)}) async-start(f32[1,8,320]{2,0,1:T(1,128)} %reshape.84), calls=%async_computation.3 | async-start | bytes 24576 | tf_op jit(solution)/shard_map/all_to_all | solution.py:284
  143.0 393.5 %collective-permute-start.3 = (f32[384,3072]{1,0:T(8,128)}, f32[384,3072]{1,0:T(8,128)}, u32[]{:S(2)}, u32[]{:S(2)}) collective-permute-start(f32[384,3072]{1,0:T(8,128)} %shard_map.148), channel_id=1, source_target_pairs={{0,8},{8,0},{1,9},{9,1},{2,10},{10,2},{3,11},{11,3},{4,12},{12,4},... | collective-permute-start | bytes 14155784 | tf_op jit(solution)/shard_map/ppermute | solution.py:229
  160.5 389.4 %collective-permute-start.4 = (f32[1536,768]{1,0:T(8,128)}, f32[1536,768]{1,0:T(8,128)}, u32[]{:S(2)}, u32[]{:S(2)}) collective-permute-start(f32[1536,768]{1,0:T(8,128)} %shard_map.150), channel_id=1, source_target_pairs={{0,8},{8,0},{1,9},{9,1},{2,10},{10,2},{3,11},{11,3},{4,12},{12,4},... | collective-permute-start | bytes 14155784 | tf_op jit(solution)/shard_map/ppermute | solution.py:229
  172.9 327.2 %collective-permute-start.5 = (f32[280,3072]{1,0:T(8,128)}, f32[280,3072]{1,0:T(8,128)}, u32[]{:S(2)}, u32[]{:S(2)}) collective-permute-start(f32[280,3072]{1,0:T(8,128)} %get-tuple-element.13), channel_id=1, source_target_pairs={{0,8},{8,0},{1,9},{9,1},{2,10},{10,2},{3,11},{11,3},{4,12},{12,4},... | collective-permute-start | bytes 10321928 | tf_op jit(solution)/shard_map/ppermute | solution.py:229
  240.6 4.7 copy-start.4
  240.7 282.9 %all-to-all-start.2 = ((bf16[1,8,320,768]{3,2,0,1:T(8,128)(2,1)}), bf16[1,8,320,768]{3,2,0,1:T(8,128)(2,1)}, u32[]{:S(2)}, u32[]{:S(2)}) async-start(bf16[1,8,320,768]{3,2,0,1:T(8,128)(2,1)} %bitcast.40), calls=%async_computation.2 | async-start | bytes 7864320 | tf_op jit(solution)/shard_map/all_to_all | solution.py:283
  245.3 43.7 %collective-permute-start.9 = (f32[8,512]{1,0:T(8,128)S(1)}, f32[8,512]{1,0:T(8,128)S(1)}, u32[]{:S(2)}, u32[]{:S(2)}) collective-permute-start(f32[8,512]{1,0:T(8,128)S(1)} %get-tuple-element.22), channel_id=1, source_target_pairs={{0,6},{1,7},{8,14},{9,15}} | collective-permute-start | bytes 49160 | tf_op jit(solution)/shard_map/ppermute | solution.py:235
  250.1 40.3 %collective-permute-start.7 = (f32[8,512]{1,0:T(8,128)S(1)}, f32[8,512]{1,0:T(8,128)S(1)}, u32[]{:S(2)}, u32[]{:S(2)}) collective-permute-start(f32[8,512]{1,0:T(8,128)S(1)} %get-tuple-element.23), channel_id=1, source_target_pairs={{0,2},{1,3},{8,10},{9,11}} | collective-permute-start | bytes 49160 | tf_op jit(solution)/shard_map/ppermute | solution.py:235
  289.1 2.7 collective-permute-start.8
  291.8 0.7 collective-permute-start.10
  292.5 186.8 %collective-permute-start.13 = (f32[8,512]{1,0:T(8,128)S(1)}, f32[8,512]{1,0:T(8,128)S(1)}, u32[]{:S(2)}, u32[]{:S(2)}) collective-permute-start(f32[8,512]{1,0:T(8,128)S(1)} %collective-permute-done.10), channel_id=1, source_target_pairs={{6,0},{7,1},{14,8},{15,9}} | collective-permute-start | bytes 49160 | tf_op jit(solution)/shard_map/ppermute | solution.py:235
  293.8 186.2 %collective-permute-start.12 = (f32[8,512]{1,0:T(8,128)S(1)}, f32[8,512]{1,0:T(8,128)S(1)}, u32[]{:S(2)}, u32[]{:S(2)}) collective-permute-start(f32[8,512]{1,0:T(8,128)S(1)} %collective-permute-done.10), channel_id=1, source_target_pairs={{4,0},{5,1},{12,8},{13,9}} | collective-permute-start | bytes 49160 | tf_op jit(solution)/shard_map/ppermute | solution.py:235
  479.3 15.5 %collective-permute-start.6 = (f32[8,1536]{1,0:T(8,128)S(1)}, f32[8,1536]{1,0:T(8,128)S(1)}, u32[]{:S(2)}, u32[]{:S(2)}) collective-permute-start(f32[8,1536]{1,0:T(8,128)S(1)} %get-tuple-element.24), channel_id=1, source_target_pairs={{2,10},{3,11},{4,12},{5,13},{6,14},{7,15},{10,2},{11,3},{12,4},{13... | collective-permute-start | bytes 147464 | tf_op jit(solution)/shard_map/ppermute | solution.py:235
  479.9 13.2 %collective-permute-start.11 = (f32[8,512]{1,0:T(8,128)S(1)}, f32[8,512]{1,0:T(8,128)S(1)}, u32[]{:S(2)}, u32[]{:S(2)}) collective-permute-start(f32[8,512]{1,0:T(8,128)S(1)} %collective-permute-done.10), channel_id=1, source_target_pairs={{2,0},{3,1},{10,8},{11,9}} | collective-permute-start | bytes 49160 | tf_op jit(solution)/shard_map/ppermute | solution.py:235
  481.4 13.4 %copy-start.6 = (f32[80,3072]{1,0:T(8,128)S(1)}, f32[80,3072]{1,0:T(8,128)}, u32[]{:S(2)}) copy-start(f32[80,3072]{1,0:T(8,128)} %get-tuple-element.15) | copy-start | bytes 2949124
  481.4 16.4 %copy-start.7 = (f32[16,3072]{1,0:T(8,128)S(1)}, f32[16,3072]{1,0:T(8,128)}, u32[]{:S(2)}) copy-start(f32[16,3072]{1,0:T(8,128)} %get-tuple-element.16) | copy-start | bytes 589828
  493.2 4.7 collective-permute-start.14
  494.8 24.5 %collective-permute-start.15 = (f32[80,3072]{1,0:T(8,128)S(1)}, f32[80,3072]{1,0:T(8,128)S(1)}, u32[]{:S(2)}, u32[]{:S(2)}) collective-permute-start(f32[80,3072]{1,0:T(8,128)S(1)} %copy-done.6), channel_id=1, source_target_pairs={{0,8},{8,0},{1,9},{9,1},{2,10},{10,2},{3,11},{11,3},{4,12},{12,4},... | collective-permute-start | bytes 2949128 | tf_op jit(solution)/shard_map/ppermute | solution.py:229
  497.8 25.0 %collective-permute-start.16 = (f32[16,3072]{1,0:T(8,128)S(1)}, f32[16,3072]{1,0:T(8,128)S(1)}, u32[]{:S(2)}, u32[]{:S(2)}) collective-permute-start(f32[16,3072]{1,0:T(8,128)S(1)} %copy-done.7), channel_id=1, source_target_pairs={{0,8},{8,0},{1,9},{9,1},{2,10},{10,2},{3,11},{11,3},{4,12},{12,4},... | collective-permute-start | bytes 589832 | tf_op jit(solution)/shard_map/ppermute | solution.py:229
  519.3 0.9 copy-start.3
  549.8 17.7 %copy-start.1 = (bf16[2048,768]{1,0:T(8,128)(2,1)S(1)}, bf16[2048,768]{1,0:T(8,128)(2,1)}, u32[]{:S(2)}) copy-start(bf16[2048,768]{1,0:T(8,128)(2,1)} %param.11) | copy-start | bytes 9437188
